TPU v7x, 512 devices: a whole 4x8x8 slice. The times are simulated.
512 devices in a mesh: dp: 64 (over y, x, core), mp: 8 (over z).
Axes of the slice: x: 4, y: 8, z: 8, core: 2. Of those that a mesh axis runs over, the one named last changes fastest.
Arguments:
- hidden: bfloat16 [960, 128, 2048], P('dp', None, 'mp'), may hold values from -6 to 6
- attn_out: bfloat16 [960, 128, 2048], P('dp', None, 'mp'), may hold values from -6 to 6
- out_proj: bfloat16 [2048, 2048], P(None, 'mp'), may hold values from -0.125 to 0.125
- norm_gain: float32 [2048], P('mp'), may hold values from 0.1 to 1.9
- reward_proj: float32 [2048, 8], P('mp'), may hold values from -0.125 to 0.125
- block_seq: int32 [960], replicated, may hold values from -1 to 383, as said below
- block_dest: int32 [960], replicated, may hold values from -1 to 639, as said below
- lengths: int32 [384], replicated, may hold values from 1 to 512, as said below
Outputs:
- token_rewards: float32 [640, 8, 128], P('dp')
- advantages: float32 [384], P('dp')
Inputs may be any that keep to these rules, and one draw needn't show every extreme that they name: `block_seq`: used slots of each index of dp come first in its 15 slots, the rest hold -1; each index of dp holds 1 to 15 used slots and some index holds exactly 15. Read over used slots in slot order, response numbers never fall, every response appears, and each has 1 to 4 blocks. `block_dest`: exactly the used slots (those of block_seq that are not -1) hold a destination; every owned slot of every owner is named exactly once, so each owner receives exactly 10 blocks; at most 1 block go from one index of dp to one owner, and that many in some pair. `lengths`: A response of n blocks has more than 128 * (n - 1) and at most 128 * n tokens.
All inputs are finite; a program needn't handle non-finite values.
Results may differ from a plain program's by a relative error of at most 0.0029.
Values may be sent and summed in bfloat16 or wider, within the bound.
No kernel may reach another device: no remote copies, remote signals or barrier semaphores. Data moves between devices by JAX's collectives and lax.ppermute only.
A program may use at most 64 MiB of HBM per device.

v0:
```python
import jax
import jax.numpy as jnp
from jax import lax
from jax.experimental import pallas as pl
from jax.experimental.pallas import tpu as pltpu
from jax.sharding import Mesh
from jax.sharding import PartitionSpec as P

OWN_CAP = 10
NORM_EPS = 1e-05
STAT_EPS = 1e-06
F32 = jnp.float32
BF16 = jnp.bfloat16
PLANES = 8
TOK = 16


def exchange(value, axis):
    return lax.all_to_all(value, axis, split_axis=0, concat_axis=0, tiled=True)


def shift(value, axis, step):
    size = lax.axis_size(axis)
    return lax.ppermute(value, axis, [(s, (s + step) % size) for s in range(size)])


def swap(value, axis):
    size = lax.axis_size(axis)
    return lax.ppermute(value, axis, [(s, s ^ 1) for s in range(size)])


def plane_step(kind, part):
    return (kind if part % 2 == 0 else PLANES - kind) + 4 * (part // 2)


def from_plane(value, part):
    pairs = []
    for y in range(8):
        for x in range(4):
            step = plane_step((y % 2) * 4 + x, part)
            for core in range(2):
                base = ((y * 4 + x) * 2 + core) * PLANES
                pairs += [(base + (z + step) % PLANES, base + z) for z in range(PLANES)]
    return lax.ppermute(value, ("y", "x", "core", "mp"), pairs)


def score_kernel(where_ref, acts_ref, *refs):
    pieces = refs[:16]
    live_ref, route_ref, out_ref, a_ref, w_ref, sq_ref, head_ref, sem = refs[16:]
    tokens = live_ref.shape[0]
    shard = acts_ref.shape[2]
    core = where_ref[32]

    def fetch(s, p):
        row = 2 * p + (core if s % 2 == 0 else 1 - core)
        return pltpu.make_async_copy(
            pieces[s].at[p], w_ref.at[where_ref[(s // 2) * 4 + p], row], sem.at[s, p]
        )

    for s in range(16):
        for p in range(4):
            fetch(s, p).start()
    for i in range(PLANES):
        a_ref[:, i * shard : (i + 1) * shard] = acts_ref[i, 0:tokens, :]
    for s in range(16):
        for p in range(4):
            fetch(s, p).wait()
    for j in range(PLANES):
        weights = w_ref[j].reshape(PLANES * shard, shard)
        proj = jnp.dot(a_ref[...], weights, preferred_element_type=F32)
        resid = (acts_ref[j, tokens : 2 * tokens, :].astype(F32) + proj).astype(BF16)
        value = resid.astype(F32)
        heads = lax.dot_general(
            resid, acts_ref[j, 2 * tokens :, :], (((1,), (1,)), ((), ())), preferred_element_type=F32
        )
        if j == 0:
            sq_ref[...] = value * value
            head_ref[...] = heads
        else:
            sq_ref[...] += value * value
            head_ref[...] += heads
    width = float(PLANES * acts_ref.shape[2])
    mean_sq = jnp.sum(sq_ref[...], axis=1, keepdims=True) / width
    scale = lax.rsqrt(mean_sq + NORM_EPS) * live_ref[...]
    k = lax.broadcasted_iota(jnp.int32, (16, 128), 0)
    lane = lax.broadcasted_iota(jnp.int32, (16, 128), 1)
    spread_heads = (k % 8 == lane // TOK).astype(F32)
    wide = jnp.dot(
        head_ref[...], spread_heads, precision=lax.Precision.HIGHEST, preferred_element_type=F32
    )
    wide = wide * scale
    row = lax.broadcasted_iota(jnp.int32, (tokens, 128), 0)
    col = lax.broadcasted_iota(jnp.int32, (tokens, 128), 1)
    by_token = jnp.where(row % TOK == col % TOK, wide, 0.0)
    by_slot = jnp.where(row // TOK == col % TOK, wide, 0.0)
    out_ref[:, 0, :] = jnp.dot(
        route_ref[...], by_token, precision=lax.Precision.HIGHEST, preferred_element_type=F32
    )
    out_ref[:, 1, :] = jnp.broadcast_to(
        jnp.sum(by_slot, axis=0, keepdims=True), (out_ref.shape[0], 128)
    )


def in_vmem(value):
    return pltpu.with_memory_space_constraint(value, pltpu.VMEM)


def score(where, *args):
    owners = args[-1].shape[0]
    tokens = args[-2].shape[0]
    width = PLANES * args[0].shape[2]
    vmem = pl.BlockSpec(memory_space=pltpu.VMEM)
    return pl.pallas_call(
        score_kernel,
        out_shape=jax.ShapeDtypeStruct((owners, 2, 128), F32),
        in_specs=[
            pl.BlockSpec(memory_space=pltpu.SMEM),
            vmem,
            *[pl.BlockSpec(memory_space=pl.ANY)] * 16,
            vmem,
            vmem,
        ],
        out_specs=vmem,
        scratch_shapes=[
            pltpu.VMEM((tokens, width), BF16),
            pltpu.VMEM((PLANES, PLANES, args[0].shape[2], args[0].shape[2]), BF16),
            pltpu.VMEM((tokens, args[0].shape[2]), F32),
            pltpu.VMEM((tokens, 16), F32),
            pltpu.SemaphoreType.DMA((16, 4)),
        ],
        compiler_params=pltpu.CompilerParams(vmem_limit_bytes=24 * 2**20),
        name="score",
    )(where, in_vmem(args[0]), *[pltpu.with_memory_space_constraint(v, pltpu.HBM) for v in args[1:17]], *args[17:])


def finish_kernel(totals_ref, lengths_ref, rank_ref, out_ref):
    totals = totals_ref[0]
    for p in range(1, PLANES):
        totals = totals + totals_ref[p]
    scores = totals / lengths_ref[...].astype(F32)
    count = float(scores.shape[1])
    worst = jnp.min(scores, axis=0, keepdims=True)
    head_mean = jnp.mean(scores, axis=0, keepdims=True)
    spread = jnp.mean((scores - head_mean) ** 2, axis=0, keepdims=True)
    penalty_scale = jnp.sum(spread, axis=1, keepdims=True) / count + STAT_EPS
    conservative = worst - spread / penalty_scale
    centre = jnp.sum(conservative, axis=1, keepdims=True) / count
    off = conservative - centre
    variance = jnp.sum(off * off, axis=1, keepdims=True) / count
    advantages = off / jnp.sqrt(variance + STAT_EPS)
    size = out_ref.shape[0]
    at = lax.broadcasted_iota(jnp.int32, (size, scores.shape[1]), 1)
    row = lax.broadcasted_iota(jnp.int32, (size, scores.shape[1]), 0)
    mine = jnp.where(at == row + rank_ref[0] * size, advantages, 0.0)
    out_ref[...] = jnp.sum(mine, axis=1, keepdims=True)


def finish(totals, lengths, rank, size):
    vmem = pl.BlockSpec(memory_space=pltpu.VMEM)
    return pl.pallas_call(
        finish_kernel,
        out_shape=jax.ShapeDtypeStruct((size, 1), F32),
        in_specs=[vmem, vmem, pl.BlockSpec(memory_space=pltpu.SMEM)],
        out_specs=vmem,
        compiler_params=pltpu.CompilerParams(vmem_limit_bytes=8 * 2**20),
        name="finish",
    )(in_vmem(totals), lengths[None, :], rank[None])


def local(hidden, attn_out, out_proj, norm_gain, reward_proj, block_seq, block_dest, lengths):
    y, x, core, plane = (lax.axis_index(n) for n in ("y", "x", "core", "mp"))
    rank = (y * lax.axis_size("x") + x) * 2 + core
    owners = 64
    slots_in, block_len, shard = hidden.shape
    seq_count = lengths.shape[0]
    seq_local = seq_count // owners
    tokens = slots_in * TOK

    parity = y % 2
    blocks = out_proj.reshape(4, 2, shard, shard)
    parts = []
    for p in range(4):
        block = lax.dynamic_index_in_dim(blocks[p], core, 0, keepdims=False)
        parts.append(from_plane(block, p))
    first = jnp.stack(parts)

    weighted = (norm_gain[:, None] * reward_proj).T
    high = lax.reduce_precision(weighted, 8, 7)
    low = weighted - high
    head_rows = jnp.concatenate([high.astype(BF16), low.astype(BF16)], axis=0)
    sliced = [
        v.reshape(slots_in, PLANES, TOK, shard).swapaxes(0, 1).reshape(PLANES, tokens, shard)
        for v in (attn_out, hidden)
    ]
    acts = jnp.concatenate([*sliced, jnp.broadcast_to(head_rows[None], (PLANES, *head_rows.shape))], axis=1)
    acts = exchange(acts, "mp")

    second = swap(first, "y")
    left0 = shift(first, "x", 1)
    right0 = shift(first, "x", -1)
    left1 = shift(second, "x", 1)
    right1 = shift(second, "x", -1)
    far0 = shift(left0, "x", 1)
    far1 = shift(right1, "x", -1)
    named = {
        "c0": first, "c1": second, "cl0": left0, "cl1": left1,
        "cr0": right0, "cr1": right1, "cf0": far0, "cf1": far1,
    }
    pieces = []
    for own in named.values():
        pieces += [own, swap(own, "core")]
    odd = jnp.array([0, 1, 0, 1, 0, 1, 0, 1], jnp.int32)
    away = jnp.array([0, 0, 3, 3, 1, 1, 2, 2], jnp.int32)
    kind = (parity ^ odd) * 4 + (x + away) % 4
    held = [(plane + plane_step(kind, p)) % PLANES for p in range(4)]
    where = jnp.concatenate([jnp.stack(held, axis=1).reshape(32), core[None]]).astype(jnp.int32)

    all_slots = jnp.arange(block_seq.shape[0], dtype=jnp.int32)
    mine = rank * slots_in + jnp.arange(slots_in, dtype=jnp.int32)
    seq_in = lax.dynamic_slice_in_dim(block_seq, rank * slots_in, slots_in)
    dest_in = lax.dynamic_slice_in_dim(block_dest, rank * slots_in, slots_in)
    earlier = (block_seq[None, :] == seq_in[:, None]) & (all_slots[None, :] < mine[:, None])
    order = jnp.sum(earlier.astype(jnp.int32), axis=1)
    seq_ids = jnp.arange(seq_count, dtype=jnp.int32)
    length_in = jnp.sum(jnp.where(seq_ids[None, :] == seq_in[:, None], lengths[None, :], 0), axis=1)
    valid = jnp.where(dest_in >= 0, jnp.minimum(block_len, length_in - block_len * order), 0)
    at = plane * TOK + jnp.arange(TOK, dtype=jnp.int32)
    live = (at[None, :] < valid[:, None]).astype(F32).reshape(tokens, 1)
    owner_in = jnp.where(dest_in >= 0, dest_in // OWN_CAP, -1)
    owner_of = jnp.broadcast_to(owner_in[:, None], (slots_in, TOK)).reshape(1, tokens)
    route = (jnp.arange(owners, dtype=jnp.int32)[:, None] == owner_of).astype(F32)

    sent = score(where, acts, *pieces, live, route)
    got = exchange(sent, ("y", "x", "core"))

    targets = rank * OWN_CAP + jnp.arange(OWN_CAP, dtype=jnp.int32)
    source = jnp.sum(jnp.where(block_dest[None, :] == targets[:, None], all_slots[None, :], 0), axis=1)
    pick = ((source // slots_in)[:, None] == jnp.arange(owners, dtype=jnp.int32)[None, :]).astype(F32)
    member = (block_seq[:, None] == seq_ids[None, :]).astype(F32)

    owned = jnp.dot(pick, got[:, 0, :], precision=lax.Precision.HIGHEST)
    sums = got[:, 1, :].reshape(owners, 8, TOK)[:, :, :slots_in].swapaxes(0, 1).reshape(8, owners * slots_in)
    totals = jnp.dot(sums, member, precision=lax.Precision.HIGHEST)
    final = jnp.concatenate([owned, totals.reshape(-1, 128)], axis=0)
    final = exchange(jnp.broadcast_to(final[None], (PLANES, *final.shape)), "mp")
    token_rewards = (
        final[:, :OWN_CAP].reshape(PLANES, OWN_CAP, 8, TOK).transpose(1, 2, 0, 3).reshape(OWN_CAP, 8, block_len)
    )
    totals = final[:, OWN_CAP:].reshape(PLANES, 8, seq_count)
    return token_rewards, finish(totals, lengths, rank, seq_local).reshape(seq_local)


def solution(mesh):
    dp = ("y", "x", "core")
    grid = Mesh(mesh.devices.reshape(8, 4, 2, PLANES), (*dp, "mp"))

    return jax.shard_map(
        local,
        mesh=grid,
        in_specs=(
            P(dp, None, "mp"),
            P(dp, None, "mp"),
            P(None, "mp"),
            P("mp"),
            P("mp", None),
            P(),
            P(),
            P(),
        ),
        out_specs=(P(dp, None, None), P(dp)),
        check_vma=False,
    )
```

profile of v0, /device:TPU:1, one launch (start us, length us, event | category | flops | bytes accessed | tf_op | source)
XLA Modules:
  0.0 180.5 jit_solution(12793952596205861186)
XLA Ops:
  0.7 1.3 copy.41
  2.3 1.5 pad_maximum_fusion
  3.7 11.0 %all-to-all-start = ((bf16[8,496,256]{2,1,0:T(8,128)(2,1)}), bf16[8,496,256]{2,1,0:T(8,128)(2,1)S(1)}, u32[]{:S(2)}, u32[]{:S(2)}) async-start(bf16[8,496,256]{2,1,0:T(8,128)(2,1)} %pad_maximum_fusion), calls=%async_computation | async-start | bytes 4063232 | tf_op jit(solution)/shard_map/all_to_all | solution.py:19
  14.9 7.3 %collective-permute-start.3 = (bf16[256,256]{1,0:T(8,128)(2,1)S(1)}, bf16[256,256]{1,0:T(8,128)(2,1)S(1)}, u32[]{:S(2)}, u32[]{:S(2)}) collective-permute-start(bf16[256,256]{1,0:T(8,128)(2,1)S(1)} %dynamic-slice_bitcast_fusion), channel_id=1, source_target_pairs={{4,0},{5,1},{6,2},{7,3},{0,4},{1,5},{2,6},{3,7},{12,8},{13,9},{14,... | collective-permute-start | bytes 393224 | tf_op jit(solution)/shard_map/ppermute | solution.py:44
  22.2 1.9 %collective-permute-start.2 = (bf16[256,256]{1,0:T(8,128)(2,1)S(1)}, bf16[256,256]{1,0:T(8,128)(2,1)S(1)}, u32[]{:S(2)}, u32[]{:S(2)}) collective-permute-start(bf16[256,256]{1,0:T(8,128)(2,1)S(1)} %dynamic-slice_bitcast_fusion.1), channel_id=1, source_target_pairs={{4,0},{5,1},{6,2},{7,3},{0,4},{1,5},{2,6},{3,7},{12,8},{13,9},{14,... | collective-permute-start | bytes 393224 | tf_op jit(solution)/shard_map/ppermute | solution.py:44
  24.1 0.7 collective-permute-start.1
  24.8 0.7 collective-permute-start
  25.5 40.8 %collective-permute-done.3 = bf16[256,256]{1,0:T(8,128)(2,1)S(1)} collective-permute-done((bf16[256,256]{1,0:T(8,128)(2,1)S(1)}, bf16[256,256]{1,0:T(8,128)(2,1)S(1)}, u32[]{:S(2)}, u32[]{:S(2)}) %collective-permute-start.3) | collective-permute-done | bytes 131104 | tf_op jit(solution)/shard_map/ppermute | solution.py:44
  66.4 9.8 %collective-permute-done.2 = bf16[256,256]{1,0:T(8,128)(2,1)S(1)} collective-permute-done((bf16[256,256]{1,0:T(8,128)(2,1)S(1)}, bf16[256,256]{1,0:T(8,128)(2,1)S(1)}, u32[]{:S(2)}, u32[]{:S(2)}) %collective-permute-start.2) | collective-permute-done | bytes 131104 | tf_op jit(solution)/shard_map/ppermute | solution.py:44
  76.3 3.2 %collective-permute-start.5 = (bf16[4,256,256]{2,1,0:T(8,128)(2,1)S(1)}, bf16[4,256,256]{2,1,0:T(8,128)(2,1)S(1)}, u32[]{:S(2)}, u32[]{:S(2)}) collective-permute-start(bf16[4,256,256]{2,1,0:T(8,128)(2,1)S(1)} %pad_maximum_fusion.1.refs_0_), channel_id=1, source_target_pairs={{0,64},{64,0},{128,192},{192,128},{256,320},{320,256},{384,448},{4... | collective-permute-start | bytes 1572872 | tf_op jit(solution)/shard_map/ppermute | solution.py:29
  79.6 2.7 %collective-permute-start.4 = (bf16[4,256,256]{2,1,0:T(8,128)(2,1)S(1)}, bf16[4,256,256]{2,1,0:T(8,128)(2,1)}, u32[]{:S(2)}, u32[]{:S(2)}) collective-permute-start(bf16[4,256,256]{2,1,0:T(8,128)(2,1)S(1)} %pad_maximum_fusion.1.refs_0_), channel_id=1, source_target_pairs={{0,8},{8,0},{1,9},{9,1},{2,10},{10,2},{3,11},{11,3},{4,12},{12,4},... | collective-permute-start | bytes 1572872 | tf_op jit(solution)/shard_map/ppermute | solution.py:29
  82.2 2.1 %collective-permute-start.7 = (bf16[4,256,256]{2,1,0:T(8,128)(2,1)S(1)}, bf16[4,256,256]{2,1,0:T(8,128)(2,1)}, u32[]{:S(2)}, u32[]{:S(2)}) collective-permute-start(bf16[4,256,256]{2,1,0:T(8,128)(2,1)S(1)} %pad_maximum_fusion.1.refs_0_), channel_id=1, source_target_pairs={{0,16},{16,32},{32,48},{48,0},{1,17},{17,33},{33,49},{49,1},{2,18}... | collective-permute-start | bytes 1572872 | tf_op jit(solution)/shard_map/ppermute | solution.py:24
  84.4 4.4 %collective-permute-start.11 = (bf16[4,256,256]{2,1,0:T(8,128)(2,1)S(1)}, bf16[4,256,256]{2,1,0:T(8,128)(2,1)}, u32[]{:S(2)}, u32[]{:S(2)}) collective-permute-start(bf16[4,256,256]{2,1,0:T(8,128)(2,1)S(1)} %pad_maximum_fusion.1.refs_0_), channel_id=1, source_target_pairs={{0,48},{16,0},{32,16},{48,32},{1,49},{17,1},{33,17},{49,33},{2,50}... | collective-permute-start | bytes 1572872 | tf_op jit(solution)/shard_map/ppermute | solution.py:24
  88.8 2.5 %collective-permute-done.5.refs_2_ = bf16[4,256,256]{2,1,0:T(8,128)(2,1)S(1)} collective-permute-done((bf16[4,256,256]{2,1,0:T(8,128)(2,1)S(1)}, bf16[4,256,256]{2,1,0:T(8,128)(2,1)S(1)}, u32[]{:S(2)}, u32[]{:S(2)}) %collective-permute-start.5) | collective-permute-done | bytes 524320 | tf_op jit(solution)/shard_map/ppermute | solution.py:29
  91.3 1.9 %collective-permute-start.13 = (bf16[4,256,256]{2,1,0:T(8,128)(2,1)S(1)}, bf16[4,256,256]{2,1,0:T(8,128)(2,1)}, u32[]{:S(2)}, u32[]{:S(2)}) collective-permute-start(bf16[4,256,256]{2,1,0:T(8,128)(2,1)S(1)} %collective-permute-done.5.refs_2_), channel_id=1, source_target_pairs={{0,48},{16,0},{32,16},{48,32},{1,49},{17,1},{33,17},{49,33},{2,50}... | collective-permute-start | bytes 1572872 | tf_op jit(solution)/shard_map/ppermute | solution.py:24
  93.5 0.2 select_reduce_fusion.1
  93.7 0.2 convert_reduce_fusion
  93.9 3.2 %collective-permute-start.6 = (bf16[4,256,256]{2,1,0:T(8,128)(2,1)S(1)}, bf16[4,256,256]{2,1,0:T(8,128)(2,1)}, u32[]{:S(2)}, u32[]{:S(2)}) collective-permute-start(bf16[4,256,256]{2,1,0:T(8,128)(2,1)S(1)} %collective-permute-done.5.refs_2_), channel_id=1, source_target_pairs={{0,8},{8,0},{1,9},{9,1},{2,10},{10,2},{3,11},{11,3},{4,12},{12,4},... | collective-permute-start | bytes 1572872 | tf_op jit(solution)/shard_map/ppermute | solution.py:29
  97.0 3.6 %collective-permute-start.9 = (bf16[4,256,256]{2,1,0:T(8,128)(2,1)S(1)}, bf16[4,256,256]{2,1,0:T(8,128)(2,1)}, u32[]{:S(2)}, u32[]{:S(2)}) collective-permute-start(bf16[4,256,256]{2,1,0:T(8,128)(2,1)S(1)} %collective-permute-done.5.refs_2_), channel_id=1, source_target_pairs={{0,16},{16,32},{32,48},{48,0},{1,17},{17,33},{33,49},{49,1},{2,18}... | collective-permute-start | bytes 1572872 | tf_op jit(solution)/shard_map/ppermute | solution.py:24
  100.7 2.2 %collective-permute-start.8 = (bf16[4,256,256]{2,1,0:T(8,128)(2,1)}, bf16[4,256,256]{2,1,0:T(8,128)(2,1)}, u32[]{:S(2)}, u32[]{:S(2)}) collective-permute-start(bf16[4,256,256]{2,1,0:T(8,128)(2,1)} %collective-permute-done.7.refs_4_), channel_id=1, source_target_pairs={{0,8},{8,0},{1,9},{9,1},{2,10},{10,2},{3,11},{11,3},{4,12},{12,4},... | collective-permute-start | bytes 1572872 | tf_op jit(solution)/shard_map/ppermute | solution.py:29
  102.9 1.9 %collective-permute-start.15 = (bf16[4,256,256]{2,1,0:T(8,128)(2,1)}, bf16[4,256,256]{2,1,0:T(8,128)(2,1)}, u32[]{:S(2)}, u32[]{:S(2)}) collective-permute-start(bf16[4,256,256]{2,1,0:T(8,128)(2,1)} %collective-permute-done.7.refs_4_), channel_id=1, source_target_pairs={{0,16},{16,32},{32,48},{48,0},{1,17},{17,33},{33,49},{49,1},{2,18}... | collective-permute-start | bytes 1572872 | tf_op jit(solution)/shard_map/ppermute | solution.py:24
  104.8 6.1 %collective-permute-done.13.refs_10_ = bf16[4,256,256]{2,1,0:T(8,128)(2,1)} collective-permute-done((bf16[4,256,256]{2,1,0:T(8,128)(2,1)S(1)}, bf16[4,256,256]{2,1,0:T(8,128)(2,1)}, u32[]{:S(2)}, u32[]{:S(2)}) %collective-permute-start.13) | collective-permute-done | bytes 524320 | tf_op jit(solution)/shard_map/ppermute | solution.py:24
  111.0 5.4 %collective-permute-start.17 = (bf16[4,256,256]{2,1,0:T(8,128)(2,1)}, bf16[4,256,256]{2,1,0:T(8,128)(2,1)}, u32[]{:S(2)}, u32[]{:S(2)}) collective-permute-start(bf16[4,256,256]{2,1,0:T(8,128)(2,1)} %collective-permute-done.13.refs_10_), channel_id=1, source_target_pairs={{0,48},{16,0},{32,16},{48,32},{1,49},{17,1},{33,17},{49,33},{2,50}... | collective-permute-start | bytes 1572872 | tf_op jit(solution)/shard_map/ppermute | solution.py:24
  116.8 3.3 %collective-permute-start.12 = (bf16[4,256,256]{2,1,0:T(8,128)(2,1)}, bf16[4,256,256]{2,1,0:T(8,128)(2,1)S(1)}, u32[]{:S(2)}, u32[]{:S(2)}) collective-permute-start(bf16[4,256,256]{2,1,0:T(8,128)(2,1)} %collective-permute-done.11.refs_8_), channel_id=1, source_target_pairs={{0,8},{8,0},{1,9},{9,1},{2,10},{10,2},{3,11},{11,3},{4,12},{12,4},... | collective-permute-start | bytes 1572872 | tf_op jit(solution)/shard_map/ppermute | solution.py:29
  120.2 1.9 %collective-permute-start.14 = (bf16[4,256,256]{2,1,0:T(8,128)(2,1)}, bf16[4,256,256]{2,1,0:T(8,128)(2,1)S(1)}, u32[]{:S(2)}, u32[]{:S(2)}) collective-permute-start(bf16[4,256,256]{2,1,0:T(8,128)(2,1)} %collective-permute-done.13.refs_10_), channel_id=1, source_target_pairs={{0,8},{8,0},{1,9},{9,1},{2,10},{10,2},{3,11},{11,3},{4,12},{12,4},... | collective-permute-start | bytes 1572872 | tf_op jit(solution)/shard_map/ppermute | solution.py:29
  122.1 2.4 %collective-permute-start.10 = (bf16[4,256,256]{2,1,0:T(8,128)(2,1)}, bf16[4,256,256]{2,1,0:T(8,128)(2,1)S(1)}, u32[]{:S(2)}, u32[]{:S(2)}) collective-permute-start(bf16[4,256,256]{2,1,0:T(8,128)(2,1)} %collective-permute-done.9.refs_6_), channel_id=1, source_target_pairs={{0,8},{8,0},{1,9},{9,1},{2,10},{10,2},{3,11},{11,3},{4,12},{12,4},... | collective-permute-start | bytes 1572872 | tf_op jit(solution)/shard_map/ppermute | solution.py:29
  124.5 0.4 collective-permute-done.15.refs_12_
  125.0 2.8 %collective-permute-start.16 = (bf16[4,256,256]{2,1,0:T(8,128)(2,1)}, bf16[4,256,256]{2,1,0:T(8,128)(2,1)S(1)}, u32[]{:S(2)}, u32[]{:S(2)}) collective-permute-start(bf16[4,256,256]{2,1,0:T(8,128)(2,1)} %collective-permute-done.15.refs_12_), channel_id=1, source_target_pairs={{0,8},{8,0},{1,9},{9,1},{2,10},{10,2},{3,11},{11,3},{4,12},{12,4},... | collective-permute-start | bytes 1572872 | tf_op jit(solution)/shard_map/ppermute | solution.py:29
  127.7 3.0 %collective-permute-start.18 = (bf16[4,256,256]{2,1,0:T(8,128)(2,1)}, bf16[4,256,256]{2,1,0:T(8,128)(2,1)}, u32[]{:S(2)}, u32[]{:S(2)}) collective-permute-start(bf16[4,256,256]{2,1,0:T(8,128)(2,1)} %collective-permute-done.17.refs_14_), channel_id=1, source_target_pairs={{0,8},{8,0},{1,9},{9,1},{2,10},{10,2},{3,11},{11,3},{4,12},{12,4},... | collective-permute-start | bytes 1572872 | tf_op jit(solution)/shard_map/ppermute | solution.py:29
  130.8 0.2 select_reduce_fusion
  131.1 0.8 copy-done.4
  131.8 0.2 copy-done.6
  132.0 0.3 copy-done.5
  132.3 0.8 copy-done.7
  133.1 10.9 %score.1 = f32[64,2,128]{2,1,0:T(2,128)} custom-call(s32[33]{0:T(128)S(1)} %pad_add_fusion.1.where_ref, bf16[8,496,256]{2,1,0:T(8,128)(2,1)S(1)} %all-to-all-done.acts_ref, bf16[4,256,256]{2,1,0:T(8,128)(2,1)} %copy-done, bf16[4,256,256]{2,1,0:T(8,128)(2,1)} %collective-permute-done.4.refs_1_, bf16[4,256,256]{2,1,0:T(8,128)(2,1)} %copy-done.3, ...), custom_call_target="tpu_custom_call" | custom-call | tf_op jit(solution)/shard_map/score/pallas_call | solution.py:113
  144.0 10.0 %all-to-all-start.1 = ((f32[64,2,128]{2,1,0:T(2,128)}), f32[64,2,128]{2,1,0:T(2,128)S(1)}, u32[]{:S(2)}, u32[]{:S(2)}) async-start(f32[64,2,128]{2,1,0:T(2,128)} %score.1), calls=%async_computation.1 | async-start | bytes 131072 | tf_op jit(solution)/shard_map/all_to_all | solution.py:19
  154.0 10.1 %all-to-all-done.1 = f32[64,2,128]{2,1,0:T(2,128)S(1)} async-done(((f32[64,2,128]{2,1,0:T(2,128)}), f32[64,2,128]{2,1,0:T(2,128)S(1)}, u32[]{:S(2)}, u32[]{:S(2)}) %all-to-all-start.1) | async-done | bytes 65568 | tf_op jit(solution)/shard_map/all_to_all | solution.py:19
  164.3 0.1 copy.44
  164.4 0.2 reshape.113
  164.6 0.6 fusion
  165.2 0.2 fusion.5
  165.4 0.7 broadcast_in_dim.46
  166.1 3.4 %all-to-all-start.2 = ((f32[8,34,128]{2,1,0:T(8,128)}), f32[8,34,128]{2,1,0:T(8,128)S(1)}, u32[]{:S(2)}, u32[]{:S(2)}) async-start(f32[8,34,128]{2,1,0:T(8,128)} %broadcast_in_dim.46), calls=%async_computation.2 | async-start | bytes 327680 | tf_op jit(solution)/shard_map/all_to_all | solution.py:19
  169.5 8.9 %all-to-all-done.2 = f32[8,34,128]{2,1,0:T(8,128)S(1)} async-done(((f32[8,34,128]{2,1,0:T(8,128)}), f32[8,34,128]{2,1,0:T(8,128)S(1)}, u32[]{:S(2)}, u32[]{:S(2)}) %all-to-all-start.2) | async-done | bytes 139296 | tf_op jit(solution)/shard_map/all_to_all | solution.py:19
  178.5 0.1 reshape.115
  178.7 0.8 reshape.116
  179.5 0.4 finish.1
  179.9 0.6 reduce
  (79 shorter events, 1.6 us)
Async XLA Ops:
  0.6 1.5 copy-start.2
  0.6 1.6 copy-start.9
  0.7 1.6 copy-start.12
  3.7 11.0 %copy-start.1 = (bf16[2048,256]{1,0:T(8,128)(2,1)S(1)}, bf16[2048,256]{1,0:T(8,128)(2,1)}, u32[]{:S(2)}) copy-start(bf16[2048,256]{1,0:T(8,128)(2,1)} %param.12) | copy-start | bytes 3145732
  3.7 129.3 %all-to-all-start = ((bf16[8,496,256]{2,1,0:T(8,128)(2,1)}), bf16[8,496,256]{2,1,0:T(8,128)(2,1)S(1)}, u32[]{:S(2)}, u32[]{:S(2)}) async-start(bf16[8,496,256]{2,1,0:T(8,128)(2,1)} %pad_maximum_fusion), calls=%async_computation | async-start | bytes 4063232 | tf_op jit(solution)/shard_map/all_to_all | solution.py:19
  14.7 64.8 %copy-start.13 = (s32[8]{0:T(128)S(1)}, s32[8]{0:T(128)}, u32[]{:S(2)}) copy-start(s32[8]{0:T(128)} %constant.116.clone) | copy-start | bytes 100
  14.7 64.8 %copy-start.14 = (s32[8]{0:T(128)S(1)}, s32[8]{0:T(128)}, u32[]{:S(2)}) copy-start(s32[8]{0:T(128)} %constant.115.clone) | copy-start | bytes 100
  14.7 78.7 %copy-start.11 = (s32[960]{0:T(1024)S(1)}, s32[960]{0:T(1024)}, u32[]{:S(2)}) copy-start(s32[960]{0:T(1024)} %param.15) | copy-start | bytes 11524
  14.8 78.7 %copy-start.8 = (s32[384]{0:T(512)S(1)}, s32[384]{0:T(512)}, u32[]{:S(2)}) copy-start(s32[384]{0:T(512)} %param.17) | copy-start | bytes 4612
  14.8 101.6 %copy-start.10 = (s32[960]{0:T(1024)S(1)}, s32[960]{0:T(1024)}, u32[]{:S(2)}) copy-start(s32[960]{0:T(1024)} %param.16) | copy-start | bytes 11524
  14.9 51.5 %collective-permute-start.3 = (bf16[256,256]{1,0:T(8,128)(2,1)S(1)}, bf16[256,256]{1,0:T(8,128)(2,1)S(1)}, u32[]{:S(2)}, u32[]{:S(2)}) collective-permute-start(bf16[256,256]{1,0:T(8,128)(2,1)S(1)} %dynamic-slice_bitcast_fusion), channel_id=1, source_target_pairs={{4,0},{5,1},{6,2},{7,3},{0,4},{1,5},{2,6},{3,7},{12,8},{13,9},{14,... | collective-permute-start | bytes 393224 | tf_op jit(solution)/shard_map/ppermute | solution.py:44
  22.2 54.0 %collective-permute-start.2 = (bf16[256,256]{1,0:T(8,128)(2,1)S(1)}, bf16[256,256]{1,0:T(8,128)(2,1)S(1)}, u32[]{:S(2)}, u32[]{:S(2)}) collective-permute-start(bf16[256,256]{1,0:T(8,128)(2,1)S(1)} %dynamic-slice_bitcast_fusion.1), channel_id=1, source_target_pairs={{4,0},{5,1},{6,2},{7,3},{0,4},{1,5},{2,6},{3,7},{12,8},{13,9},{14,... | collective-permute-start | bytes 393224 | tf_op jit(solution)/shard_map/ppermute | solution.py:44
  24.1 52.1 %collective-permute-start.1 = (bf16[256,256]{1,0:T(8,128)(2,1)S(1)}, bf16[256,256]{1,0:T(8,128)(2,1)S(1)}, u32[]{:S(2)}, u32[]{:S(2)}) collective-permute-start(bf16[256,256]{1,0:T(8,128)(2,1)S(1)} %dynamic-slice_bitcast_fusion.2), channel_id=1, source_target_pairs={{0,0},{1,1},{2,2},{3,3},{4,4},{5,5},{6,6},{7,7},{8,8},{9,9},{10,10... | collective-permute-start | bytes 393224 | tf_op jit(solution)/shard_map/ppermute | solution.py:44
  24.8 51.4 %collective-permute-start = (bf16[256,256]{1,0:T(8,128)(2,1)S(1)}, bf16[256,256]{1,0:T(8,128)(2,1)S(1)}, u32[]{:S(2)}, u32[]{:S(2)}) collective-permute-start(bf16[256,256]{1,0:T(8,128)(2,1)S(1)} %dynamic-slice_bitcast_fusion.3), channel_id=1, source_target_pairs={{0,0},{1,1},{2,2},{3,3},{4,4},{5,5},{6,6},{7,7},{8,8},{9,9},{10,10... | collective-permute-start | bytes 393224 | tf_op jit(solution)/shard_map/ppermute | solution.py:44
  76.3 56.8 %copy-start = (bf16[4,256,256]{2,1,0:T(8,128)(2,1)}, bf16[4,256,256]{2,1,0:T(8,128)(2,1)S(1)}, u32[]{:S(2)}) copy-start(bf16[4,256,256]{2,1,0:T(8,128)(2,1)S(1)} %pad_maximum_fusion.1.refs_0_) | copy-start | bytes 1572868
  76.3 15.0 %collective-permute-start.5 = (bf16[4,256,256]{2,1,0:T(8,128)(2,1)S(1)}, bf16[4,256,256]{2,1,0:T(8,128)(2,1)S(1)}, u32[]{:S(2)}, u32[]{:S(2)}) collective-permute-start(bf16[4,256,256]{2,1,0:T(8,128)(2,1)S(1)} %pad_maximum_fusion.1.refs_0_), channel_id=1, source_target_pairs={{0,64},{64,0},{128,192},{192,128},{256,320},{320,256},{384,448},{4... | collective-permute-start | bytes 1572872 | tf_op jit(solution)/shard_map/ppermute | solution.py:29
  79.6 17.5 %collective-permute-start.4 = (bf16[4,256,256]{2,1,0:T(8,128)(2,1)S(1)}, bf16[4,256,256]{2,1,0:T(8,128)(2,1)}, u32[]{:S(2)}, u32[]{:S(2)}) collective-permute-start(bf16[4,256,256]{2,1,0:T(8,128)(2,1)S(1)} %pad_maximum_fusion.1.refs_0_), channel_id=1, source_target_pairs={{0,8},{8,0},{1,9},{9,1},{2,10},{10,2},{3,11},{11,3},{4,12},{12,4},... | collective-permute-start | bytes 1572872 | tf_op jit(solution)/shard_map/ppermute | solution.py:29
  82.2 18.4 %collective-permute-start.7 = (bf16[4,256,256]{2,1,0:T(8,128)(2,1)S(1)}, bf16[4,256,256]{2,1,0:T(8,128)(2,1)}, u32[]{:S(2)}, u32[]{:S(2)}) collective-permute-start(bf16[4,256,256]{2,1,0:T(8,128)(2,1)S(1)} %pad_maximum_fusion.1.refs_0_), channel_id=1, source_target_pairs={{0,16},{16,32},{32,48},{48,0},{1,17},{17,33},{33,49},{49,1},{2,18}... | collective-permute-start | bytes 1572872 | tf_op jit(solution)/shard_map/ppermute | solution.py:24
  84.4 18.5 %collective-permute-start.11 = (bf16[4,256,256]{2,1,0:T(8,128)(2,1)S(1)}, bf16[4,256,256]{2,1,0:T(8,128)(2,1)}, u32[]{:S(2)}, u32[]{:S(2)}) collective-permute-start(bf16[4,256,256]{2,1,0:T(8,128)(2,1)S(1)} %pad_maximum_fusion.1.refs_0_), channel_id=1, source_target_pairs={{0,48},{16,0},{32,16},{48,32},{1,49},{17,1},{33,17},{49,33},{2,50}... | collective-permute-start | bytes 1572872 | tf_op jit(solution)/shard_map/ppermute | solution.py:24
  91.3 41.8 %copy-start.3 = (bf16[4,256,256]{2,1,0:T(8,128)(2,1)}, bf16[4,256,256]{2,1,0:T(8,128)(2,1)S(1)}, u32[]{:S(2)}) copy-start(bf16[4,256,256]{2,1,0:T(8,128)(2,1)S(1)} %collective-permute-done.5.refs_2_) | copy-start | bytes 1572868
  91.3 19.7 %collective-permute-start.13 = (bf16[4,256,256]{2,1,0:T(8,128)(2,1)S(1)}, bf16[4,256,256]{2,1,0:T(8,128)(2,1)}, u32[]{:S(2)}, u32[]{:S(2)}) collective-permute-start(bf16[4,256,256]{2,1,0:T(8,128)(2,1)S(1)} %collective-permute-done.5.refs_2_), channel_id=1, source_target_pairs={{0,48},{16,0},{32,16},{48,32},{1,49},{17,1},{33,17},{49,33},{2,50}... | collective-permute-start | bytes 1572872 | tf_op jit(solution)/shard_map/ppermute | solution.py:24
  93.9 23.0 %collective-permute-start.6 = (bf16[4,256,256]{2,1,0:T(8,128)(2,1)S(1)}, bf16[4,256,256]{2,1,0:T(8,128)(2,1)}, u32[]{:S(2)}, u32[]{:S(2)}) collective-permute-start(bf16[4,256,256]{2,1,0:T(8,128)(2,1)S(1)} %collective-permute-done.5.refs_2_), channel_id=1, source_target_pairs={{0,8},{8,0},{1,9},{9,1},{2,10},{10,2},{3,11},{11,3},{4,12},{12,4},... | collective-permute-start | bytes 1572872 | tf_op jit(solution)/shard_map/ppermute | solution.py:29
  97.0 25.1 %collective-permute-start.9 = (bf16[4,256,256]{2,1,0:T(8,128)(2,1)S(1)}, bf16[4,256,256]{2,1,0:T(8,128)(2,1)}, u32[]{:S(2)}, u32[]{:S(2)}) collective-permute-start(bf16[4,256,256]{2,1,0:T(8,128)(2,1)S(1)} %collective-permute-done.5.refs_2_), channel_id=1, source_target_pairs={{0,16},{16,32},{32,48},{48,0},{1,17},{17,33},{33,49},{49,1},{2,18}... | collective-permute-start | bytes 1572872 | tf_op jit(solution)/shard_map/ppermute | solution.py:24
  100.7 19.5 %collective-permute-start.8 = (bf16[4,256,256]{2,1,0:T(8,128)(2,1)}, bf16[4,256,256]{2,1,0:T(8,128)(2,1)}, u32[]{:S(2)}, u32[]{:S(2)}) collective-permute-start(bf16[4,256,256]{2,1,0:T(8,128)(2,1)} %collective-permute-done.7.refs_4_), channel_id=1, source_target_pairs={{0,8},{8,0},{1,9},{9,1},{2,10},{10,2},{3,11},{11,3},{4,12},{12,4},... | collective-permute-start | bytes 1572872 | tf_op jit(solution)/shard_map/ppermute | solution.py:29
  102.9 22.0 %collective-permute-start.15 = (bf16[4,256,256]{2,1,0:T(8,128)(2,1)}, bf16[4,256,256]{2,1,0:T(8,128)(2,1)}, u32[]{:S(2)}, u32[]{:S(2)}) collective-permute-start(bf16[4,256,256]{2,1,0:T(8,128)(2,1)} %collective-permute-done.7.refs_4_), channel_id=1, source_target_pairs={{0,16},{16,32},{32,48},{48,0},{1,17},{17,33},{33,49},{49,1},{2,18}... | collective-permute-start | bytes 1572872 | tf_op jit(solution)/shard_map/ppermute | solution.py:24
  111.0 16.8 %collective-permute-start.17 = (bf16[4,256,256]{2,1,0:T(8,128)(2,1)}, bf16[4,256,256]{2,1,0:T(8,128)(2,1)}, u32[]{:S(2)}, u32[]{:S(2)}) collective-permute-start(bf16[4,256,256]{2,1,0:T(8,128)(2,1)} %collective-permute-done.13.refs_10_), channel_id=1, source_target_pairs={{0,48},{16,0},{32,16},{48,32},{1,49},{17,1},{33,17},{49,33},{2,50}... | collective-permute-start | bytes 1572872 | tf_op jit(solution)/shard_map/ppermute | solution.py:24
  116.8 14.2 %collective-permute-start.12 = (bf16[4,256,256]{2,1,0:T(8,128)(2,1)}, bf16[4,256,256]{2,1,0:T(8,128)(2,1)S(1)}, u32[]{:S(2)}, u32[]{:S(2)}) collective-permute-start(bf16[4,256,256]{2,1,0:T(8,128)(2,1)} %collective-permute-done.11.refs_8_), channel_id=1, source_target_pairs={{0,8},{8,0},{1,9},{9,1},{2,10},{10,2},{3,11},{11,3},{4,12},{12,4},... | collective-permute-start | bytes 1572872 | tf_op jit(solution)/shard_map/ppermute | solution.py:29
  120.2 10.9 %collective-permute-start.14 = (bf16[4,256,256]{2,1,0:T(8,128)(2,1)}, bf16[4,256,256]{2,1,0:T(8,128)(2,1)S(1)}, u32[]{:S(2)}, u32[]{:S(2)}) collective-permute-start(bf16[4,256,256]{2,1,0:T(8,128)(2,1)} %collective-permute-done.13.refs_10_), channel_id=1, source_target_pairs={{0,8},{8,0},{1,9},{9,1},{2,10},{10,2},{3,11},{11,3},{4,12},{12,4},... | collective-permute-start | bytes 1572872 | tf_op jit(solution)/shard_map/ppermute | solution.py:29
  122.1 8.9 %collective-permute-start.10 = (bf16[4,256,256]{2,1,0:T(8,128)(2,1)}, bf16[4,256,256]{2,1,0:T(8,128)(2,1)S(1)}, u32[]{:S(2)}, u32[]{:S(2)}) collective-permute-start(bf16[4,256,256]{2,1,0:T(8,128)(2,1)} %collective-permute-done.9.refs_6_), channel_id=1, source_target_pairs={{0,8},{8,0},{1,9},{9,1},{2,10},{10,2},{3,11},{11,3},{4,12},{12,4},... | collective-permute-start | bytes 1572872 | tf_op jit(solution)/shard_map/ppermute | solution.py:29
  125.0 6.1 %collective-permute-start.16 = (bf16[4,256,256]{2,1,0:T(8,128)(2,1)}, bf16[4,256,256]{2,1,0:T(8,128)(2,1)S(1)}, u32[]{:S(2)}, u32[]{:S(2)}) collective-permute-start(bf16[4,256,256]{2,1,0:T(8,128)(2,1)} %collective-permute-done.15.refs_12_), channel_id=1, source_target_pairs={{0,8},{8,0},{1,9},{9,1},{2,10},{10,2},{3,11},{11,3},{4,12},{12,4},... | collective-permute-start | bytes 1572872 | tf_op jit(solution)/shard_map/ppermute | solution.py:29
  127.7 5.3 %collective-permute-start.18 = (bf16[4,256,256]{2,1,0:T(8,128)(2,1)}, bf16[4,256,256]{2,1,0:T(8,128)(2,1)}, u32[]{:S(2)}, u32[]{:S(2)}) collective-permute-start(bf16[4,256,256]{2,1,0:T(8,128)(2,1)} %collective-permute-done.17.refs_14_), channel_id=1, source_target_pairs={{0,8},{8,0},{1,9},{9,1},{2,10},{10,2},{3,11},{11,3},{4,12},{12,4},... | collective-permute-start | bytes 1572872 | tf_op jit(solution)/shard_map/ppermute | solution.py:29
  131.0 0.8 copy-start.4
  131.0 1.0 copy-start.6
  131.1 1.2 copy-start.5
  132.3 0.8 copy-start.7
  144.0 20.1 %all-to-all-start.1 = ((f32[64,2,128]{2,1,0:T(2,128)}), f32[64,2,128]{2,1,0:T(2,128)S(1)}, u32[]{:S(2)}, u32[]{:S(2)}) async-start(f32[64,2,128]{2,1,0:T(2,128)} %score.1), calls=%async_computation.1 | async-start | bytes 131072 | tf_op jit(solution)/shard_map/all_to_all | solution.py:19
  166.1 12.3 %all-to-all-start.2 = ((f32[8,34,128]{2,1,0:T(8,128)}), f32[8,34,128]{2,1,0:T(8,128)S(1)}, u32[]{:S(2)}, u32[]{:S(2)}) async-start(f32[8,34,128]{2,1,0:T(8,128)} %broadcast_in_dim.46), calls=%async_computation.2 | async-start | bytes 327680 | tf_op jit(solution)/shard_map/all_to_all | solution.py:19
where the time goes:
time: 181 us
  starting transfers between devices  78.9 us (44%)
  waiting for transfers between devices  78.8 us (44%)
  Pallas kernels  11.3 us (6%)
  local copies, waits for them, and re-layouts  6.36 us (4%)
  other arithmetic  3.1 us (2%)
    ppermute x4, waiting for transfers between devices, from_plane(): return lax.ppermute(value, ('y', 'x', 'core', 'mp'), pairs)  50.7 us
    ppermute x9, starting transfers between devices, swap(): return lax.ppermute(value, axis, [(s, s ^ 1) for s in range(size)])  24.6 us
    all_to_all x3, starting transfers between devices, exchange(): return lax.all_to_all(value, axis, split_axis=0, concat_axis=0, tiled=True)  24.4 us
    ppermute x6, starting transfers between devices, shift(): lax.ppermute(value, axis, [(s, (s + step) % size) for s in range(size)])  19.4 us
    all_to_all x3, waiting for transfers between devices, exchange(): return lax.all_to_all(value, axis, split_axis=0, concat_axis=0, tiled=True)  19 us
    pallas_call x1, Pallas kernels, score(): pl.pallas_call(score_kernel, out_shape=jax.ShapeDtypeStruct((owners, 2, 1...  10.9 us
    ppermute x4, starting transfers between devices, from_plane(): return lax.ppermute(value, ('y', 'x', 'core', 'mp'), pairs)  10.5 us
    ppermute x6, waiting for transfers between devices, shift(): lax.ppermute(value, axis, [(s, (s + step) % size) for s in range(size)])  6.53 us
  transfers between devices with their start and end apart: 22, of which 7 were waited for; matrix products, arithmetic and copies ran while one was open for 1% of the time, Pallas kernels for 0%

commit v1 on v0

--- a/solution.py
+++ b/solution.py
@@ -29,73 +29,87 @@
     return lax.ppermute(value, axis, [(s, s ^ 1) for s in range(size)])
 
 
-def plane_step(kind, part):
-    return (kind if part % 2 == 0 else PLANES - kind) + 4 * (part // 2)
+REACH = tuple(
+    tuple(((4, 1, 7, 6) if kind < 4 else (0, 2, 3, 5))[(kind + part) % 4] for part in range(4))
+    for kind in range(PLANES)
+)
 
 
 def from_plane(value, part):
     pairs = []
     for y in range(8):
         for x in range(4):
-            step = plane_step((y % 2) * 4 + x, part)
+            step = REACH[(y % 2) * 4 + x][part]
             for core in range(2):
                 base = ((y * 4 + x) * 2 + core) * PLANES
                 pairs += [(base + (z + step) % PLANES, base + z) for z in range(PLANES)]
     return lax.ppermute(value, ("y", "x", "core", "mp"), pairs)
 
 
-def score_kernel(where_ref, acts_ref, *refs):
+def thirds(value):
+    high = value.astype(BF16)
+    left = value - high.astype(F32)
+    mid = left.astype(BF16)
+    return high, mid, (left - mid.astype(F32)).astype(BF16)
+
+
+def score_kernel(
+    where_ref, acts_ref, *refs,
+):
     pieces = refs[:16]
-    live_ref, route_ref, out_ref, a_ref, w_ref, sq_ref, head_ref, sem = refs[16:]
+    live_ref, route_ref, out_ref, a_ref, w_ref, proj_ref, resid_ref, inv_ref, sem = refs[16:]
     tokens = live_ref.shape[0]
     shard = acts_ref.shape[2]
     core = where_ref[32]
-
-    def fetch(s, p):
-        row = 2 * p + (core if s % 2 == 0 else 1 - core)
-        return pltpu.make_async_copy(
-            pieces[s].at[p], w_ref.at[where_ref[(s // 2) * 4 + p], row], sem.at[s, p]
-        )
-
-    for s in range(16):
-        for p in range(4):
-            fetch(s, p).start()
-    for i in range(PLANES):
-        a_ref[:, i * shard : (i + 1) * shard] = acts_ref[i, 0:tokens, :]
-    for s in range(16):
-        for p in range(4):
-            fetch(s, p).wait()
-    for j in range(PLANES):
-        weights = w_ref[j].reshape(PLANES * shard, shard)
-        proj = jnp.dot(a_ref[...], weights, preferred_element_type=F32)
-        resid = (acts_ref[j, tokens : 2 * tokens, :].astype(F32) + proj).astype(BF16)
-        value = resid.astype(F32)
-        heads = lax.dot_general(
-            resid, acts_ref[j, 2 * tokens :, :], (((1,), (1,)), ((), ())), preferred_element_type=F32
-        )
-        if j == 0:
-            sq_ref[...] = value * value
-            head_ref[...] = heads
-        else:
-            sq_ref[...] += value * value
-            head_ref[...] += heads
-    width = float(PLANES * acts_ref.shape[2])
-    mean_sq = jnp.sum(sq_ref[...], axis=1, keepdims=True) / width
-    scale = lax.rsqrt(mean_sq + NORM_EPS) * live_ref[...]
-    k = lax.broadcasted_iota(jnp.int32, (16, 128), 0)
-    lane = lax.broadcasted_iota(jnp.int32, (16, 128), 1)
-    spread_heads = (k % 8 == lane // TOK).astype(F32)
-    wide = jnp.dot(
-        head_ref[...], spread_heads, precision=lax.Precision.HIGHEST, preferred_element_type=F32
-    )
-    wide = wide * scale
+    def fetch(side, s, p):
+        target = w_ref.at[side, where_ref[8 * p + s], pl.ds(p * shard, shard)]
+        return pltpu.make_async_copy(pieces[2 * s + side].at[p], target, sem.at[side, s, p])
+
+    for side in range(2):
+        for s in range(8):
+            for p in range(4):
+                fetch(side, s, p).start()
+    for p in range(4):
+        a_ref[0, :, p * shard : (p + 1) * shard] = acts_ref[2 * p + core, 0:tokens, :]
+        a_ref[1, :, p * shard : (p + 1) * shard] = acts_ref[2 * p + 1 - core, 0:tokens, :]
+    head_rows = jnp.concatenate([acts_ref[j, 2 * tokens :, :] for j in range(PLANES)], axis=1)
+    for side in range(2):
+        for s in range(8):
+            for p in range(4):
+                fetch(side, s, p).wait()
+        for j in range(PLANES):
+            part = jnp.dot(a_ref[side], w_ref[side, j], preferred_element_type=F32)
+            if side == 0:
+                proj_ref[j] = part
+            else:
+                proj_ref[j] += part
+    step = 16
+    for row in range(0, tokens, step):
+        total = jnp.zeros((step, shard), F32)
+        for j in range(PLANES):
+            hidden = acts_ref[j, tokens + row : tokens + row + step, :].astype(F32)
+            resid = (hidden + proj_ref[j, row : row + step, :]).astype(BF16)
+            resid_ref[row : row + step, j * shard : (j + 1) * shard] = resid
+            value = resid.astype(F32)
+            total = total + value * value
+        mean_sq = jnp.sum(total, axis=1, keepdims=True) / float(PLANES * shard)
+        inv_ref[row : row + step, :] = jnp.broadcast_to(lax.rsqrt(mean_sq + NORM_EPS), (step, 128))
+    heads = lax.dot_general(
+        resid_ref[...], head_rows, (((1,), (1,)), ((), ())), preferred_element_type=F32
+    )
+    k = lax.broadcasted_iota(jnp.int32, (48, 128), 0)
+    lane = lax.broadcasted_iota(jnp.int32, (48, 128), 1)
+    spread_heads = (k % 8 == lane // TOK).astype(BF16)
+    wide = jnp.dot(jnp.concatenate(thirds(heads), axis=1), spread_heads, preferred_element_type=F32)
+    wide = wide * (inv_ref[...] * live_ref[...])
     row = lax.broadcasted_iota(jnp.int32, (tokens, 128), 0)
     col = lax.broadcasted_iota(jnp.int32, (tokens, 128), 1)
     by_token = jnp.where(row % TOK == col % TOK, wide, 0.0)
     by_slot = jnp.where(row // TOK == col % TOK, wide, 0.0)
-    out_ref[:, 0, :] = jnp.dot(
-        route_ref[...], by_token, precision=lax.Precision.HIGHEST, preferred_element_type=F32
-    )
+    routed = jnp.dot(
+        route_ref[...], jnp.concatenate(thirds(by_token), axis=1), preferred_element_type=F32
+    )
+    out_ref[:, 0, :] = routed[:, 0:128] + routed[:, 128:256] + routed[:, 256:384]
     out_ref[:, 1, :] = jnp.broadcast_to(
         jnp.sum(by_slot, axis=0, keepdims=True), (out_ref.shape[0], 128)
     )
@@ -105,10 +119,9 @@
     return pltpu.with_memory_space_constraint(value, pltpu.VMEM)
 
 
-def score(where, *args):
-    owners = args[-1].shape[0]
-    tokens = args[-2].shape[0]
-    width = PLANES * args[0].shape[2]
+def score(where, acts, pieces, live, route):
+    owners, tokens = route.shape
+    shard = acts.shape[2]
     vmem = pl.BlockSpec(memory_space=pltpu.VMEM)
     return pl.pallas_call(
         score_kernel,
@@ -122,15 +135,16 @@
         ],
         out_specs=vmem,
         scratch_shapes=[
-            pltpu.VMEM((tokens, width), BF16),
-            pltpu.VMEM((PLANES, PLANES, args[0].shape[2], args[0].shape[2]), BF16),
-            pltpu.VMEM((tokens, args[0].shape[2]), F32),
-            pltpu.VMEM((tokens, 16), F32),
-            pltpu.SemaphoreType.DMA((16, 4)),
+            pltpu.VMEM((2, tokens, 4 * shard), BF16),
+            pltpu.VMEM((2, PLANES, 4 * shard, shard), BF16),
+            pltpu.VMEM((PLANES, tokens, shard), F32),
+            pltpu.VMEM((tokens, PLANES * shard), BF16),
+            pltpu.VMEM((tokens, 128), F32),
+            pltpu.SemaphoreType.DMA((2, 8, 4)),
         ],
         compiler_params=pltpu.CompilerParams(vmem_limit_bytes=24 * 2**20),
         name="score",
-    )(where, in_vmem(args[0]), *[pltpu.with_memory_space_constraint(v, pltpu.HBM) for v in args[1:17]], *args[17:])
+    )(where, in_vmem(acts), *[pltpu.with_memory_space_constraint(v, pltpu.HBM) for v in pieces], live, route)
 
 
 def finish_kernel(totals_ref, lengths_ref, rank_ref, out_ref):
@@ -164,7 +178,7 @@
         out_specs=vmem,
         compiler_params=pltpu.CompilerParams(vmem_limit_bytes=8 * 2**20),
         name="finish",
-    )(in_vmem(totals), lengths[None, :], rank[None])
+    )(in_vmem(totals), lengths, rank[None])
 
 
 def local(hidden, attn_out, out_proj, norm_gain, reward_proj, block_seq, block_dest, lengths):
@@ -202,18 +216,22 @@
     right1 = shift(second, "x", -1)
     far0 = shift(left0, "x", 1)
     far1 = shift(right1, "x", -1)
-    named = {
-        "c0": first, "c1": second, "cl0": left0, "cl1": left1,
-        "cr0": right0, "cr1": right1, "cf0": far0, "cf1": far1,
+    held = {
+        "c0": first, "c1": second, "cl0": left0, "cr0": right0,
+        "cl1": left1, "cr1": right1, "cf0": far0, "cf1": far1,
     }
     pieces = []
-    for own in named.values():
+    for own in held.values():
         pieces += [own, swap(own, "core")]
-    odd = jnp.array([0, 1, 0, 1, 0, 1, 0, 1], jnp.int32)
-    away = jnp.array([0, 0, 3, 3, 1, 1, 2, 2], jnp.int32)
+    slot = jnp.arange(8, dtype=jnp.int32)
+    odd = ((slot == 1) | (slot == 4) | (slot == 5) | (slot == 7)).astype(jnp.int32)
+    away = jnp.where(slot < 2, 0, jnp.where(slot > 5, 2, 3 - 2 * (slot % 2)))
     kind = (parity ^ odd) * 4 + (x + away) % 4
-    held = [(plane + plane_step(kind, p)) % PLANES for p in range(4)]
-    where = jnp.concatenate([jnp.stack(held, axis=1).reshape(32), core[None]]).astype(jnp.int32)
+    turn = (kind[None, :] + jnp.arange(4, dtype=jnp.int32)[:, None]) % 4
+    low_kind = jnp.where(turn == 0, 4, jnp.where(turn == 1, 1, 9 - turn))
+    high_kind = jnp.where(turn == 0, 0, jnp.where(turn == 3, 5, turn + 1))
+    reach = jnp.where(kind[None, :] < 4, low_kind, high_kind)
+    where = jnp.concatenate([((plane + reach) % PLANES).reshape(32), core[None]]).astype(jnp.int32)
 
     all_slots = jnp.arange(block_seq.shape[0], dtype=jnp.int32)
     mine = rank * slots_in + jnp.arange(slots_in, dtype=jnp.int32)
@@ -226,17 +244,21 @@
     valid = jnp.where(dest_in >= 0, jnp.minimum(block_len, length_in - block_len * order), 0)
     at = plane * TOK + jnp.arange(TOK, dtype=jnp.int32)
     live = (at[None, :] < valid[:, None]).astype(F32).reshape(tokens, 1)
+    live = jnp.broadcast_to(live, (tokens, 128))
     owner_in = jnp.where(dest_in >= 0, dest_in // OWN_CAP, -1)
     owner_of = jnp.broadcast_to(owner_in[:, None], (slots_in, TOK)).reshape(1, tokens)
-    route = (jnp.arange(owners, dtype=jnp.int32)[:, None] == owner_of).astype(F32)
-
-    sent = score(where, acts, *pieces, live, route)
-    got = exchange(sent, ("y", "x", "core"))
+    route = (jnp.arange(owners, dtype=jnp.int32)[:, None] == owner_of).astype(BF16)
 
     targets = rank * OWN_CAP + jnp.arange(OWN_CAP, dtype=jnp.int32)
     source = jnp.sum(jnp.where(block_dest[None, :] == targets[:, None], all_slots[None, :], 0), axis=1)
-    pick = ((source // slots_in)[:, None] == jnp.arange(owners, dtype=jnp.int32)[None, :]).astype(F32)
-    member = (block_seq[:, None] == seq_ids[None, :]).astype(F32)
+    source, tall, wide, where = lax.optimization_barrier(
+        (source // slots_in, block_seq, lengths[None, :], where)
+    )
+    sent = score(where, acts, pieces, live, route)
+    got = exchange(sent, ("y", "x", "core"))
+
+    pick = (source[:, None] == jnp.arange(owners, dtype=jnp.int32)[None, :]).astype(F32)
+    member = (tall[:, None] == seq_ids[None, :]).astype(F32)
 
     owned = jnp.dot(pick, got[:, 0, :], precision=lax.Precision.HIGHEST)
     sums = got[:, 1, :].reshape(owners, 8, TOK)[:, :, :slots_in].swapaxes(0, 1).reshape(8, owners * slots_in)
@@ -247,7 +269,7 @@
         final[:, :OWN_CAP].reshape(PLANES, OWN_CAP, 8, TOK).transpose(1, 2, 0, 3).reshape(OWN_CAP, 8, block_len)
     )
     totals = final[:, OWN_CAP:].reshape(PLANES, 8, seq_count)
-    return token_rewards, finish(totals, lengths, rank, seq_local).reshape(seq_local)
+    return token_rewards, finish(totals, wide, rank, seq_local).reshape(seq_local)
 
 
 def solution(mesh):

time: 181 us -> 175 us (0.967)
  blocking collectives: 0 us -> 30.9 us
  waiting for transfers between devices: 78.8 us -> 55.5 us
  starting transfers between devices: 78.9 us -> 72 us
  Pallas kernels: 11.3 us -> 7.07 us
  local copies, waits for them, and re-layouts: 6.36 us -> 3.79 us
    all_to_all x0 -> x2, blocking collectives: none -> 30.9 us  [exchange(): return lax.all_to_all(value, axis, split_axis=0, concat_axis=0, tiled=True)]
    all_to_all x3 -> x1, waiting for transfers between devices: 19 us -> 0.01 us  [exchange(): return lax.all_to_all(value, axis, split_axis=0, concat_axis=0, tiled=True)]
    all_to_all x3 -> x1, starting transfers between devices: 24.4 us -> 11 us  [exchange(): return lax.all_to_all(value, axis, split_axis=0, concat_axis=0, tiled=True)]
    ppermute x4, starting transfers between devices: 10.5 us -> 15.9 us  [from_plane(): return lax.ppermute(value, ('y', 'x', 'core', 'mp'), pairs)]
    ppermute x4, waiting for transfers between devices: 50.7 us -> 46.2 us  [from_plane(): return lax.ppermute(value, ('y', 'x', 'core', 'mp'), pairs)]
    pallas_call x1, Pallas kernels: 10.9 us -> 6.72 us  [score(): pl.pallas_call(score_kernel, out_shape=jax.ShapeDtypeStruct((owners, 2, 1...]
    ppermute x9, starting transfers between devices: 24.6 us -> 27.8 us  [swap(): return lax.ppermute(value, axis, [(s, s ^ 1) for s in range(size)])]
    ppermute x9, waiting for transfers between devices: 2.55 us -> 5.47 us  [swap(): return lax.ppermute(value, axis, [(s, s ^ 1) for s in range(size)])]
  transfers between devices with their start and end apart: 22 -> 20, of which waited for: 7 -> 7; matrix products, arithmetic and copies ran while one was open for 1% -> 1% of each run, Pallas kernels for 0% -> 0%
where the time goes in v1:
time: 175 us; the launch traced here: 174 us
  starting transfers between devices  72 us (41%)
  waiting for transfers between devices  55.5 us (32%)
  blocking collectives  30.9 us (18%)
  Pallas kernels  7.07 us (4%)
  local copies, waits for them, and re-layouts  3.79 us (2%)
  other arithmetic  3.08 us (2%)
    ppermute x4, waiting for transfers between devices, from_plane(): return lax.ppermute(value, ('y', 'x', 'core', 'mp'), pairs)  46.2 us
    all_to_all x2, blocking collectives, exchange(): return lax.all_to_all(value, axis, split_axis=0, concat_axis=0, tiled=True)  30.9 us
    ppermute x9, starting transfers between devices, swap(): return lax.ppermute(value, axis, [(s, s ^ 1) for s in range(size)])  27.8 us
    ppermute x6, starting transfers between devices, shift(): lax.ppermute(value, axis, [(s, (s + step) % size) for s in range(size)])  17.2 us
    ppermute x4, starting transfers between devices, from_plane(): return lax.ppermute(value, ('y', 'x', 'core', 'mp'), pairs)  15.9 us
    all_to_all x1, starting transfers between devices, exchange(): return lax.all_to_all(value, axis, split_axis=0, concat_axis=0, tiled=True)  11 us
    pallas_call x1, Pallas kernels, score(): pl.pallas_call(score_kernel, out_shape=jax.ShapeDtypeStruct((owners, 2, 1...  6.72 us
    ppermute x9, waiting for transfers between devices, swap(): return lax.ppermute(value, axis, [(s, s ^ 1) for s in range(size)])  5.47 us
  transfers between devices with their start and end apart: 20, of which 7 were waited for; matrix products, arithmetic and copies ran while one was open for 1% of the time, Pallas kernels for 0%

profile of v1, /device:TPU:1, one launch (start us, length us, event | category | flops | bytes accessed | tf_op | source)
XLA Modules:
  0.0 174.4 jit_solution(18324774331075375896)
XLA Ops:
  0.7 1.3 copy.31
  2.0 0.1 copy-done.2
  2.3 1.5 pad_maximum_fusion
  3.7 11.0 %all-to-all-start = ((bf16[8,496,256]{2,1,0:T(8,128)(2,1)}), bf16[8,496,256]{2,1,0:T(8,128)(2,1)S(1)}, u32[]{:S(2)}, u32[]{:S(2)}) async-start(bf16[8,496,256]{2,1,0:T(8,128)(2,1)} %pad_maximum_fusion), calls=%async_computation | async-start | bytes 4063232 | tf_op jit(solution)/shard_map/all_to_all | solution.py:19
  14.8 3.4 %collective-permute-start.2 = (bf16[256,256]{1,0:T(8,128)(2,1)S(1)}, bf16[256,256]{1,0:T(8,128)(2,1)S(1)}, u32[]{:S(2)}, u32[]{:S(2)}) collective-permute-start(bf16[256,256]{1,0:T(8,128)(2,1)S(1)} %dynamic-slice_bitcast_fusion.1), channel_id=1, source_target_pairs={{7,0},{0,1},{1,2},{2,3},{3,4},{4,5},{5,6},{6,7},{15,8},{8,9},{9,10... | collective-permute-start | bytes 393224 | tf_op jit(solution)/shard_map/ppermute | solution.py:46
  18.2 4.0 %collective-permute-start.3 = (bf16[256,256]{1,0:T(8,128)(2,1)S(1)}, bf16[256,256]{1,0:T(8,128)(2,1)S(1)}, u32[]{:S(2)}, u32[]{:S(2)}) collective-permute-start(bf16[256,256]{1,0:T(8,128)(2,1)S(1)} %dynamic-slice_bitcast_fusion), channel_id=1, source_target_pairs={{6,0},{7,1},{0,2},{1,3},{2,4},{3,5},{4,6},{5,7},{14,8},{15,9},{8,1... | collective-permute-start | bytes 393224 | tf_op jit(solution)/shard_map/ppermute | solution.py:46
  22.3 3.4 %collective-permute-start.1 = (bf16[256,256]{1,0:T(8,128)(2,1)S(1)}, bf16[256,256]{1,0:T(8,128)(2,1)S(1)}, u32[]{:S(2)}, u32[]{:S(2)}) collective-permute-start(bf16[256,256]{1,0:T(8,128)(2,1)S(1)} %dynamic-slice_bitcast_fusion.2), channel_id=1, source_target_pairs={{1,0},{2,1},{3,2},{4,3},{5,4},{6,5},{7,6},{0,7},{9,8},{10,9},{11,1... | collective-permute-start | bytes 393224 | tf_op jit(solution)/shard_map/ppermute | solution.py:46
  25.7 5.2 %collective-permute-start = (bf16[256,256]{1,0:T(8,128)(2,1)S(1)}, bf16[256,256]{1,0:T(8,128)(2,1)S(1)}, u32[]{:S(2)}, u32[]{:S(2)}) collective-permute-start(bf16[256,256]{1,0:T(8,128)(2,1)S(1)} %dynamic-slice_bitcast_fusion.3), channel_id=1, source_target_pairs={{4,0},{5,1},{6,2},{7,3},{0,4},{1,5},{2,6},{3,7},{12,8},{13,9},{14,... | collective-permute-start | bytes 393224 | tf_op jit(solution)/shard_map/ppermute | solution.py:46
  30.9 32.7 %collective-permute-done.2 = bf16[256,256]{1,0:T(8,128)(2,1)S(1)} collective-permute-done((bf16[256,256]{1,0:T(8,128)(2,1)S(1)}, bf16[256,256]{1,0:T(8,128)(2,1)S(1)}, u32[]{:S(2)}, u32[]{:S(2)}) %collective-permute-start.2) | collective-permute-done | bytes 131104 | tf_op jit(solution)/shard_map/ppermute | solution.py:46
  63.6 5.9 %collective-permute-done.3 = bf16[256,256]{1,0:T(8,128)(2,1)S(1)} collective-permute-done((bf16[256,256]{1,0:T(8,128)(2,1)S(1)}, bf16[256,256]{1,0:T(8,128)(2,1)S(1)}, u32[]{:S(2)}, u32[]{:S(2)}) %collective-permute-start.3) | collective-permute-done | bytes 131104 | tf_op jit(solution)/shard_map/ppermute | solution.py:46
  69.5 7.6 %collective-permute-done = bf16[256,256]{1,0:T(8,128)(2,1)S(1)} collective-permute-done((bf16[256,256]{1,0:T(8,128)(2,1)S(1)}, bf16[256,256]{1,0:T(8,128)(2,1)S(1)}, u32[]{:S(2)}, u32[]{:S(2)}) %collective-permute-start) | collective-permute-done | bytes 131104 | tf_op jit(solution)/shard_map/ppermute | solution.py:46
  77.2 1.9 %collective-permute-start.5 = (bf16[4,256,256]{2,1,0:T(8,128)(2,1)S(1)}, bf16[4,256,256]{2,1,0:T(8,128)(2,1)S(1)}, u32[]{:S(2)}, u32[]{:S(2)}) collective-permute-start(bf16[4,256,256]{2,1,0:T(8,128)(2,1)S(1)} %pad_maximum_fusion.1.refs_0_), channel_id=1, source_target_pairs={{0,64},{64,0},{128,192},{192,128},{256,320},{320,256},{384,448},{4... | collective-permute-start | bytes 1572872 | tf_op jit(solution)/shard_map/ppermute | solution.py:29
  79.1 0.1 broadcast_in_dim.107
  79.4 3.7 %collective-permute-start.9 = (bf16[4,256,256]{2,1,0:T(8,128)(2,1)S(1)}, bf16[4,256,256]{2,1,0:T(8,128)(2,1)}, u32[]{:S(2)}, u32[]{:S(2)}) collective-permute-start(bf16[4,256,256]{2,1,0:T(8,128)(2,1)S(1)} %pad_maximum_fusion.1.refs_0_), channel_id=1, source_target_pairs={{0,48},{16,0},{32,16},{48,32},{1,49},{17,1},{33,17},{49,33},{2,50}... | collective-permute-start | bytes 1572872 | tf_op jit(solution)/shard_map/ppermute | solution.py:24
  83.2 1.9 %collective-permute-start.7 = (bf16[4,256,256]{2,1,0:T(8,128)(2,1)S(1)}, bf16[4,256,256]{2,1,0:T(8,128)(2,1)}, u32[]{:S(2)}, u32[]{:S(2)}) collective-permute-start(bf16[4,256,256]{2,1,0:T(8,128)(2,1)S(1)} %pad_maximum_fusion.1.refs_0_), channel_id=1, source_target_pairs={{0,16},{16,32},{32,48},{48,0},{1,17},{17,33},{33,49},{49,1},{2,18}... | collective-permute-start | bytes 1572872 | tf_op jit(solution)/shard_map/ppermute | solution.py:24
  85.1 3.6 %collective-permute-start.4 = (bf16[4,256,256]{2,1,0:T(8,128)(2,1)S(1)}, bf16[4,256,256]{2,1,0:T(8,128)(2,1)S(1)}, u32[]{:S(2)}, u32[]{:S(2)}) collective-permute-start(bf16[4,256,256]{2,1,0:T(8,128)(2,1)S(1)} %pad_maximum_fusion.1.refs_0_), channel_id=1, source_target_pairs={{0,8},{8,0},{1,9},{9,1},{2,10},{10,2},{3,11},{11,3},{4,12},{12,4},... | collective-permute-start | bytes 1572872 | tf_op jit(solution)/shard_map/ppermute | solution.py:29
  88.7 3.5 %collective-permute-done.5.refs_2_ = bf16[4,256,256]{2,1,0:T(8,128)(2,1)S(1)} collective-permute-done((bf16[4,256,256]{2,1,0:T(8,128)(2,1)S(1)}, bf16[4,256,256]{2,1,0:T(8,128)(2,1)S(1)}, u32[]{:S(2)}, u32[]{:S(2)}) %collective-permute-start.5) | collective-permute-done | bytes 524320 | tf_op jit(solution)/shard_map/ppermute | solution.py:29
  92.1 2.8 %collective-permute-start.13 = (bf16[4,256,256]{2,1,0:T(8,128)(2,1)S(1)}, bf16[4,256,256]{2,1,0:T(8,128)(2,1)}, u32[]{:S(2)}, u32[]{:S(2)}) collective-permute-start(bf16[4,256,256]{2,1,0:T(8,128)(2,1)S(1)} %collective-permute-done.5.refs_2_), channel_id=1, source_target_pairs={{0,48},{16,0},{32,16},{48,32},{1,49},{17,1},{33,17},{49,33},{2,50}... | collective-permute-start | bytes 1572872 | tf_op jit(solution)/shard_map/ppermute | solution.py:24
  95.1 0.2 select_reduce_fusion
  95.3 2.9 %collective-permute-done.7.refs_4_ = bf16[4,256,256]{2,1,0:T(8,128)(2,1)} collective-permute-done((bf16[4,256,256]{2,1,0:T(8,128)(2,1)S(1)}, bf16[4,256,256]{2,1,0:T(8,128)(2,1)}, u32[]{:S(2)}, u32[]{:S(2)}) %collective-permute-start.7) | collective-permute-done | bytes 524320 | tf_op jit(solution)/shard_map/ppermute | solution.py:24
  98.2 1.9 %collective-permute-start.15 = (bf16[4,256,256]{2,1,0:T(8,128)(2,1)}, bf16[4,256,256]{2,1,0:T(8,128)(2,1)}, u32[]{:S(2)}, u32[]{:S(2)}) collective-permute-start(bf16[4,256,256]{2,1,0:T(8,128)(2,1)} %collective-permute-done.7.refs_4_), channel_id=1, source_target_pairs={{0,16},{16,32},{32,48},{48,0},{1,17},{17,33},{33,49},{49,1},{2,18}... | collective-permute-start | bytes 1572872 | tf_op jit(solution)/shard_map/ppermute | solution.py:24
  100.1 4.4 %collective-permute-start.8 = (bf16[4,256,256]{2,1,0:T(8,128)(2,1)}, bf16[4,256,256]{2,1,0:T(8,128)(2,1)}, u32[]{:S(2)}, u32[]{:S(2)}) collective-permute-start(bf16[4,256,256]{2,1,0:T(8,128)(2,1)} %collective-permute-done.7.refs_4_), channel_id=1, source_target_pairs={{0,8},{8,0},{1,9},{9,1},{2,10},{10,2},{3,11},{11,3},{4,12},{12,4},... | collective-permute-start | bytes 1572872 | tf_op jit(solution)/shard_map/ppermute | solution.py:29
  104.6 1.9 %collective-permute-start.11 = (bf16[4,256,256]{2,1,0:T(8,128)(2,1)S(1)}, bf16[4,256,256]{2,1,0:T(8,128)(2,1)}, u32[]{:S(2)}, u32[]{:S(2)}) collective-permute-start(bf16[4,256,256]{2,1,0:T(8,128)(2,1)S(1)} %collective-permute-done.5.refs_2_), channel_id=1, source_target_pairs={{0,16},{16,32},{32,48},{48,0},{1,17},{17,33},{33,49},{49,1},{2,18}... | collective-permute-start | bytes 1572872 | tf_op jit(solution)/shard_map/ppermute | solution.py:24
  106.5 1.9 %collective-permute-start.10 = (bf16[4,256,256]{2,1,0:T(8,128)(2,1)}, bf16[4,256,256]{2,1,0:T(8,128)(2,1)}, u32[]{:S(2)}, u32[]{:S(2)}) collective-permute-start(bf16[4,256,256]{2,1,0:T(8,128)(2,1)} %collective-permute-done.9.refs_6_), channel_id=1, source_target_pairs={{0,8},{8,0},{1,9},{9,1},{2,10},{10,2},{3,11},{11,3},{4,12},{12,4},... | collective-permute-start | bytes 1572872 | tf_op jit(solution)/shard_map/ppermute | solution.py:29
  108.5 4.9 %collective-permute-start.17 = (bf16[4,256,256]{2,1,0:T(8,128)(2,1)}, bf16[4,256,256]{2,1,0:T(8,128)(2,1)}, u32[]{:S(2)}, u32[]{:S(2)}) collective-permute-start(bf16[4,256,256]{2,1,0:T(8,128)(2,1)} %collective-permute-done.13.refs_10_), channel_id=1, source_target_pairs={{0,48},{16,0},{32,16},{48,32},{1,49},{17,1},{33,17},{49,33},{2,50}... | collective-permute-start | bytes 1572872 | tf_op jit(solution)/shard_map/ppermute | solution.py:24
  113.3 0.2 select_reduce_fusion.1
  113.5 0.2 convert_reduce_fusion
  113.7 0.1 compare_select_fusion.10
  114.0 2.7 %collective-permute-start.6 = (bf16[4,256,256]{2,1,0:T(8,128)(2,1)S(1)}, bf16[4,256,256]{2,1,0:T(8,128)(2,1)}, u32[]{:S(2)}, u32[]{:S(2)}) collective-permute-start(bf16[4,256,256]{2,1,0:T(8,128)(2,1)S(1)} %collective-permute-done.5.refs_2_), channel_id=1, source_target_pairs={{0,8},{8,0},{1,9},{9,1},{2,10},{10,2},{3,11},{11,3},{4,12},{12,4},... | collective-permute-start | bytes 1572872 | tf_op jit(solution)/shard_map/ppermute | solution.py:29
  116.7 4.1 %collective-permute-start.14 = (bf16[4,256,256]{2,1,0:T(8,128)(2,1)}, bf16[4,256,256]{2,1,0:T(8,128)(2,1)}, u32[]{:S(2)}, u32[]{:S(2)}) collective-permute-start(bf16[4,256,256]{2,1,0:T(8,128)(2,1)} %collective-permute-done.13.refs_10_), channel_id=1, source_target_pairs={{0,8},{8,0},{1,9},{9,1},{2,10},{10,2},{3,11},{11,3},{4,12},{12,4},... | collective-permute-start | bytes 1572872 | tf_op jit(solution)/shard_map/ppermute | solution.py:29
  120.8 1.9 %collective-permute-start.16 = (bf16[4,256,256]{2,1,0:T(8,128)(2,1)}, bf16[4,256,256]{2,1,0:T(8,128)(2,1)}, u32[]{:S(2)}, u32[]{:S(2)}) collective-permute-start(bf16[4,256,256]{2,1,0:T(8,128)(2,1)} %collective-permute-done.15.refs_12_), channel_id=1, source_target_pairs={{0,8},{8,0},{1,9},{9,1},{2,10},{10,2},{3,11},{11,3},{4,12},{12,4},... | collective-permute-start | bytes 1572872 | tf_op jit(solution)/shard_map/ppermute | solution.py:29
  122.8 1.0 collective-permute-done.11.refs_8_
  123.8 5.3 %collective-permute-start.12 = (bf16[4,256,256]{2,1,0:T(8,128)(2,1)}, bf16[4,256,256]{2,1,0:T(8,128)(2,1)}, u32[]{:S(2)}, u32[]{:S(2)}) collective-permute-start(bf16[4,256,256]{2,1,0:T(8,128)(2,1)} %collective-permute-done.11.refs_8_), channel_id=1, source_target_pairs={{0,8},{8,0},{1,9},{9,1},{2,10},{10,2},{3,11},{11,3},{4,12},{12,4},... | collective-permute-start | bytes 1572872 | tf_op jit(solution)/shard_map/ppermute | solution.py:29
  129.1 1.9 %collective-permute-start.18 = (bf16[4,256,256]{2,1,0:T(8,128)(2,1)}, bf16[4,256,256]{2,1,0:T(8,128)(2,1)}, u32[]{:S(2)}, u32[]{:S(2)}) collective-permute-start(bf16[4,256,256]{2,1,0:T(8,128)(2,1)} %collective-permute-done.17.refs_14_), channel_id=1, source_target_pairs={{0,8},{8,0},{1,9},{9,1},{2,10},{10,2},{3,11},{11,3},{4,12},{12,4},... | collective-permute-start | bytes 1572872 | tf_op jit(solution)/shard_map/ppermute | solution.py:29
  131.2 2.0 %collective-permute-done.18.refs_15_ = bf16[4,256,256]{2,1,0:T(8,128)(2,1)} collective-permute-done((bf16[4,256,256]{2,1,0:T(8,128)(2,1)}, bf16[4,256,256]{2,1,0:T(8,128)(2,1)}, u32[]{:S(2)}, u32[]{:S(2)}) %collective-permute-start.18) | collective-permute-done | bytes 524320 | tf_op jit(solution)/shard_map/ppermute | solution.py:29
  133.2 0.1 broadcast_in_dim.113.refs_16_
  133.3 6.7 %score.1 = f32[64,2,128]{2,1,0:T(2,128)S(1)} custom-call(s32[33]{0:T(128)S(1)} %pad_add_fusion.where_ref, bf16[8,496,256]{2,1,0:T(8,128)(2,1)S(1)} %all-to-all-done.acts_ref, bf16[4,256,256]{2,1,0:T(8,128)(2,1)} %copy-done, bf16[4,256,256]{2,1,0:T(8,128)(2,1)} %copy-done.4, bf16[4,256,256]{2,1,0:T(8,128)(2,1)} %copy-done.3, ...), custom_call_target="tpu_custom_call" | custom-call | tf_op jit(solution)/shard_map/score/pallas_call | solution.py:126
  140.1 17.8 %all_to_all.15 = f32[64,2,128]{2,1,0:T(2,128)S(1)} all-to-all(f32[64,2,128]{2,1,0:T(2,128)S(1)} %score.1), channel_id=1, replica_groups=mesh['y'=8,'x'=4,'core'=2,'mp'=8] {'y','x','core'}, dimensions={0} | all-to-all | bytes 131072 | tf_op jit(solution)/shard_map/all_to_all | solution.py:19
  158.0 0.1 copy.32
  158.1 0.1 copy.33
  158.2 0.2 reshape.143
  158.4 0.6 fusion
  159.0 0.2 fusion.5
  159.3 13.1 %all_to_all.16 = f32[8,34,128]{2,1,0:T(8,128)S(1)} all-to-all(f32[8,34,128]{2,1,0:T(8,128)S(1)} %broadcast_in_dim.115), channel_id=1, replica_groups=mesh['y'=8,'x'=4,'core'=2,'mp'=8] {'mp'}, dimensions={0} | all-to-all | bytes 278528 | tf_op jit(solution)/shard_map/all_to_all | solution.py:19
  172.4 0.1 reshape.145
  172.6 0.8 reshape.146
  173.4 0.4 finish.1
  173.7 0.6 reduce
  (69 shorter events, 1.2 us)
Async XLA Ops:
  0.6 1.5 copy-start.2
  0.6 1.6 copy-start.6
  0.7 1.6 copy-start.9
  3.7 11.0 %copy-start.1 = (bf16[2048,256]{1,0:T(8,128)(2,1)S(1)}, bf16[2048,256]{1,0:T(8,128)(2,1)}, u32[]{:S(2)}) copy-start(bf16[2048,256]{1,0:T(8,128)(2,1)} %param.10) | copy-start | bytes 3145732
  3.7 129.5 %all-to-all-start = ((bf16[8,496,256]{2,1,0:T(8,128)(2,1)}), bf16[8,496,256]{2,1,0:T(8,128)(2,1)S(1)}, u32[]{:S(2)}, u32[]{:S(2)}) async-start(bf16[8,496,256]{2,1,0:T(8,128)(2,1)} %pad_maximum_fusion), calls=%async_computation | async-start | bytes 4063232 | tf_op jit(solution)/shard_map/all_to_all | solution.py:19
  14.7 64.5 %copy-start.5 = (s32[384]{0:T(512)S(1)}, s32[384]{0:T(512)}, u32[]{:S(2)}) copy-start(s32[384]{0:T(512)} %param.15) | copy-start | bytes 4612
  14.7 64.6 %copy-start.8 = (s32[960]{0:T(1024)S(1)}, s32[960]{0:T(1024)}, u32[]{:S(2)}) copy-start(s32[960]{0:T(1024)} %param.13) | copy-start | bytes 11524
  14.7 80.4 %copy-start.7 = (s32[960]{0:T(1024)S(1)}, s32[960]{0:T(1024)}, u32[]{:S(2)}) copy-start(s32[960]{0:T(1024)} %param.14) | copy-start | bytes 11524
  14.8 48.7 %collective-permute-start.2 = (bf16[256,256]{1,0:T(8,128)(2,1)S(1)}, bf16[256,256]{1,0:T(8,128)(2,1)S(1)}, u32[]{:S(2)}, u32[]{:S(2)}) collective-permute-start(bf16[256,256]{1,0:T(8,128)(2,1)S(1)} %dynamic-slice_bitcast_fusion.1), channel_id=1, source_target_pairs={{7,0},{0,1},{1,2},{2,3},{3,4},{4,5},{5,6},{6,7},{15,8},{8,9},{9,10... | collective-permute-start | bytes 393224 | tf_op jit(solution)/shard_map/ppermute | solution.py:46
  18.2 51.3 %collective-permute-start.3 = (bf16[256,256]{1,0:T(8,128)(2,1)S(1)}, bf16[256,256]{1,0:T(8,128)(2,1)S(1)}, u32[]{:S(2)}, u32[]{:S(2)}) collective-permute-start(bf16[256,256]{1,0:T(8,128)(2,1)S(1)} %dynamic-slice_bitcast_fusion), channel_id=1, source_target_pairs={{6,0},{7,1},{0,2},{1,3},{2,4},{3,5},{4,6},{5,7},{14,8},{15,9},{8,1... | collective-permute-start | bytes 393224 | tf_op jit(solution)/shard_map/ppermute | solution.py:46
  22.3 47.3 %collective-permute-start.1 = (bf16[256,256]{1,0:T(8,128)(2,1)S(1)}, bf16[256,256]{1,0:T(8,128)(2,1)S(1)}, u32[]{:S(2)}, u32[]{:S(2)}) collective-permute-start(bf16[256,256]{1,0:T(8,128)(2,1)S(1)} %dynamic-slice_bitcast_fusion.2), channel_id=1, source_target_pairs={{1,0},{2,1},{3,2},{4,3},{5,4},{6,5},{7,6},{0,7},{9,8},{10,9},{11,1... | collective-permute-start | bytes 393224 | tf_op jit(solution)/shard_map/ppermute | solution.py:46
  25.7 51.4 %collective-permute-start = (bf16[256,256]{1,0:T(8,128)(2,1)S(1)}, bf16[256,256]{1,0:T(8,128)(2,1)S(1)}, u32[]{:S(2)}, u32[]{:S(2)}) collective-permute-start(bf16[256,256]{1,0:T(8,128)(2,1)S(1)} %dynamic-slice_bitcast_fusion.3), channel_id=1, source_target_pairs={{4,0},{5,1},{6,2},{7,3},{0,4},{1,5},{2,6},{3,7},{12,8},{13,9},{14,... | collective-permute-start | bytes 393224 | tf_op jit(solution)/shard_map/ppermute | solution.py:46
  77.2 56.2 %copy-start = (bf16[4,256,256]{2,1,0:T(8,128)(2,1)}, bf16[4,256,256]{2,1,0:T(8,128)(2,1)S(1)}, u32[]{:S(2)}) copy-start(bf16[4,256,256]{2,1,0:T(8,128)(2,1)S(1)} %pad_maximum_fusion.1.refs_0_) | copy-start | bytes 1572868
  77.2 15.0 %collective-permute-start.5 = (bf16[4,256,256]{2,1,0:T(8,128)(2,1)S(1)}, bf16[4,256,256]{2,1,0:T(8,128)(2,1)S(1)}, u32[]{:S(2)}, u32[]{:S(2)}) collective-permute-start(bf16[4,256,256]{2,1,0:T(8,128)(2,1)S(1)} %pad_maximum_fusion.1.refs_0_), channel_id=1, source_target_pairs={{0,64},{64,0},{128,192},{192,128},{256,320},{320,256},{384,448},{4... | collective-permute-start | bytes 1572872 | tf_op jit(solution)/shard_map/ppermute | solution.py:29
  79.4 25.1 %collective-permute-start.9 = (bf16[4,256,256]{2,1,0:T(8,128)(2,1)S(1)}, bf16[4,256,256]{2,1,0:T(8,128)(2,1)}, u32[]{:S(2)}, u32[]{:S(2)}) collective-permute-start(bf16[4,256,256]{2,1,0:T(8,128)(2,1)S(1)} %pad_maximum_fusion.1.refs_0_), channel_id=1, source_target_pairs={{0,48},{16,0},{32,16},{48,32},{1,49},{17,1},{33,17},{49,33},{2,50}... | collective-permute-start | bytes 1572872 | tf_op jit(solution)/shard_map/ppermute | solution.py:24
  83.2 15.0 %collective-permute-start.7 = (bf16[4,256,256]{2,1,0:T(8,128)(2,1)S(1)}, bf16[4,256,256]{2,1,0:T(8,128)(2,1)}, u32[]{:S(2)}, u32[]{:S(2)}) collective-permute-start(bf16[4,256,256]{2,1,0:T(8,128)(2,1)S(1)} %pad_maximum_fusion.1.refs_0_), channel_id=1, source_target_pairs={{0,16},{16,32},{32,48},{48,0},{1,17},{17,33},{33,49},{49,1},{2,18}... | collective-permute-start | bytes 1572872 | tf_op jit(solution)/shard_map/ppermute | solution.py:24
  85.1 21.4 %collective-permute-start.4 = (bf16[4,256,256]{2,1,0:T(8,128)(2,1)S(1)}, bf16[4,256,256]{2,1,0:T(8,128)(2,1)S(1)}, u32[]{:S(2)}, u32[]{:S(2)}) collective-permute-start(bf16[4,256,256]{2,1,0:T(8,128)(2,1)S(1)} %pad_maximum_fusion.1.refs_0_), channel_id=1, source_target_pairs={{0,8},{8,0},{1,9},{9,1},{2,10},{10,2},{3,11},{11,3},{4,12},{12,4},... | collective-permute-start | bytes 1572872 | tf_op jit(solution)/shard_map/ppermute | solution.py:29
  92.1 41.2 %copy-start.3 = (bf16[4,256,256]{2,1,0:T(8,128)(2,1)}, bf16[4,256,256]{2,1,0:T(8,128)(2,1)S(1)}, u32[]{:S(2)}) copy-start(bf16[4,256,256]{2,1,0:T(8,128)(2,1)S(1)} %collective-permute-done.5.refs_2_) | copy-start | bytes 1572868
  92.1 16.3 %collective-permute-start.13 = (bf16[4,256,256]{2,1,0:T(8,128)(2,1)S(1)}, bf16[4,256,256]{2,1,0:T(8,128)(2,1)}, u32[]{:S(2)}, u32[]{:S(2)}) collective-permute-start(bf16[4,256,256]{2,1,0:T(8,128)(2,1)S(1)} %collective-permute-done.5.refs_2_), channel_id=1, source_target_pairs={{0,48},{16,0},{32,16},{48,32},{1,49},{17,1},{33,17},{49,33},{2,50}... | collective-permute-start | bytes 1572872 | tf_op jit(solution)/shard_map/ppermute | solution.py:24
  98.2 18.5 %collective-permute-start.15 = (bf16[4,256,256]{2,1,0:T(8,128)(2,1)}, bf16[4,256,256]{2,1,0:T(8,128)(2,1)}, u32[]{:S(2)}, u32[]{:S(2)}) collective-permute-start(bf16[4,256,256]{2,1,0:T(8,128)(2,1)} %collective-permute-done.7.refs_4_), channel_id=1, source_target_pairs={{0,16},{16,32},{32,48},{48,0},{1,17},{17,33},{33,49},{49,1},{2,18}... | collective-permute-start | bytes 1572872 | tf_op jit(solution)/shard_map/ppermute | solution.py:24
  100.1 20.7 %collective-permute-start.8 = (bf16[4,256,256]{2,1,0:T(8,128)(2,1)}, bf16[4,256,256]{2,1,0:T(8,128)(2,1)}, u32[]{:S(2)}, u32[]{:S(2)}) collective-permute-start(bf16[4,256,256]{2,1,0:T(8,128)(2,1)} %collective-permute-done.7.refs_4_), channel_id=1, source_target_pairs={{0,8},{8,0},{1,9},{9,1},{2,10},{10,2},{3,11},{11,3},{4,12},{12,4},... | collective-permute-start | bytes 1572872 | tf_op jit(solution)/shard_map/ppermute | solution.py:29
  104.6 19.2 %collective-permute-start.11 = (bf16[4,256,256]{2,1,0:T(8,128)(2,1)S(1)}, bf16[4,256,256]{2,1,0:T(8,128)(2,1)}, u32[]{:S(2)}, u32[]{:S(2)}) collective-permute-start(bf16[4,256,256]{2,1,0:T(8,128)(2,1)S(1)} %collective-permute-done.5.refs_2_), channel_id=1, source_target_pairs={{0,16},{16,32},{32,48},{48,0},{1,17},{17,33},{33,49},{49,1},{2,18}... | collective-permute-start | bytes 1572872 | tf_op jit(solution)/shard_map/ppermute | solution.py:24
  106.5 2.0 %copy-start.4 = (bf16[4,256,256]{2,1,0:T(8,128)(2,1)}, bf16[4,256,256]{2,1,0:T(8,128)(2,1)S(1)}, u32[]{:S(2)}) copy-start(bf16[4,256,256]{2,1,0:T(8,128)(2,1)S(1)} %collective-permute-done.4.refs_1_) | copy-start | bytes 1572868
  106.5 7.4 %collective-permute-start.10 = (bf16[4,256,256]{2,1,0:T(8,128)(2,1)}, bf16[4,256,256]{2,1,0:T(8,128)(2,1)}, u32[]{:S(2)}, u32[]{:S(2)}) collective-permute-start(bf16[4,256,256]{2,1,0:T(8,128)(2,1)} %collective-permute-done.9.refs_6_), channel_id=1, source_target_pairs={{0,8},{8,0},{1,9},{9,1},{2,10},{10,2},{3,11},{11,3},{4,12},{12,4},... | collective-permute-start | bytes 1572872 | tf_op jit(solution)/shard_map/ppermute | solution.py:29
  108.5 20.6 %collective-permute-start.17 = (bf16[4,256,256]{2,1,0:T(8,128)(2,1)}, bf16[4,256,256]{2,1,0:T(8,128)(2,1)}, u32[]{:S(2)}, u32[]{:S(2)}) collective-permute-start(bf16[4,256,256]{2,1,0:T(8,128)(2,1)} %collective-permute-done.13.refs_10_), channel_id=1, source_target_pairs={{0,48},{16,0},{32,16},{48,32},{1,49},{17,1},{33,17},{49,33},{2,50}... | collective-permute-start | bytes 1572872 | tf_op jit(solution)/shard_map/ppermute | solution.py:24
  114.0 17.2 %collective-permute-start.6 = (bf16[4,256,256]{2,1,0:T(8,128)(2,1)S(1)}, bf16[4,256,256]{2,1,0:T(8,128)(2,1)}, u32[]{:S(2)}, u32[]{:S(2)}) collective-permute-start(bf16[4,256,256]{2,1,0:T(8,128)(2,1)S(1)} %collective-permute-done.5.refs_2_), channel_id=1, source_target_pairs={{0,8},{8,0},{1,9},{9,1},{2,10},{10,2},{3,11},{11,3},{4,12},{12,4},... | collective-permute-start | bytes 1572872 | tf_op jit(solution)/shard_map/ppermute | solution.py:29
  116.7 14.6 %collective-permute-start.14 = (bf16[4,256,256]{2,1,0:T(8,128)(2,1)}, bf16[4,256,256]{2,1,0:T(8,128)(2,1)}, u32[]{:S(2)}, u32[]{:S(2)}) collective-permute-start(bf16[4,256,256]{2,1,0:T(8,128)(2,1)} %collective-permute-done.13.refs_10_), channel_id=1, source_target_pairs={{0,8},{8,0},{1,9},{9,1},{2,10},{10,2},{3,11},{11,3},{4,12},{12,4},... | collective-permute-start | bytes 1572872 | tf_op jit(solution)/shard_map/ppermute | solution.py:29
  120.8 10.4 %collective-permute-start.16 = (bf16[4,256,256]{2,1,0:T(8,128)(2,1)}, bf16[4,256,256]{2,1,0:T(8,128)(2,1)}, u32[]{:S(2)}, u32[]{:S(2)}) collective-permute-start(bf16[4,256,256]{2,1,0:T(8,128)(2,1)} %collective-permute-done.15.refs_12_), channel_id=1, source_target_pairs={{0,8},{8,0},{1,9},{9,1},{2,10},{10,2},{3,11},{11,3},{4,12},{12,4},... | collective-permute-start | bytes 1572872 | tf_op jit(solution)/shard_map/ppermute | solution.py:29
  123.8 7.4 %collective-permute-start.12 = (bf16[4,256,256]{2,1,0:T(8,128)(2,1)}, bf16[4,256,256]{2,1,0:T(8,128)(2,1)}, u32[]{:S(2)}, u32[]{:S(2)}) collective-permute-start(bf16[4,256,256]{2,1,0:T(8,128)(2,1)} %collective-permute-done.11.refs_8_), channel_id=1, source_target_pairs={{0,8},{8,0},{1,9},{9,1},{2,10},{10,2},{3,11},{11,3},{4,12},{12,4},... | collective-permute-start | bytes 1572872 | tf_op jit(solution)/shard_map/ppermute | solution.py:29
  129.1 4.1 %collective-permute-start.18 = (bf16[4,256,256]{2,1,0:T(8,128)(2,1)}, bf16[4,256,256]{2,1,0:T(8,128)(2,1)}, u32[]{:S(2)}, u32[]{:S(2)}) collective-permute-start(bf16[4,256,256]{2,1,0:T(8,128)(2,1)} %collective-permute-done.17.refs_14_), channel_id=1, source_target_pairs={{0,8},{8,0},{1,9},{9,1},{2,10},{10,2},{3,11},{11,3},{4,12},{12,4},... | collective-permute-start | bytes 1572872 | tf_op jit(solution)/shard_map/ppermute | solution.py:29

commit v2 on v1

--- a/solution.py
+++ b/solution.py
@@ -22,6 +22,11 @@
 def shift(value, axis, step):
     size = lax.axis_size(axis)
     return lax.ppermute(value, axis, [(s, (s + step) % size) for s in range(size)])
+
+
+def swap_odd(value, axis):
+    size = lax.axis_size(axis)
+    return lax.ppermute(value, axis, [(s, (s + 2 * (s % 2) - 1) % size) for s in range(size)])
 
 
 def swap(value, axis):
@@ -162,18 +167,17 @@
     off = conservative - centre
     variance = jnp.sum(off * off, axis=1, keepdims=True) / count
     advantages = off / jnp.sqrt(variance + STAT_EPS)
-    size = out_ref.shape[0]
-    at = lax.broadcasted_iota(jnp.int32, (size, scores.shape[1]), 1)
-    row = lax.broadcasted_iota(jnp.int32, (size, scores.shape[1]), 0)
-    mine = jnp.where(at == row + rank_ref[0] * size, advantages, 0.0)
-    out_ref[...] = jnp.sum(mine, axis=1, keepdims=True)
+    size = out_ref.shape[1]
+    total = scores.shape[1]
+    turned = pltpu.roll(advantages, total - rank_ref[0] * size, axis=1)
+    out_ref[...] = turned[:, 0:size]
 
 
 def finish(totals, lengths, rank, size):
     vmem = pl.BlockSpec(memory_space=pltpu.VMEM)
     return pl.pallas_call(
         finish_kernel,
-        out_shape=jax.ShapeDtypeStruct((size, 1), F32),
+        out_shape=jax.ShapeDtypeStruct((1, size), F32),
         in_specs=[vmem, vmem, pl.BlockSpec(memory_space=pltpu.SMEM)],
         out_specs=vmem,
         compiler_params=pltpu.CompilerParams(vmem_limit_bytes=8 * 2**20),
@@ -212,10 +216,10 @@
     second = swap(first, "y")
     left0 = shift(first, "x", 1)
     right0 = shift(first, "x", -1)
-    left1 = shift(second, "x", 1)
+    left1 = swap_odd(left0, "y")
     right1 = shift(second, "x", -1)
     far0 = shift(left0, "x", 1)
-    far1 = shift(right1, "x", -1)
+    far1 = swap(far0, "y")
     held = {
         "c0": first, "c1": second, "cl0": left0, "cr0": right0,
         "cl1": left1, "cr1": right1, "cf0": far0, "cf1": far1,

time: 175 us -> 170 us (0.971)
  waiting for transfers between devices: 55.5 us -> 53.4 us
  starting transfers between devices: 72 us -> 70.1 us
    ppermute x6 -> x4, starting transfers between devices: 17.2 us -> 13 us  [shift(): lax.ppermute(value, axis, [(s, (s + step) % size) for s in range(size)])]
    ppermute x9 -> x10, waiting for transfers between devices: 5.47 us -> 2.53 us  [swap(): return lax.ppermute(value, axis, [(s, s ^ 1) for s in range(size)])]
    ppermute x0 -> x1, starting transfers between devices: none -> 2.13 us  [swap_odd(): lax.ppermute(value, axis, [(s, (s + 2 * (s % 2) - 1) % size) for s in ran...]
    ppermute x6 -> x4, waiting for transfers between devices: 3.92 us -> 4.72 us  [shift(): lax.ppermute(value, axis, [(s, (s + step) % size) for s in range(size)])]
    ppermute x9 -> x10, starting transfers between devices: 27.8 us -> 28.1 us  [swap(): return lax.ppermute(value, axis, [(s, s ^ 1) for s in range(size)])]
where the time goes in v2:
time: 170 us; the launch traced here: 169 us
  starting transfers between devices  70.1 us (41%)
  waiting for transfers between devices  53.4 us (31%)
  blocking collectives  29.8 us (18%)
  Pallas kernels  7.59 us (4%)
  local copies, waits for them, and re-layouts  3.79 us (2%)
  other arithmetic  2.42 us (1%)
    ppermute x4, waiting for transfers between devices, from_plane(): return lax.ppermute(value, ('y', 'x', 'core', 'mp'), pairs)  46.2 us
    all_to_all x2, blocking collectives, exchange(): return lax.all_to_all(value, axis, split_axis=0, concat_axis=0, tiled=True)  29.8 us
    ppermute x10, starting transfers between devices, swap(): return lax.ppermute(value, axis, [(s, s ^ 1) for s in range(size)])  28.1 us
    ppermute x4, starting transfers between devices, from_plane(): return lax.ppermute(value, ('y', 'x', 'core', 'mp'), pairs)  15.9 us
    ppermute x4, starting transfers between devices, shift(): lax.ppermute(value, axis, [(s, (s + step) % size) for s in range(size)])  13 us
    all_to_all x1, starting transfers between devices, exchange(): return lax.all_to_all(value, axis, split_axis=0, concat_axis=0, tiled=True)  11 us
    pallas_call x1, Pallas kernels, score(): pl.pallas_call(score_kernel, out_shape=jax.ShapeDtypeStruct((owners, 2, 1...  6.72 us
    ppermute x4, waiting for transfers between devices, shift(): lax.ppermute(value, axis, [(s, (s + step) % size) for s in range(size)])  4.72 us
  transfers between devices with their start and end apart: 20, of which 7 were waited for; matrix products, arithmetic and copies ran while one was open for 1% of the time, Pallas kernels for 0%

profile of v2, /device:TPU:1, one launch (start us, length us, event | category | flops | bytes accessed | tf_op | source)
XLA Modules:
  0.0 169.2 jit_solution(4692902201498305218)
XLA Ops:
  0.7 1.3 copy.31
  2.0 0.1 copy-done.2
  2.3 1.4 pad_maximum_fusion
  3.7 11.0 %all-to-all-start = ((bf16[8,496,256]{2,1,0:T(8,128)(2,1)}), bf16[8,496,256]{2,1,0:T(8,128)(2,1)S(1)}, u32[]{:S(2)}, u32[]{:S(2)}) async-start(bf16[8,496,256]{2,1,0:T(8,128)(2,1)} %pad_maximum_fusion), calls=%async_computation | async-start | bytes 4063232 | tf_op jit(solution)/shard_map/all_to_all | solution.py:19
  14.8 3.4 %collective-permute-start.2 = (bf16[256,256]{1,0:T(8,128)(2,1)S(1)}, bf16[256,256]{1,0:T(8,128)(2,1)S(1)}, u32[]{:S(2)}, u32[]{:S(2)}) collective-permute-start(bf16[256,256]{1,0:T(8,128)(2,1)S(1)} %dynamic-slice_bitcast_fusion.1), channel_id=1, source_target_pairs={{7,0},{0,1},{1,2},{2,3},{3,4},{4,5},{5,6},{6,7},{15,8},{8,9},{9,10... | collective-permute-start | bytes 393224 | tf_op jit(solution)/shard_map/ppermute | solution.py:51
  18.2 4.0 %collective-permute-start.3 = (bf16[256,256]{1,0:T(8,128)(2,1)S(1)}, bf16[256,256]{1,0:T(8,128)(2,1)S(1)}, u32[]{:S(2)}, u32[]{:S(2)}) collective-permute-start(bf16[256,256]{1,0:T(8,128)(2,1)S(1)} %dynamic-slice_bitcast_fusion), channel_id=1, source_target_pairs={{6,0},{7,1},{0,2},{1,3},{2,4},{3,5},{4,6},{5,7},{14,8},{15,9},{8,1... | collective-permute-start | bytes 393224 | tf_op jit(solution)/shard_map/ppermute | solution.py:51
  22.2 3.4 %collective-permute-start.1 = (bf16[256,256]{1,0:T(8,128)(2,1)S(1)}, bf16[256,256]{1,0:T(8,128)(2,1)S(1)}, u32[]{:S(2)}, u32[]{:S(2)}) collective-permute-start(bf16[256,256]{1,0:T(8,128)(2,1)S(1)} %dynamic-slice_bitcast_fusion.2), channel_id=1, source_target_pairs={{1,0},{2,1},{3,2},{4,3},{5,4},{6,5},{7,6},{0,7},{9,8},{10,9},{11,1... | collective-permute-start | bytes 393224 | tf_op jit(solution)/shard_map/ppermute | solution.py:51
  25.7 5.2 %collective-permute-start = (bf16[256,256]{1,0:T(8,128)(2,1)S(1)}, bf16[256,256]{1,0:T(8,128)(2,1)S(1)}, u32[]{:S(2)}, u32[]{:S(2)}) collective-permute-start(bf16[256,256]{1,0:T(8,128)(2,1)S(1)} %dynamic-slice_bitcast_fusion.3), channel_id=1, source_target_pairs={{4,0},{5,1},{6,2},{7,3},{0,4},{1,5},{2,6},{3,7},{12,8},{13,9},{14,... | collective-permute-start | bytes 393224 | tf_op jit(solution)/shard_map/ppermute | solution.py:51
  30.9 32.7 %collective-permute-done.2 = bf16[256,256]{1,0:T(8,128)(2,1)S(1)} collective-permute-done((bf16[256,256]{1,0:T(8,128)(2,1)S(1)}, bf16[256,256]{1,0:T(8,128)(2,1)S(1)}, u32[]{:S(2)}, u32[]{:S(2)}) %collective-permute-start.2) | collective-permute-done | bytes 131104 | tf_op jit(solution)/shard_map/ppermute | solution.py:51
  63.6 5.9 %collective-permute-done.3 = bf16[256,256]{1,0:T(8,128)(2,1)S(1)} collective-permute-done((bf16[256,256]{1,0:T(8,128)(2,1)S(1)}, bf16[256,256]{1,0:T(8,128)(2,1)S(1)}, u32[]{:S(2)}, u32[]{:S(2)}) %collective-permute-start.3) | collective-permute-done | bytes 131104 | tf_op jit(solution)/shard_map/ppermute | solution.py:51
  69.5 7.6 %collective-permute-done = bf16[256,256]{1,0:T(8,128)(2,1)S(1)} collective-permute-done((bf16[256,256]{1,0:T(8,128)(2,1)S(1)}, bf16[256,256]{1,0:T(8,128)(2,1)S(1)}, u32[]{:S(2)}, u32[]{:S(2)}) %collective-permute-start) | collective-permute-done | bytes 131104 | tf_op jit(solution)/shard_map/ppermute | solution.py:51
  77.2 1.9 %collective-permute-start.7 = (bf16[4,256,256]{2,1,0:T(8,128)(2,1)S(1)}, bf16[4,256,256]{2,1,0:T(8,128)(2,1)S(1)}, u32[]{:S(2)}, u32[]{:S(2)}) collective-permute-start(bf16[4,256,256]{2,1,0:T(8,128)(2,1)S(1)} %pad_maximum_fusion.1.refs_0_), channel_id=1, source_target_pairs={{0,16},{16,32},{32,48},{48,0},{1,17},{17,33},{33,49},{49,1},{2,18}... | collective-permute-start | bytes 1572872 | tf_op jit(solution)/shard_map/ppermute | solution.py:24
  79.1 0.1 broadcast_in_dim.107
  79.2 0.1 add.154
  79.4 4.6 %collective-permute-start.9 = (bf16[4,256,256]{2,1,0:T(8,128)(2,1)S(1)}, bf16[4,256,256]{2,1,0:T(8,128)(2,1)}, u32[]{:S(2)}, u32[]{:S(2)}) collective-permute-start(bf16[4,256,256]{2,1,0:T(8,128)(2,1)S(1)} %pad_maximum_fusion.1.refs_0_), channel_id=1, source_target_pairs={{0,48},{16,0},{32,16},{48,32},{1,49},{17,1},{33,17},{49,33},{2,50}... | collective-permute-start | bytes 1572872 | tf_op jit(solution)/shard_map/ppermute | solution.py:24
  84.0 1.9 %collective-permute-start.5 = (bf16[4,256,256]{2,1,0:T(8,128)(2,1)S(1)}, bf16[4,256,256]{2,1,0:T(8,128)(2,1)}, u32[]{:S(2)}, u32[]{:S(2)}) collective-permute-start(bf16[4,256,256]{2,1,0:T(8,128)(2,1)S(1)} %pad_maximum_fusion.1.refs_0_), channel_id=1, source_target_pairs={{0,64},{64,0},{128,192},{192,128},{256,320},{320,256},{384,448},{4... | collective-permute-start | bytes 1572872 | tf_op jit(solution)/shard_map/ppermute | solution.py:34
  85.9 3.4 %collective-permute-start.4 = (bf16[4,256,256]{2,1,0:T(8,128)(2,1)S(1)}, bf16[4,256,256]{2,1,0:T(8,128)(2,1)S(1)}, u32[]{:S(2)}, u32[]{:S(2)}) collective-permute-start(bf16[4,256,256]{2,1,0:T(8,128)(2,1)S(1)} %pad_maximum_fusion.1.refs_0_), channel_id=1, source_target_pairs={{0,8},{8,0},{1,9},{9,1},{2,10},{10,2},{3,11},{11,3},{4,12},{12,4},... | collective-permute-start | bytes 1572872 | tf_op jit(solution)/shard_map/ppermute | solution.py:34
  89.4 3.9 %collective-permute-done.7.refs_4_ = bf16[4,256,256]{2,1,0:T(8,128)(2,1)S(1)} collective-permute-done((bf16[4,256,256]{2,1,0:T(8,128)(2,1)S(1)}, bf16[4,256,256]{2,1,0:T(8,128)(2,1)S(1)}, u32[]{:S(2)}, u32[]{:S(2)}) %collective-permute-start.7) | collective-permute-done | bytes 524320 | tf_op jit(solution)/shard_map/ppermute | solution.py:24
  93.2 1.9 %collective-permute-start.15 = (bf16[4,256,256]{2,1,0:T(8,128)(2,1)S(1)}, bf16[4,256,256]{2,1,0:T(8,128)(2,1)}, u32[]{:S(2)}, u32[]{:S(2)}) collective-permute-start(bf16[4,256,256]{2,1,0:T(8,128)(2,1)S(1)} %collective-permute-done.7.refs_4_), channel_id=1, source_target_pairs={{0,16},{16,32},{32,48},{48,0},{1,17},{17,33},{33,49},{49,1},{2,18}... | collective-permute-start | bytes 1572872 | tf_op jit(solution)/shard_map/ppermute | solution.py:24
  95.2 0.2 select_reduce_fusion
  95.5 2.1 %collective-permute-start.11 = (bf16[4,256,256]{2,1,0:T(8,128)(2,1)S(1)}, bf16[4,256,256]{2,1,0:T(8,128)(2,1)}, u32[]{:S(2)}, u32[]{:S(2)}) collective-permute-start(bf16[4,256,256]{2,1,0:T(8,128)(2,1)S(1)} %collective-permute-done.7.refs_4_), channel_id=1, source_target_pairs={{0,448},{64,128},{128,64},{192,256},{256,192},{320,384},{384,320},... | collective-permute-start | bytes 1572872 | tf_op jit(solution)/shard_map/ppermute | solution.py:29
  97.6 3.5 %collective-permute-start.8 = (bf16[4,256,256]{2,1,0:T(8,128)(2,1)S(1)}, bf16[4,256,256]{2,1,0:T(8,128)(2,1)}, u32[]{:S(2)}, u32[]{:S(2)}) collective-permute-start(bf16[4,256,256]{2,1,0:T(8,128)(2,1)S(1)} %collective-permute-done.7.refs_4_), channel_id=1, source_target_pairs={{0,8},{8,0},{1,9},{9,1},{2,10},{10,2},{3,11},{11,3},{4,12},{12,4},... | collective-permute-start | bytes 1572872 | tf_op jit(solution)/shard_map/ppermute | solution.py:34
  101.2 1.9 %collective-permute-start.10 = (bf16[4,256,256]{2,1,0:T(8,128)(2,1)}, bf16[4,256,256]{2,1,0:T(8,128)(2,1)}, u32[]{:S(2)}, u32[]{:S(2)}) collective-permute-start(bf16[4,256,256]{2,1,0:T(8,128)(2,1)} %collective-permute-done.9.refs_6_), channel_id=1, source_target_pairs={{0,8},{8,0},{1,9},{9,1},{2,10},{10,2},{3,11},{11,3},{4,12},{12,4},... | collective-permute-start | bytes 1572872 | tf_op jit(solution)/shard_map/ppermute | solution.py:34
  103.1 4.6 %collective-permute-start.13 = (bf16[4,256,256]{2,1,0:T(8,128)(2,1)}, bf16[4,256,256]{2,1,0:T(8,128)(2,1)}, u32[]{:S(2)}, u32[]{:S(2)}) collective-permute-start(bf16[4,256,256]{2,1,0:T(8,128)(2,1)} %collective-permute-done.5.refs_2_), channel_id=1, source_target_pairs={{0,48},{16,0},{32,16},{48,32},{1,49},{17,1},{33,17},{49,33},{2,50}... | collective-permute-start | bytes 1572872 | tf_op jit(solution)/shard_map/ppermute | solution.py:24
  107.7 0.8 collective-permute-done.15.refs_12_
  108.6 3.7 %collective-permute-start.17 = (bf16[4,256,256]{2,1,0:T(8,128)(2,1)}, bf16[4,256,256]{2,1,0:T(8,128)(2,1)}, u32[]{:S(2)}, u32[]{:S(2)}) collective-permute-start(bf16[4,256,256]{2,1,0:T(8,128)(2,1)} %collective-permute-done.15.refs_12_), channel_id=1, source_target_pairs={{0,64},{64,0},{128,192},{192,128},{256,320},{320,256},{384,448},{4... | collective-permute-start | bytes 1572872 | tf_op jit(solution)/shard_map/ppermute | solution.py:34
  112.3 0.2 select_reduce_fusion.1
  112.5 0.2 convert_reduce_fusion
  112.7 0.1 compare_select_fusion.10
  112.9 3.0 %collective-permute-start.6 = (bf16[4,256,256]{2,1,0:T(8,128)(2,1)}, bf16[4,256,256]{2,1,0:T(8,128)(2,1)}, u32[]{:S(2)}, u32[]{:S(2)}) collective-permute-start(bf16[4,256,256]{2,1,0:T(8,128)(2,1)} %collective-permute-done.5.refs_2_), channel_id=1, source_target_pairs={{0,8},{8,0},{1,9},{9,1},{2,10},{10,2},{3,11},{11,3},{4,12},{12,4},... | collective-permute-start | bytes 1572872 | tf_op jit(solution)/shard_map/ppermute | solution.py:34
  115.9 1.9 %collective-permute-start.16 = (bf16[4,256,256]{2,1,0:T(8,128)(2,1)}, bf16[4,256,256]{2,1,0:T(8,128)(2,1)}, u32[]{:S(2)}, u32[]{:S(2)}) collective-permute-start(bf16[4,256,256]{2,1,0:T(8,128)(2,1)} %collective-permute-done.15.refs_12_), channel_id=1, source_target_pairs={{0,8},{8,0},{1,9},{9,1},{2,10},{10,2},{3,11},{11,3},{4,12},{12,4},... | collective-permute-start | bytes 1572872 | tf_op jit(solution)/shard_map/ppermute | solution.py:34
  117.9 2.4 %collective-permute-start.12 = (bf16[4,256,256]{2,1,0:T(8,128)(2,1)}, bf16[4,256,256]{2,1,0:T(8,128)(2,1)}, u32[]{:S(2)}, u32[]{:S(2)}) collective-permute-start(bf16[4,256,256]{2,1,0:T(8,128)(2,1)} %collective-permute-done.11.refs_8_), channel_id=1, source_target_pairs={{0,8},{8,0},{1,9},{9,1},{2,10},{10,2},{3,11},{11,3},{4,12},{12,4},... | collective-permute-start | bytes 1572872 | tf_op jit(solution)/shard_map/ppermute | solution.py:34
  120.3 1.9 %collective-permute-start.14 = (bf16[4,256,256]{2,1,0:T(8,128)(2,1)}, bf16[4,256,256]{2,1,0:T(8,128)(2,1)}, u32[]{:S(2)}, u32[]{:S(2)}) collective-permute-start(bf16[4,256,256]{2,1,0:T(8,128)(2,1)} %collective-permute-done.13.refs_10_), channel_id=1, source_target_pairs={{0,8},{8,0},{1,9},{9,1},{2,10},{10,2},{3,11},{11,3},{4,12},{12,4},... | collective-permute-start | bytes 1572872 | tf_op jit(solution)/shard_map/ppermute | solution.py:34
  122.2 0.9 collective-permute-done.17.refs_14_
  123.1 4.3 %collective-permute-start.18 = (bf16[4,256,256]{2,1,0:T(8,128)(2,1)}, bf16[4,256,256]{2,1,0:T(8,128)(2,1)}, u32[]{:S(2)}, u32[]{:S(2)}) collective-permute-start(bf16[4,256,256]{2,1,0:T(8,128)(2,1)} %collective-permute-done.17.refs_14_), channel_id=1, source_target_pairs={{0,8},{8,0},{1,9},{9,1},{2,10},{10,2},{3,11},{11,3},{4,12},{12,4},... | collective-permute-start | bytes 1572872 | tf_op jit(solution)/shard_map/ppermute | solution.py:34
  127.6 1.6 collective-permute-done.18.refs_15_
  129.2 0.1 broadcast_in_dim.113.refs_16_
  129.4 6.7 %score.1 = f32[64,2,128]{2,1,0:T(2,128)S(1)} custom-call(s32[33]{0:T(128)S(1)} %pad_add_fusion.where_ref, bf16[8,496,256]{2,1,0:T(8,128)(2,1)S(1)} %all-to-all-done.acts_ref, bf16[4,256,256]{2,1,0:T(8,128)(2,1)} %copy-done, bf16[4,256,256]{2,1,0:T(8,128)(2,1)} %copy-done.4, bf16[4,256,256]{2,1,0:T(8,128)(2,1)} %collective-permute-done.5.refs_2_, ...), custom_call_target="tpu_custom_call" | custom-call | tf_op jit(solution)/shard_map/score/pallas_call | solution.py:131
  136.1 18.1 %all_to_all.15 = f32[64,2,128]{2,1,0:T(2,128)S(1)} all-to-all(f32[64,2,128]{2,1,0:T(2,128)S(1)} %score.1), channel_id=1, replica_groups=mesh['y'=8,'x'=4,'core'=2,'mp'=8] {'y','x','core'}, dimensions={0} | all-to-all | bytes 131072 | tf_op jit(solution)/shard_map/all_to_all | solution.py:19
  154.3 0.1 copy.32
  154.4 0.1 copy.33
  154.5 0.2 reshape.143
  154.7 0.6 fusion
  155.3 0.2 fusion.5
  155.6 11.7 %all_to_all.16 = f32[8,34,128]{2,1,0:T(8,128)S(1)} all-to-all(f32[8,34,128]{2,1,0:T(8,128)S(1)} %broadcast_in_dim.115), channel_id=1, replica_groups=mesh['y'=8,'x'=4,'core'=2,'mp'=8] {'mp'}, dimensions={0} | all-to-all | bytes 278528 | tf_op jit(solution)/shard_map/all_to_all | solution.py:19
  167.3 0.1 reshape.145
  167.5 0.8 reshape.146
  168.3 0.9 finish.1
  (68 shorter events, 1.1 us)
Async XLA Ops:
  0.6 1.5 copy-start.2
  0.6 1.6 copy-start.6
  0.7 1.6 copy-start.9
  3.7 11.0 %copy-start.1 = (bf16[2048,256]{1,0:T(8,128)(2,1)S(1)}, bf16[2048,256]{1,0:T(8,128)(2,1)}, u32[]{:S(2)}) copy-start(bf16[2048,256]{1,0:T(8,128)(2,1)} %param.10) | copy-start | bytes 3145732
  3.7 125.5 %all-to-all-start = ((bf16[8,496,256]{2,1,0:T(8,128)(2,1)}), bf16[8,496,256]{2,1,0:T(8,128)(2,1)S(1)}, u32[]{:S(2)}, u32[]{:S(2)}) async-start(bf16[8,496,256]{2,1,0:T(8,128)(2,1)} %pad_maximum_fusion), calls=%async_computation | async-start | bytes 4063232 | tf_op jit(solution)/shard_map/all_to_all | solution.py:19
  14.7 64.5 %copy-start.5 = (s32[384]{0:T(512)S(1)}, s32[384]{0:T(512)}, u32[]{:S(2)}) copy-start(s32[384]{0:T(512)} %param.15) | copy-start | bytes 4612
  14.7 64.6 %copy-start.8 = (s32[960]{0:T(1024)S(1)}, s32[960]{0:T(1024)}, u32[]{:S(2)}) copy-start(s32[960]{0:T(1024)} %param.13) | copy-start | bytes 11524
  14.7 80.5 %copy-start.7 = (s32[960]{0:T(1024)S(1)}, s32[960]{0:T(1024)}, u32[]{:S(2)}) copy-start(s32[960]{0:T(1024)} %param.14) | copy-start | bytes 11524
  14.8 48.7 %collective-permute-start.2 = (bf16[256,256]{1,0:T(8,128)(2,1)S(1)}, bf16[256,256]{1,0:T(8,128)(2,1)S(1)}, u32[]{:S(2)}, u32[]{:S(2)}) collective-permute-start(bf16[256,256]{1,0:T(8,128)(2,1)S(1)} %dynamic-slice_bitcast_fusion.1), channel_id=1, source_target_pairs={{7,0},{0,1},{1,2},{2,3},{3,4},{4,5},{5,6},{6,7},{15,8},{8,9},{9,10... | collective-permute-start | bytes 393224 | tf_op jit(solution)/shard_map/ppermute | solution.py:51
  18.2 51.3 %collective-permute-start.3 = (bf16[256,256]{1,0:T(8,128)(2,1)S(1)}, bf16[256,256]{1,0:T(8,128)(2,1)S(1)}, u32[]{:S(2)}, u32[]{:S(2)}) collective-permute-start(bf16[256,256]{1,0:T(8,128)(2,1)S(1)} %dynamic-slice_bitcast_fusion), channel_id=1, source_target_pairs={{6,0},{7,1},{0,2},{1,3},{2,4},{3,5},{4,6},{5,7},{14,8},{15,9},{8,1... | collective-permute-start | bytes 393224 | tf_op jit(solution)/shard_map/ppermute | solution.py:51
  22.2 47.3 %collective-permute-start.1 = (bf16[256,256]{1,0:T(8,128)(2,1)S(1)}, bf16[256,256]{1,0:T(8,128)(2,1)S(1)}, u32[]{:S(2)}, u32[]{:S(2)}) collective-permute-start(bf16[256,256]{1,0:T(8,128)(2,1)S(1)} %dynamic-slice_bitcast_fusion.2), channel_id=1, source_target_pairs={{1,0},{2,1},{3,2},{4,3},{5,4},{6,5},{7,6},{0,7},{9,8},{10,9},{11,1... | collective-permute-start | bytes 393224 | tf_op jit(solution)/shard_map/ppermute | solution.py:51
  25.7 51.4 %collective-permute-start = (bf16[256,256]{1,0:T(8,128)(2,1)S(1)}, bf16[256,256]{1,0:T(8,128)(2,1)S(1)}, u32[]{:S(2)}, u32[]{:S(2)}) collective-permute-start(bf16[256,256]{1,0:T(8,128)(2,1)S(1)} %dynamic-slice_bitcast_fusion.3), channel_id=1, source_target_pairs={{4,0},{5,1},{6,2},{7,3},{0,4},{1,5},{2,6},{3,7},{12,8},{13,9},{14,... | collective-permute-start | bytes 393224 | tf_op jit(solution)/shard_map/ppermute | solution.py:51
  77.1 52.2 %copy-start = (bf16[4,256,256]{2,1,0:T(8,128)(2,1)}, bf16[4,256,256]{2,1,0:T(8,128)(2,1)S(1)}, u32[]{:S(2)}) copy-start(bf16[4,256,256]{2,1,0:T(8,128)(2,1)S(1)} %pad_maximum_fusion.1.refs_0_) | copy-start | bytes 1572868
  77.2 16.1 %collective-permute-start.7 = (bf16[4,256,256]{2,1,0:T(8,128)(2,1)S(1)}, bf16[4,256,256]{2,1,0:T(8,128)(2,1)S(1)}, u32[]{:S(2)}, u32[]{:S(2)}) collective-permute-start(bf16[4,256,256]{2,1,0:T(8,128)(2,1)S(1)} %pad_maximum_fusion.1.refs_0_), channel_id=1, source_target_pairs={{0,16},{16,32},{32,48},{48,0},{1,17},{17,33},{33,49},{49,1},{2,18}... | collective-permute-start | bytes 1572872 | tf_op jit(solution)/shard_map/ppermute | solution.py:24
  79.4 18.2 %collective-permute-start.9 = (bf16[4,256,256]{2,1,0:T(8,128)(2,1)S(1)}, bf16[4,256,256]{2,1,0:T(8,128)(2,1)}, u32[]{:S(2)}, u32[]{:S(2)}) collective-permute-start(bf16[4,256,256]{2,1,0:T(8,128)(2,1)S(1)} %pad_maximum_fusion.1.refs_0_), channel_id=1, source_target_pairs={{0,48},{16,0},{32,16},{48,32},{1,49},{17,1},{33,17},{49,33},{2,50}... | collective-permute-start | bytes 1572872 | tf_op jit(solution)/shard_map/ppermute | solution.py:24
  84.0 17.2 %collective-permute-start.5 = (bf16[4,256,256]{2,1,0:T(8,128)(2,1)S(1)}, bf16[4,256,256]{2,1,0:T(8,128)(2,1)}, u32[]{:S(2)}, u32[]{:S(2)}) collective-permute-start(bf16[4,256,256]{2,1,0:T(8,128)(2,1)S(1)} %pad_maximum_fusion.1.refs_0_), channel_id=1, source_target_pairs={{0,64},{64,0},{128,192},{192,128},{256,320},{320,256},{384,448},{4... | collective-permute-start | bytes 1572872 | tf_op jit(solution)/shard_map/ppermute | solution.py:34
  85.9 17.2 %collective-permute-start.4 = (bf16[4,256,256]{2,1,0:T(8,128)(2,1)S(1)}, bf16[4,256,256]{2,1,0:T(8,128)(2,1)S(1)}, u32[]{:S(2)}, u32[]{:S(2)}) collective-permute-start(bf16[4,256,256]{2,1,0:T(8,128)(2,1)S(1)} %pad_maximum_fusion.1.refs_0_), channel_id=1, source_target_pairs={{0,8},{8,0},{1,9},{9,1},{2,10},{10,2},{3,11},{11,3},{4,12},{12,4},... | collective-permute-start | bytes 1572872 | tf_op jit(solution)/shard_map/ppermute | solution.py:34
  93.2 36.1 %copy-start.3 = (bf16[4,256,256]{2,1,0:T(8,128)(2,1)}, bf16[4,256,256]{2,1,0:T(8,128)(2,1)S(1)}, u32[]{:S(2)}) copy-start(bf16[4,256,256]{2,1,0:T(8,128)(2,1)S(1)} %collective-permute-done.7.refs_4_) | copy-start | bytes 1572868
  93.2 15.3 %collective-permute-start.15 = (bf16[4,256,256]{2,1,0:T(8,128)(2,1)S(1)}, bf16[4,256,256]{2,1,0:T(8,128)(2,1)}, u32[]{:S(2)}, u32[]{:S(2)}) collective-permute-start(bf16[4,256,256]{2,1,0:T(8,128)(2,1)S(1)} %collective-permute-done.7.refs_4_), channel_id=1, source_target_pairs={{0,16},{16,32},{32,48},{48,0},{1,17},{17,33},{33,49},{49,1},{2,18}... | collective-permute-start | bytes 1572872 | tf_op jit(solution)/shard_map/ppermute | solution.py:24
  95.5 20.5 %collective-permute-start.11 = (bf16[4,256,256]{2,1,0:T(8,128)(2,1)S(1)}, bf16[4,256,256]{2,1,0:T(8,128)(2,1)}, u32[]{:S(2)}, u32[]{:S(2)}) collective-permute-start(bf16[4,256,256]{2,1,0:T(8,128)(2,1)S(1)} %collective-permute-done.7.refs_4_), channel_id=1, source_target_pairs={{0,448},{64,128},{128,64},{192,256},{256,192},{320,384},{384,320},... | collective-permute-start | bytes 1572872 | tf_op jit(solution)/shard_map/ppermute | solution.py:29
  97.6 20.3 %collective-permute-start.8 = (bf16[4,256,256]{2,1,0:T(8,128)(2,1)S(1)}, bf16[4,256,256]{2,1,0:T(8,128)(2,1)}, u32[]{:S(2)}, u32[]{:S(2)}) collective-permute-start(bf16[4,256,256]{2,1,0:T(8,128)(2,1)S(1)} %collective-permute-done.7.refs_4_), channel_id=1, source_target_pairs={{0,8},{8,0},{1,9},{9,1},{2,10},{10,2},{3,11},{11,3},{4,12},{12,4},... | collective-permute-start | bytes 1572872 | tf_op jit(solution)/shard_map/ppermute | solution.py:34
  101.2 11.8 %collective-permute-start.10 = (bf16[4,256,256]{2,1,0:T(8,128)(2,1)}, bf16[4,256,256]{2,1,0:T(8,128)(2,1)}, u32[]{:S(2)}, u32[]{:S(2)}) collective-permute-start(bf16[4,256,256]{2,1,0:T(8,128)(2,1)} %collective-permute-done.9.refs_6_), channel_id=1, source_target_pairs={{0,8},{8,0},{1,9},{9,1},{2,10},{10,2},{3,11},{11,3},{4,12},{12,4},... | collective-permute-start | bytes 1572872 | tf_op jit(solution)/shard_map/ppermute | solution.py:34
  103.1 5.5 %copy-start.4 = (bf16[4,256,256]{2,1,0:T(8,128)(2,1)}, bf16[4,256,256]{2,1,0:T(8,128)(2,1)S(1)}, u32[]{:S(2)}) copy-start(bf16[4,256,256]{2,1,0:T(8,128)(2,1)S(1)} %collective-permute-done.4.refs_1_) | copy-start | bytes 1572868
  103.1 17.2 %collective-permute-start.13 = (bf16[4,256,256]{2,1,0:T(8,128)(2,1)}, bf16[4,256,256]{2,1,0:T(8,128)(2,1)}, u32[]{:S(2)}, u32[]{:S(2)}) collective-permute-start(bf16[4,256,256]{2,1,0:T(8,128)(2,1)} %collective-permute-done.5.refs_2_), channel_id=1, source_target_pairs={{0,48},{16,0},{32,16},{48,32},{1,49},{17,1},{33,17},{49,33},{2,50}... | collective-permute-start | bytes 1572872 | tf_op jit(solution)/shard_map/ppermute | solution.py:24
  108.6 14.5 %collective-permute-start.17 = (bf16[4,256,256]{2,1,0:T(8,128)(2,1)}, bf16[4,256,256]{2,1,0:T(8,128)(2,1)}, u32[]{:S(2)}, u32[]{:S(2)}) collective-permute-start(bf16[4,256,256]{2,1,0:T(8,128)(2,1)} %collective-permute-done.15.refs_12_), channel_id=1, source_target_pairs={{0,64},{64,0},{128,192},{192,128},{256,320},{320,256},{384,448},{4... | collective-permute-start | bytes 1572872 | tf_op jit(solution)/shard_map/ppermute | solution.py:34
  112.9 14.6 %collective-permute-start.6 = (bf16[4,256,256]{2,1,0:T(8,128)(2,1)}, bf16[4,256,256]{2,1,0:T(8,128)(2,1)}, u32[]{:S(2)}, u32[]{:S(2)}) collective-permute-start(bf16[4,256,256]{2,1,0:T(8,128)(2,1)} %collective-permute-done.5.refs_2_), channel_id=1, source_target_pairs={{0,8},{8,0},{1,9},{9,1},{2,10},{10,2},{3,11},{11,3},{4,12},{12,4},... | collective-permute-start | bytes 1572872 | tf_op jit(solution)/shard_map/ppermute | solution.py:34
  115.9 11.7 %collective-permute-start.16 = (bf16[4,256,256]{2,1,0:T(8,128)(2,1)}, bf16[4,256,256]{2,1,0:T(8,128)(2,1)}, u32[]{:S(2)}, u32[]{:S(2)}) collective-permute-start(bf16[4,256,256]{2,1,0:T(8,128)(2,1)} %collective-permute-done.15.refs_12_), channel_id=1, source_target_pairs={{0,8},{8,0},{1,9},{9,1},{2,10},{10,2},{3,11},{11,3},{4,12},{12,4},... | collective-permute-start | bytes 1572872 | tf_op jit(solution)/shard_map/ppermute | solution.py:34
  117.9 9.7 %collective-permute-start.12 = (bf16[4,256,256]{2,1,0:T(8,128)(2,1)}, bf16[4,256,256]{2,1,0:T(8,128)(2,1)}, u32[]{:S(2)}, u32[]{:S(2)}) collective-permute-start(bf16[4,256,256]{2,1,0:T(8,128)(2,1)} %collective-permute-done.11.refs_8_), channel_id=1, source_target_pairs={{0,8},{8,0},{1,9},{9,1},{2,10},{10,2},{3,11},{11,3},{4,12},{12,4},... | collective-permute-start | bytes 1572872 | tf_op jit(solution)/shard_map/ppermute | solution.py:34
  120.3 7.3 %collective-permute-start.14 = (bf16[4,256,256]{2,1,0:T(8,128)(2,1)}, bf16[4,256,256]{2,1,0:T(8,128)(2,1)}, u32[]{:S(2)}, u32[]{:S(2)}) collective-permute-start(bf16[4,256,256]{2,1,0:T(8,128)(2,1)} %collective-permute-done.13.refs_10_), channel_id=1, source_target_pairs={{0,8},{8,0},{1,9},{9,1},{2,10},{10,2},{3,11},{11,3},{4,12},{12,4},... | collective-permute-start | bytes 1572872 | tf_op jit(solution)/shard_map/ppermute | solution.py:34
  123.1 6.1 %collective-permute-start.18 = (bf16[4,256,256]{2,1,0:T(8,128)(2,1)}, bf16[4,256,256]{2,1,0:T(8,128)(2,1)}, u32[]{:S(2)}, u32[]{:S(2)}) collective-permute-start(bf16[4,256,256]{2,1,0:T(8,128)(2,1)} %collective-permute-done.17.refs_14_), channel_id=1, source_target_pairs={{0,8},{8,0},{1,9},{9,1},{2,10},{10,2},{3,11},{11,3},{4,12},{12,4},... | collective-permute-start | bytes 1572872 | tf_op jit(solution)/shard_map/ppermute | solution.py:34

commit v3 on v2

--- a/solution.py
+++ b/solution.py
@@ -13,6 +13,8 @@
 BF16 = jnp.bfloat16
 PLANES = 8
 TOK = 16
+
+CHUNKS = ((0, 0, 2), (0, 2, 2), (1, 0, 2), (1, 2, 1), (1, 3, 1))
 
 
 def exchange(value, axis):
@@ -71,20 +73,21 @@
         return pltpu.make_async_copy(pieces[2 * s + side].at[p], target, sem.at[side, s, p])
 
     for side in range(2):
-        for s in range(8):
-            for p in range(4):
+        for p in range(4):
+            for s in range(8):
                 fetch(side, s, p).start()
     for p in range(4):
         a_ref[0, :, p * shard : (p + 1) * shard] = acts_ref[2 * p + core, 0:tokens, :]
         a_ref[1, :, p * shard : (p + 1) * shard] = acts_ref[2 * p + 1 - core, 0:tokens, :]
     head_rows = jnp.concatenate([acts_ref[j, 2 * tokens :, :] for j in range(PLANES)], axis=1)
-    for side in range(2):
-        for s in range(8):
-            for p in range(4):
-                fetch(side, s, p).wait()
+    for side, p, parts in CHUNKS:
+        for q in range(p, p + parts):
+            for s in range(8):
+                fetch(side, s, q).wait()
+        at = slice(p * shard, (p + parts) * shard)
         for j in range(PLANES):
-            part = jnp.dot(a_ref[side], w_ref[side, j], preferred_element_type=F32)
-            if side == 0:
+            part = jnp.dot(a_ref[side, :, at], w_ref[side, j, at], preferred_element_type=F32)
+            if side == 0 and p == 0:
                 proj_ref[j] = part
             else:
                 proj_ref[j] += part
@@ -152,10 +155,34 @@
     )(where, in_vmem(acts), *[pltpu.with_memory_space_constraint(v, pltpu.HBM) for v in pieces], live, route)
 
 
-def finish_kernel(totals_ref, lengths_ref, rank_ref, out_ref):
-    totals = totals_ref[0]
+def gather_kernel(source_ref, got_ref, totals_ref, out_ref):
+    owned = jnp.concatenate([got_ref[source_ref[q], 0:1, :] for q in range(OWN_CAP)], axis=0)
+    groups = totals_ref.shape[1] // 128
+    for p in range(PLANES):
+        for g in range(groups):
+            out_ref[p, 8 * g : 8 * g + 8, :] = totals_ref[:, 128 * g : 128 * g + 128]
+        out_ref[p, 8 * groups : 8 * groups + OWN_CAP, :] = owned
+
+
+def gather(source, got, totals):
+    vmem = pl.BlockSpec(memory_space=pltpu.VMEM)
+    rows = totals.shape[1] // 128 * 8 + OWN_CAP
+    return pl.pallas_call(
+        gather_kernel,
+        out_shape=jax.ShapeDtypeStruct((PLANES, rows, 128), F32),
+        in_specs=[pl.BlockSpec(memory_space=pltpu.SMEM), vmem, vmem],
+        out_specs=vmem,
+        compiler_params=pltpu.CompilerParams(vmem_limit_bytes=8 * 2**20),
+        name="gather",
+    )(source, in_vmem(got), in_vmem(totals))
+
+
+def finish_kernel(final_ref, lengths_ref, rank_ref, out_ref):
+    groups = lengths_ref.shape[1] // 128
+    totals = final_ref[0, 0 : 8 * groups, :]
     for p in range(1, PLANES):
-        totals = totals + totals_ref[p]
+        totals = totals + final_ref[p, 0 : 8 * groups, :]
+    totals = jnp.concatenate([totals[8 * g : 8 * g + 8, :] for g in range(groups)], axis=1)
     scores = totals / lengths_ref[...].astype(F32)
     count = float(scores.shape[1])
     worst = jnp.min(scores, axis=0, keepdims=True)
@@ -173,7 +200,7 @@
     out_ref[...] = turned[:, 0:size]
 
 
-def finish(totals, lengths, rank, size):
+def finish(final, lengths, rank, size):
     vmem = pl.BlockSpec(memory_space=pltpu.VMEM)
     return pl.pallas_call(
         finish_kernel,
@@ -182,7 +209,7 @@
         out_specs=vmem,
         compiler_params=pltpu.CompilerParams(vmem_limit_bytes=8 * 2**20),
         name="finish",
-    )(in_vmem(totals), lengths, rank[None])
+    )(in_vmem(final), lengths, rank[None])
 
 
 def local(hidden, attn_out, out_proj, norm_gain, reward_proj, block_seq, block_dest, lengths):
@@ -256,24 +283,19 @@
     targets = rank * OWN_CAP + jnp.arange(OWN_CAP, dtype=jnp.int32)
     source = jnp.sum(jnp.where(block_dest[None, :] == targets[:, None], all_slots[None, :], 0), axis=1)
     source, tall, wide, where = lax.optimization_barrier(
-        (source // slots_in, block_seq, lengths[None, :], where)
+        (jnp.minimum(source // slots_in, owners - 1), block_seq, lengths[None, :], where)
     )
     sent = score(where, acts, pieces, live, route)
     got = exchange(sent, ("y", "x", "core"))
 
-    pick = (source[:, None] == jnp.arange(owners, dtype=jnp.int32)[None, :]).astype(F32)
     member = (tall[:, None] == seq_ids[None, :]).astype(F32)
-
-    owned = jnp.dot(pick, got[:, 0, :], precision=lax.Precision.HIGHEST)
     sums = got[:, 1, :].reshape(owners, 8, TOK)[:, :, :slots_in].swapaxes(0, 1).reshape(8, owners * slots_in)
     totals = jnp.dot(sums, member, precision=lax.Precision.HIGHEST)
-    final = jnp.concatenate([owned, totals.reshape(-1, 128)], axis=0)
-    final = exchange(jnp.broadcast_to(final[None], (PLANES, *final.shape)), "mp")
+    final = exchange(gather(source, got, totals), "mp")
     token_rewards = (
-        final[:, :OWN_CAP].reshape(PLANES, OWN_CAP, 8, TOK).transpose(1, 2, 0, 3).reshape(OWN_CAP, 8, block_len)
-    )
-    totals = final[:, OWN_CAP:].reshape(PLANES, 8, seq_count)
-    return token_rewards, finish(totals, wide, rank, seq_local).reshape(seq_local)
+        final[:, -OWN_CAP:].reshape(PLANES, OWN_CAP, 8, TOK).transpose(1, 2, 0, 3).reshape(OWN_CAP, 8, block_len)
+    )
+    return token_rewards, finish(final, wide, rank, seq_local).reshape(seq_local)
 
 
 def solution(mesh):

time: 170 us -> 170 us (level)
  no operation moved by 1% of the time
where the time goes in v3:
time: 170 us; the launch traced here: 169 us
  starting transfers between devices  70.1 us (41%)
  waiting for transfers between devices  53.4 us (31%)
  blocking collectives  29.8 us (18%)
  Pallas kernels  7.75 us (5%)
  local copies, waits for them, and re-layouts  3.72 us (2%)
  other arithmetic  2.41 us (1%)
    ppermute x4, waiting for transfers between devices, from_plane(): return lax.ppermute(value, ('y', 'x', 'core', 'mp'), pairs)  46.2 us
    all_to_all x2, blocking collectives, exchange(): return lax.all_to_all(value, axis, split_axis=0, concat_axis=0, tiled=True)  29.8 us
    ppermute x10, starting transfers between devices, swap(): return lax.ppermute(value, axis, [(s, s ^ 1) for s in range(size)])  28.1 us
    ppermute x4, starting transfers between devices, from_plane(): return lax.ppermute(value, ('y', 'x', 'core', 'mp'), pairs)  15.9 us
    ppermute x4, starting transfers between devices, shift(): lax.ppermute(value, axis, [(s, (s + step) % size) for s in range(size)])  13 us
    all_to_all x1, starting transfers between devices, exchange(): return lax.all_to_all(value, axis, split_axis=0, concat_axis=0, tiled=True)  11 us
    pallas_call x1, Pallas kernels, score(): pl.pallas_call(score_kernel, out_shape=jax.ShapeDtypeStruct((owners, 2, 1...  6.29 us
    ppermute x4, waiting for transfers between devices, shift(): lax.ppermute(value, axis, [(s, (s + step) % size) for s in range(size)])  4.72 us
  transfers between devices with their start and end apart: 20, of which 7 were waited for; matrix products, arithmetic and copies ran while one was open for 1% of the time, Pallas kernels for 0%

profile of v3, /device:TPU:1, one launch (start us, length us, event | category | flops | bytes accessed | tf_op | source)
XLA Modules:
  0.0 169.0 jit_solution(11735910825564071111)
XLA Ops:
  0.7 1.3 copy.25
  2.0 0.1 copy-done.2
  2.3 1.4 pad_maximum_fusion
  3.7 11.0 %all-to-all-start = ((bf16[8,496,256]{2,1,0:T(8,128)(2,1)}), bf16[8,496,256]{2,1,0:T(8,128)(2,1)S(1)}, u32[]{:S(2)}, u32[]{:S(2)}) async-start(bf16[8,496,256]{2,1,0:T(8,128)(2,1)} %pad_maximum_fusion), calls=%async_computation | async-start | bytes 4063232 | tf_op jit(solution)/shard_map/all_to_all | solution.py:21
  14.8 3.4 %collective-permute-start.2 = (bf16[256,256]{1,0:T(8,128)(2,1)S(1)}, bf16[256,256]{1,0:T(8,128)(2,1)S(1)}, u32[]{:S(2)}, u32[]{:S(2)}) collective-permute-start(bf16[256,256]{1,0:T(8,128)(2,1)S(1)} %dynamic-slice_bitcast_fusion.1), channel_id=1, source_target_pairs={{7,0},{0,1},{1,2},{2,3},{3,4},{4,5},{5,6},{6,7},{15,8},{8,9},{9,10... | collective-permute-start | bytes 393224 | tf_op jit(solution)/shard_map/ppermute | solution.py:53
  18.2 4.0 %collective-permute-start.3 = (bf16[256,256]{1,0:T(8,128)(2,1)S(1)}, bf16[256,256]{1,0:T(8,128)(2,1)S(1)}, u32[]{:S(2)}, u32[]{:S(2)}) collective-permute-start(bf16[256,256]{1,0:T(8,128)(2,1)S(1)} %dynamic-slice_bitcast_fusion), channel_id=1, source_target_pairs={{6,0},{7,1},{0,2},{1,3},{2,4},{3,5},{4,6},{5,7},{14,8},{15,9},{8,1... | collective-permute-start | bytes 393224 | tf_op jit(solution)/shard_map/ppermute | solution.py:53
  22.2 3.4 %collective-permute-start.1 = (bf16[256,256]{1,0:T(8,128)(2,1)S(1)}, bf16[256,256]{1,0:T(8,128)(2,1)S(1)}, u32[]{:S(2)}, u32[]{:S(2)}) collective-permute-start(bf16[256,256]{1,0:T(8,128)(2,1)S(1)} %dynamic-slice_bitcast_fusion.2), channel_id=1, source_target_pairs={{1,0},{2,1},{3,2},{4,3},{5,4},{6,5},{7,6},{0,7},{9,8},{10,9},{11,1... | collective-permute-start | bytes 393224 | tf_op jit(solution)/shard_map/ppermute | solution.py:53
  25.7 5.2 %collective-permute-start = (bf16[256,256]{1,0:T(8,128)(2,1)S(1)}, bf16[256,256]{1,0:T(8,128)(2,1)S(1)}, u32[]{:S(2)}, u32[]{:S(2)}) collective-permute-start(bf16[256,256]{1,0:T(8,128)(2,1)S(1)} %dynamic-slice_bitcast_fusion.3), channel_id=1, source_target_pairs={{4,0},{5,1},{6,2},{7,3},{0,4},{1,5},{2,6},{3,7},{12,8},{13,9},{14,... | collective-permute-start | bytes 393224 | tf_op jit(solution)/shard_map/ppermute | solution.py:53
  30.9 32.7 %collective-permute-done.2 = bf16[256,256]{1,0:T(8,128)(2,1)S(1)} collective-permute-done((bf16[256,256]{1,0:T(8,128)(2,1)S(1)}, bf16[256,256]{1,0:T(8,128)(2,1)S(1)}, u32[]{:S(2)}, u32[]{:S(2)}) %collective-permute-start.2) | collective-permute-done | bytes 131104 | tf_op jit(solution)/shard_map/ppermute | solution.py:53
  63.6 5.9 %collective-permute-done.3 = bf16[256,256]{1,0:T(8,128)(2,1)S(1)} collective-permute-done((bf16[256,256]{1,0:T(8,128)(2,1)S(1)}, bf16[256,256]{1,0:T(8,128)(2,1)S(1)}, u32[]{:S(2)}, u32[]{:S(2)}) %collective-permute-start.3) | collective-permute-done | bytes 131104 | tf_op jit(solution)/shard_map/ppermute | solution.py:53
  69.5 7.6 %collective-permute-done = bf16[256,256]{1,0:T(8,128)(2,1)S(1)} collective-permute-done((bf16[256,256]{1,0:T(8,128)(2,1)S(1)}, bf16[256,256]{1,0:T(8,128)(2,1)S(1)}, u32[]{:S(2)}, u32[]{:S(2)}) %collective-permute-start) | collective-permute-done | bytes 131104 | tf_op jit(solution)/shard_map/ppermute | solution.py:53
  77.2 1.9 %collective-permute-start.7 = (bf16[4,256,256]{2,1,0:T(8,128)(2,1)S(1)}, bf16[4,256,256]{2,1,0:T(8,128)(2,1)S(1)}, u32[]{:S(2)}, u32[]{:S(2)}) collective-permute-start(bf16[4,256,256]{2,1,0:T(8,128)(2,1)S(1)} %pad_maximum_fusion.1.refs_0_), channel_id=1, source_target_pairs={{0,16},{16,32},{32,48},{48,0},{1,17},{17,33},{33,49},{49,1},{2,18}... | collective-permute-start | bytes 1572872 | tf_op jit(solution)/shard_map/ppermute | solution.py:26
  79.1 0.1 broadcast_in_dim.99
  79.2 0.1 add.154
  79.4 4.6 %collective-permute-start.9 = (bf16[4,256,256]{2,1,0:T(8,128)(2,1)S(1)}, bf16[4,256,256]{2,1,0:T(8,128)(2,1)}, u32[]{:S(2)}, u32[]{:S(2)}) collective-permute-start(bf16[4,256,256]{2,1,0:T(8,128)(2,1)S(1)} %pad_maximum_fusion.1.refs_0_), channel_id=1, source_target_pairs={{0,48},{16,0},{32,16},{48,32},{1,49},{17,1},{33,17},{49,33},{2,50}... | collective-permute-start | bytes 1572872 | tf_op jit(solution)/shard_map/ppermute | solution.py:26
  84.0 1.9 %collective-permute-start.5 = (bf16[4,256,256]{2,1,0:T(8,128)(2,1)S(1)}, bf16[4,256,256]{2,1,0:T(8,128)(2,1)}, u32[]{:S(2)}, u32[]{:S(2)}) collective-permute-start(bf16[4,256,256]{2,1,0:T(8,128)(2,1)S(1)} %pad_maximum_fusion.1.refs_0_), channel_id=1, source_target_pairs={{0,64},{64,0},{128,192},{192,128},{256,320},{320,256},{384,448},{4... | collective-permute-start | bytes 1572872 | tf_op jit(solution)/shard_map/ppermute | solution.py:36
  85.9 3.4 %collective-permute-start.4 = (bf16[4,256,256]{2,1,0:T(8,128)(2,1)S(1)}, bf16[4,256,256]{2,1,0:T(8,128)(2,1)S(1)}, u32[]{:S(2)}, u32[]{:S(2)}) collective-permute-start(bf16[4,256,256]{2,1,0:T(8,128)(2,1)S(1)} %pad_maximum_fusion.1.refs_0_), channel_id=1, source_target_pairs={{0,8},{8,0},{1,9},{9,1},{2,10},{10,2},{3,11},{11,3},{4,12},{12,4},... | collective-permute-start | bytes 1572872 | tf_op jit(solution)/shard_map/ppermute | solution.py:36
  89.4 3.9 %collective-permute-done.7.refs_4_ = bf16[4,256,256]{2,1,0:T(8,128)(2,1)S(1)} collective-permute-done((bf16[4,256,256]{2,1,0:T(8,128)(2,1)S(1)}, bf16[4,256,256]{2,1,0:T(8,128)(2,1)S(1)}, u32[]{:S(2)}, u32[]{:S(2)}) %collective-permute-start.7) | collective-permute-done | bytes 524320 | tf_op jit(solution)/shard_map/ppermute | solution.py:26
  93.2 1.9 %collective-permute-start.15 = (bf16[4,256,256]{2,1,0:T(8,128)(2,1)S(1)}, bf16[4,256,256]{2,1,0:T(8,128)(2,1)}, u32[]{:S(2)}, u32[]{:S(2)}) collective-permute-start(bf16[4,256,256]{2,1,0:T(8,128)(2,1)S(1)} %collective-permute-done.7.refs_4_), channel_id=1, source_target_pairs={{0,16},{16,32},{32,48},{48,0},{1,17},{17,33},{33,49},{49,1},{2,18}... | collective-permute-start | bytes 1572872 | tf_op jit(solution)/shard_map/ppermute | solution.py:26
  95.2 0.2 select_reduce_fusion
  95.5 2.1 %collective-permute-start.11 = (bf16[4,256,256]{2,1,0:T(8,128)(2,1)S(1)}, bf16[4,256,256]{2,1,0:T(8,128)(2,1)}, u32[]{:S(2)}, u32[]{:S(2)}) collective-permute-start(bf16[4,256,256]{2,1,0:T(8,128)(2,1)S(1)} %collective-permute-done.7.refs_4_), channel_id=1, source_target_pairs={{0,448},{64,128},{128,64},{192,256},{256,192},{320,384},{384,320},... | collective-permute-start | bytes 1572872 | tf_op jit(solution)/shard_map/ppermute | solution.py:31
  97.6 3.5 %collective-permute-start.8 = (bf16[4,256,256]{2,1,0:T(8,128)(2,1)S(1)}, bf16[4,256,256]{2,1,0:T(8,128)(2,1)}, u32[]{:S(2)}, u32[]{:S(2)}) collective-permute-start(bf16[4,256,256]{2,1,0:T(8,128)(2,1)S(1)} %collective-permute-done.7.refs_4_), channel_id=1, source_target_pairs={{0,8},{8,0},{1,9},{9,1},{2,10},{10,2},{3,11},{11,3},{4,12},{12,4},... | collective-permute-start | bytes 1572872 | tf_op jit(solution)/shard_map/ppermute | solution.py:36
  101.2 1.9 %collective-permute-start.10 = (bf16[4,256,256]{2,1,0:T(8,128)(2,1)}, bf16[4,256,256]{2,1,0:T(8,128)(2,1)}, u32[]{:S(2)}, u32[]{:S(2)}) collective-permute-start(bf16[4,256,256]{2,1,0:T(8,128)(2,1)} %collective-permute-done.9.refs_6_), channel_id=1, source_target_pairs={{0,8},{8,0},{1,9},{9,1},{2,10},{10,2},{3,11},{11,3},{4,12},{12,4},... | collective-permute-start | bytes 1572872 | tf_op jit(solution)/shard_map/ppermute | solution.py:36
  103.1 4.6 %collective-permute-start.13 = (bf16[4,256,256]{2,1,0:T(8,128)(2,1)}, bf16[4,256,256]{2,1,0:T(8,128)(2,1)}, u32[]{:S(2)}, u32[]{:S(2)}) collective-permute-start(bf16[4,256,256]{2,1,0:T(8,128)(2,1)} %collective-permute-done.5.refs_2_), channel_id=1, source_target_pairs={{0,48},{16,0},{32,16},{48,32},{1,49},{17,1},{33,17},{49,33},{2,50}... | collective-permute-start | bytes 1572872 | tf_op jit(solution)/shard_map/ppermute | solution.py:26
  107.7 0.8 collective-permute-done.15.refs_12_
  108.6 3.7 %collective-permute-start.17 = (bf16[4,256,256]{2,1,0:T(8,128)(2,1)}, bf16[4,256,256]{2,1,0:T(8,128)(2,1)}, u32[]{:S(2)}, u32[]{:S(2)}) collective-permute-start(bf16[4,256,256]{2,1,0:T(8,128)(2,1)} %collective-permute-done.15.refs_12_), channel_id=1, source_target_pairs={{0,64},{64,0},{128,192},{192,128},{256,320},{320,256},{384,448},{4... | collective-permute-start | bytes 1572872 | tf_op jit(solution)/shard_map/ppermute | solution.py:36
  112.3 0.2 select_reduce_fusion.1
  112.5 0.2 convert_reduce_fusion
  112.7 0.1 compare_select_fusion.10
  112.9 3.0 %collective-permute-start.6 = (bf16[4,256,256]{2,1,0:T(8,128)(2,1)}, bf16[4,256,256]{2,1,0:T(8,128)(2,1)}, u32[]{:S(2)}, u32[]{:S(2)}) collective-permute-start(bf16[4,256,256]{2,1,0:T(8,128)(2,1)} %collective-permute-done.5.refs_2_), channel_id=1, source_target_pairs={{0,8},{8,0},{1,9},{9,1},{2,10},{10,2},{3,11},{11,3},{4,12},{12,4},... | collective-permute-start | bytes 1572872 | tf_op jit(solution)/shard_map/ppermute | solution.py:36
  115.9 1.9 %collective-permute-start.16 = (bf16[4,256,256]{2,1,0:T(8,128)(2,1)}, bf16[4,256,256]{2,1,0:T(8,128)(2,1)}, u32[]{:S(2)}, u32[]{:S(2)}) collective-permute-start(bf16[4,256,256]{2,1,0:T(8,128)(2,1)} %collective-permute-done.15.refs_12_), channel_id=1, source_target_pairs={{0,8},{8,0},{1,9},{9,1},{2,10},{10,2},{3,11},{11,3},{4,12},{12,4},... | collective-permute-start | bytes 1572872 | tf_op jit(solution)/shard_map/ppermute | solution.py:36
  117.9 2.4 %collective-permute-start.12 = (bf16[4,256,256]{2,1,0:T(8,128)(2,1)}, bf16[4,256,256]{2,1,0:T(8,128)(2,1)}, u32[]{:S(2)}, u32[]{:S(2)}) collective-permute-start(bf16[4,256,256]{2,1,0:T(8,128)(2,1)} %collective-permute-done.11.refs_8_), channel_id=1, source_target_pairs={{0,8},{8,0},{1,9},{9,1},{2,10},{10,2},{3,11},{11,3},{4,12},{12,4},... | collective-permute-start | bytes 1572872 | tf_op jit(solution)/shard_map/ppermute | solution.py:36
  120.3 1.9 %collective-permute-start.14 = (bf16[4,256,256]{2,1,0:T(8,128)(2,1)}, bf16[4,256,256]{2,1,0:T(8,128)(2,1)}, u32[]{:S(2)}, u32[]{:S(2)}) collective-permute-start(bf16[4,256,256]{2,1,0:T(8,128)(2,1)} %collective-permute-done.13.refs_10_), channel_id=1, source_target_pairs={{0,8},{8,0},{1,9},{9,1},{2,10},{10,2},{3,11},{11,3},{4,12},{12,4},... | collective-permute-start | bytes 1572872 | tf_op jit(solution)/shard_map/ppermute | solution.py:36
  122.2 0.9 collective-permute-done.17.refs_14_
  123.1 4.3 %collective-permute-start.18 = (bf16[4,256,256]{2,1,0:T(8,128)(2,1)}, bf16[4,256,256]{2,1,0:T(8,128)(2,1)}, u32[]{:S(2)}, u32[]{:S(2)}) collective-permute-start(bf16[4,256,256]{2,1,0:T(8,128)(2,1)} %collective-permute-done.17.refs_14_), channel_id=1, source_target_pairs={{0,8},{8,0},{1,9},{9,1},{2,10},{10,2},{3,11},{11,3},{4,12},{12,4},... | collective-permute-start | bytes 1572872 | tf_op jit(solution)/shard_map/ppermute | solution.py:36
  127.6 1.6 collective-permute-done.18.refs_15_
  129.2 0.1 broadcast_in_dim.105.refs_16_
  129.4 6.3 %score.1 = f32[64,2,128]{2,1,0:T(2,128)S(1)} custom-call(s32[33]{0:T(128)S(1)} %pad_add_fusion.where_ref, bf16[8,496,256]{2,1,0:T(8,128)(2,1)S(1)} %all-to-all-done.acts_ref, bf16[4,256,256]{2,1,0:T(8,128)(2,1)} %copy-done, bf16[4,256,256]{2,1,0:T(8,128)(2,1)} %copy-done.4, bf16[4,256,256]{2,1,0:T(8,128)(2,1)} %collective-permute-done.5.refs_2_, ...), custom_call_target="tpu_custom_call" | custom-call | tf_op jit(solution)/shard_map/score/pallas_call | solution.py:134
  135.7 18.1 %all_to_all.15.got_ref = f32[64,2,128]{2,1,0:T(2,128)S(1)} all-to-all(f32[64,2,128]{2,1,0:T(2,128)S(1)} %score.1), channel_id=1, replica_groups=mesh['y'=8,'x'=4,'core'=2,'mp'=8] {'y','x','core'}, dimensions={0} | all-to-all | bytes 131072 | tf_op jit(solution)/shard_map/all_to_all | solution.py:21
  153.8 0.1 copy.26
  153.9 0.1 copy.27
  154.1 0.2 reshape.135
  154.2 0.6 fusion.totals_ref
  154.8 0.6 gather.1
  155.4 11.7 %all_to_all.16.final_ref = f32[8,34,128]{2,1,0:T(8,128)S(1)} all-to-all(f32[8,34,128]{2,1,0:T(8,128)S(1)} %gather.1), channel_id=1, replica_groups=mesh['y'=8,'x'=4,'core'=2,'mp'=8] {'mp'}, dimensions={0} | all-to-all | bytes 278528 | tf_op jit(solution)/shard_map/all_to_all | solution.py:21
  167.1 0.1 reshape.136
  167.4 0.8 reshape.137
  168.1 0.9 finish.1
  (63 shorter events, 1.0 us)
Async XLA Ops:
  0.6 1.5 copy-start.2
  0.6 1.6 copy-start.6
  0.7 1.6 copy-start.9
  3.7 11.0 %copy-start.1 = (bf16[2048,256]{1,0:T(8,128)(2,1)S(1)}, bf16[2048,256]{1,0:T(8,128)(2,1)}, u32[]{:S(2)}) copy-start(bf16[2048,256]{1,0:T(8,128)(2,1)} %param.10) | copy-start | bytes 3145732
  3.7 125.5 %all-to-all-start = ((bf16[8,496,256]{2,1,0:T(8,128)(2,1)}), bf16[8,496,256]{2,1,0:T(8,128)(2,1)S(1)}, u32[]{:S(2)}, u32[]{:S(2)}) async-start(bf16[8,496,256]{2,1,0:T(8,128)(2,1)} %pad_maximum_fusion), calls=%async_computation | async-start | bytes 4063232 | tf_op jit(solution)/shard_map/all_to_all | solution.py:21
  14.7 64.5 %copy-start.5 = (s32[384]{0:T(512)S(1)}, s32[384]{0:T(512)}, u32[]{:S(2)}) copy-start(s32[384]{0:T(512)} %param.15) | copy-start | bytes 4612
  14.7 64.6 %copy-start.8 = (s32[960]{0:T(1024)S(1)}, s32[960]{0:T(1024)}, u32[]{:S(2)}) copy-start(s32[960]{0:T(1024)} %param.13) | copy-start | bytes 11524
  14.7 80.5 %copy-start.7 = (s32[960]{0:T(1024)S(1)}, s32[960]{0:T(1024)}, u32[]{:S(2)}) copy-start(s32[960]{0:T(1024)} %param.14) | copy-start | bytes 11524
  14.8 48.7 %collective-permute-start.2 = (bf16[256,256]{1,0:T(8,128)(2,1)S(1)}, bf16[256,256]{1,0:T(8,128)(2,1)S(1)}, u32[]{:S(2)}, u32[]{:S(2)}) collective-permute-start(bf16[256,256]{1,0:T(8,128)(2,1)S(1)} %dynamic-slice_bitcast_fusion.1), channel_id=1, source_target_pairs={{7,0},{0,1},{1,2},{2,3},{3,4},{4,5},{5,6},{6,7},{15,8},{8,9},{9,10... | collective-permute-start | bytes 393224 | tf_op jit(solution)/shard_map/ppermute | solution.py:53
  18.2 51.3 %collective-permute-start.3 = (bf16[256,256]{1,0:T(8,128)(2,1)S(1)}, bf16[256,256]{1,0:T(8,128)(2,1)S(1)}, u32[]{:S(2)}, u32[]{:S(2)}) collective-permute-start(bf16[256,256]{1,0:T(8,128)(2,1)S(1)} %dynamic-slice_bitcast_fusion), channel_id=1, source_target_pairs={{6,0},{7,1},{0,2},{1,3},{2,4},{3,5},{4,6},{5,7},{14,8},{15,9},{8,1... | collective-permute-start | bytes 393224 | tf_op jit(solution)/shard_map/ppermute | solution.py:53
  22.2 47.3 %collective-permute-start.1 = (bf16[256,256]{1,0:T(8,128)(2,1)S(1)}, bf16[256,256]{1,0:T(8,128)(2,1)S(1)}, u32[]{:S(2)}, u32[]{:S(2)}) collective-permute-start(bf16[256,256]{1,0:T(8,128)(2,1)S(1)} %dynamic-slice_bitcast_fusion.2), channel_id=1, source_target_pairs={{1,0},{2,1},{3,2},{4,3},{5,4},{6,5},{7,6},{0,7},{9,8},{10,9},{11,1... | collective-permute-start | bytes 393224 | tf_op jit(solution)/shard_map/ppermute | solution.py:53
  25.7 51.4 %collective-permute-start = (bf16[256,256]{1,0:T(8,128)(2,1)S(1)}, bf16[256,256]{1,0:T(8,128)(2,1)S(1)}, u32[]{:S(2)}, u32[]{:S(2)}) collective-permute-start(bf16[256,256]{1,0:T(8,128)(2,1)S(1)} %dynamic-slice_bitcast_fusion.3), channel_id=1, source_target_pairs={{4,0},{5,1},{6,2},{7,3},{0,4},{1,5},{2,6},{3,7},{12,8},{13,9},{14,... | collective-permute-start | bytes 393224 | tf_op jit(solution)/shard_map/ppermute | solution.py:53
  77.1 52.2 %copy-start = (bf16[4,256,256]{2,1,0:T(8,128)(2,1)}, bf16[4,256,256]{2,1,0:T(8,128)(2,1)S(1)}, u32[]{:S(2)}) copy-start(bf16[4,256,256]{2,1,0:T(8,128)(2,1)S(1)} %pad_maximum_fusion.1.refs_0_) | copy-start | bytes 1572868
  77.2 16.1 %collective-permute-start.7 = (bf16[4,256,256]{2,1,0:T(8,128)(2,1)S(1)}, bf16[4,256,256]{2,1,0:T(8,128)(2,1)S(1)}, u32[]{:S(2)}, u32[]{:S(2)}) collective-permute-start(bf16[4,256,256]{2,1,0:T(8,128)(2,1)S(1)} %pad_maximum_fusion.1.refs_0_), channel_id=1, source_target_pairs={{0,16},{16,32},{32,48},{48,0},{1,17},{17,33},{33,49},{49,1},{2,18}... | collective-permute-start | bytes 1572872 | tf_op jit(solution)/shard_map/ppermute | solution.py:26
  79.4 18.2 %collective-permute-start.9 = (bf16[4,256,256]{2,1,0:T(8,128)(2,1)S(1)}, bf16[4,256,256]{2,1,0:T(8,128)(2,1)}, u32[]{:S(2)}, u32[]{:S(2)}) collective-permute-start(bf16[4,256,256]{2,1,0:T(8,128)(2,1)S(1)} %pad_maximum_fusion.1.refs_0_), channel_id=1, source_target_pairs={{0,48},{16,0},{32,16},{48,32},{1,49},{17,1},{33,17},{49,33},{2,50}... | collective-permute-start | bytes 1572872 | tf_op jit(solution)/shard_map/ppermute | solution.py:26
  84.0 17.2 %collective-permute-start.5 = (bf16[4,256,256]{2,1,0:T(8,128)(2,1)S(1)}, bf16[4,256,256]{2,1,0:T(8,128)(2,1)}, u32[]{:S(2)}, u32[]{:S(2)}) collective-permute-start(bf16[4,256,256]{2,1,0:T(8,128)(2,1)S(1)} %pad_maximum_fusion.1.refs_0_), channel_id=1, source_target_pairs={{0,64},{64,0},{128,192},{192,128},{256,320},{320,256},{384,448},{4... | collective-permute-start | bytes 1572872 | tf_op jit(solution)/shard_map/ppermute | solution.py:36
  85.9 17.2 %collective-permute-start.4 = (bf16[4,256,256]{2,1,0:T(8,128)(2,1)S(1)}, bf16[4,256,256]{2,1,0:T(8,128)(2,1)S(1)}, u32[]{:S(2)}, u32[]{:S(2)}) collective-permute-start(bf16[4,256,256]{2,1,0:T(8,128)(2,1)S(1)} %pad_maximum_fusion.1.refs_0_), channel_id=1, source_target_pairs={{0,8},{8,0},{1,9},{9,1},{2,10},{10,2},{3,11},{11,3},{4,12},{12,4},... | collective-permute-start | bytes 1572872 | tf_op jit(solution)/shard_map/ppermute | solution.py:36
  93.2 36.1 %copy-start.3 = (bf16[4,256,256]{2,1,0:T(8,128)(2,1)}, bf16[4,256,256]{2,1,0:T(8,128)(2,1)S(1)}, u32[]{:S(2)}) copy-start(bf16[4,256,256]{2,1,0:T(8,128)(2,1)S(1)} %collective-permute-done.7.refs_4_) | copy-start | bytes 1572868
  93.2 15.3 %collective-permute-start.15 = (bf16[4,256,256]{2,1,0:T(8,128)(2,1)S(1)}, bf16[4,256,256]{2,1,0:T(8,128)(2,1)}, u32[]{:S(2)}, u32[]{:S(2)}) collective-permute-start(bf16[4,256,256]{2,1,0:T(8,128)(2,1)S(1)} %collective-permute-done.7.refs_4_), channel_id=1, source_target_pairs={{0,16},{16,32},{32,48},{48,0},{1,17},{17,33},{33,49},{49,1},{2,18}... | collective-permute-start | bytes 1572872 | tf_op jit(solution)/shard_map/ppermute | solution.py:26
  95.5 20.5 %collective-permute-start.11 = (bf16[4,256,256]{2,1,0:T(8,128)(2,1)S(1)}, bf16[4,256,256]{2,1,0:T(8,128)(2,1)}, u32[]{:S(2)}, u32[]{:S(2)}) collective-permute-start(bf16[4,256,256]{2,1,0:T(8,128)(2,1)S(1)} %collective-permute-done.7.refs_4_), channel_id=1, source_target_pairs={{0,448},{64,128},{128,64},{192,256},{256,192},{320,384},{384,320},... | collective-permute-start | bytes 1572872 | tf_op jit(solution)/shard_map/ppermute | solution.py:31
  97.6 20.3 %collective-permute-start.8 = (bf16[4,256,256]{2,1,0:T(8,128)(2,1)S(1)}, bf16[4,256,256]{2,1,0:T(8,128)(2,1)}, u32[]{:S(2)}, u32[]{:S(2)}) collective-permute-start(bf16[4,256,256]{2,1,0:T(8,128)(2,1)S(1)} %collective-permute-done.7.refs_4_), channel_id=1, source_target_pairs={{0,8},{8,0},{1,9},{9,1},{2,10},{10,2},{3,11},{11,3},{4,12},{12,4},... | collective-permute-start | bytes 1572872 | tf_op jit(solution)/shard_map/ppermute | solution.py:36
  101.2 11.8 %collective-permute-start.10 = (bf16[4,256,256]{2,1,0:T(8,128)(2,1)}, bf16[4,256,256]{2,1,0:T(8,128)(2,1)}, u32[]{:S(2)}, u32[]{:S(2)}) collective-permute-start(bf16[4,256,256]{2,1,0:T(8,128)(2,1)} %collective-permute-done.9.refs_6_), channel_id=1, source_target_pairs={{0,8},{8,0},{1,9},{9,1},{2,10},{10,2},{3,11},{11,3},{4,12},{12,4},... | collective-permute-start | bytes 1572872 | tf_op jit(solution)/shard_map/ppermute | solution.py:36
  103.1 5.5 %copy-start.4 = (bf16[4,256,256]{2,1,0:T(8,128)(2,1)}, bf16[4,256,256]{2,1,0:T(8,128)(2,1)S(1)}, u32[]{:S(2)}) copy-start(bf16[4,256,256]{2,1,0:T(8,128)(2,1)S(1)} %collective-permute-done.4.refs_1_) | copy-start | bytes 1572868
  103.1 17.2 %collective-permute-start.13 = (bf16[4,256,256]{2,1,0:T(8,128)(2,1)}, bf16[4,256,256]{2,1,0:T(8,128)(2,1)}, u32[]{:S(2)}, u32[]{:S(2)}) collective-permute-start(bf16[4,256,256]{2,1,0:T(8,128)(2,1)} %collective-permute-done.5.refs_2_), channel_id=1, source_target_pairs={{0,48},{16,0},{32,16},{48,32},{1,49},{17,1},{33,17},{49,33},{2,50}... | collective-permute-start | bytes 1572872 | tf_op jit(solution)/shard_map/ppermute | solution.py:26
  108.6 14.5 %collective-permute-start.17 = (bf16[4,256,256]{2,1,0:T(8,128)(2,1)}, bf16[4,256,256]{2,1,0:T(8,128)(2,1)}, u32[]{:S(2)}, u32[]{:S(2)}) collective-permute-start(bf16[4,256,256]{2,1,0:T(8,128)(2,1)} %collective-permute-done.15.refs_12_), channel_id=1, source_target_pairs={{0,64},{64,0},{128,192},{192,128},{256,320},{320,256},{384,448},{4... | collective-permute-start | bytes 1572872 | tf_op jit(solution)/shard_map/ppermute | solution.py:36
  112.9 14.6 %collective-permute-start.6 = (bf16[4,256,256]{2,1,0:T(8,128)(2,1)}, bf16[4,256,256]{2,1,0:T(8,128)(2,1)}, u32[]{:S(2)}, u32[]{:S(2)}) collective-permute-start(bf16[4,256,256]{2,1,0:T(8,128)(2,1)} %collective-permute-done.5.refs_2_), channel_id=1, source_target_pairs={{0,8},{8,0},{1,9},{9,1},{2,10},{10,2},{3,11},{11,3},{4,12},{12,4},... | collective-permute-start | bytes 1572872 | tf_op jit(solution)/shard_map/ppermute | solution.py:36
  115.9 11.7 %collective-permute-start.16 = (bf16[4,256,256]{2,1,0:T(8,128)(2,1)}, bf16[4,256,256]{2,1,0:T(8,128)(2,1)}, u32[]{:S(2)}, u32[]{:S(2)}) collective-permute-start(bf16[4,256,256]{2,1,0:T(8,128)(2,1)} %collective-permute-done.15.refs_12_), channel_id=1, source_target_pairs={{0,8},{8,0},{1,9},{9,1},{2,10},{10,2},{3,11},{11,3},{4,12},{12,4},... | collective-permute-start | bytes 1572872 | tf_op jit(solution)/shard_map/ppermute | solution.py:36
  117.9 9.7 %collective-permute-start.12 = (bf16[4,256,256]{2,1,0:T(8,128)(2,1)}, bf16[4,256,256]{2,1,0:T(8,128)(2,1)}, u32[]{:S(2)}, u32[]{:S(2)}) collective-permute-start(bf16[4,256,256]{2,1,0:T(8,128)(2,1)} %collective-permute-done.11.refs_8_), channel_id=1, source_target_pairs={{0,8},{8,0},{1,9},{9,1},{2,10},{10,2},{3,11},{11,3},{4,12},{12,4},... | collective-permute-start | bytes 1572872 | tf_op jit(solution)/shard_map/ppermute | solution.py:36
  120.3 7.3 %collective-permute-start.14 = (bf16[4,256,256]{2,1,0:T(8,128)(2,1)}, bf16[4,256,256]{2,1,0:T(8,128)(2,1)}, u32[]{:S(2)}, u32[]{:S(2)}) collective-permute-start(bf16[4,256,256]{2,1,0:T(8,128)(2,1)} %collective-permute-done.13.refs_10_), channel_id=1, source_target_pairs={{0,8},{8,0},{1,9},{9,1},{2,10},{10,2},{3,11},{11,3},{4,12},{12,4},... | collective-permute-start | bytes 1572872 | tf_op jit(solution)/shard_map/ppermute | solution.py:36
  123.1 6.1 %collective-permute-start.18 = (bf16[4,256,256]{2,1,0:T(8,128)(2,1)}, bf16[4,256,256]{2,1,0:T(8,128)(2,1)}, u32[]{:S(2)}, u32[]{:S(2)}) collective-permute-start(bf16[4,256,256]{2,1,0:T(8,128)(2,1)} %collective-permute-done.17.refs_14_), channel_id=1, source_target_pairs={{0,8},{8,0},{1,9},{9,1},{2,10},{10,2},{3,11},{11,3},{4,12},{12,4},... | collective-permute-start | bytes 1572872 | tf_op jit(solution)/shard_map/ppermute | solution.py:36

commit v4 on v2

--- a/solution.py
+++ b/solution.py
@@ -13,6 +13,8 @@
 BF16 = jnp.bfloat16
 PLANES = 8
 TOK = 16
+
+CHUNKS = ((0, 0, 2), (0, 2, 2), (1, 0, 2), (1, 2, 1), (1, 3, 1))
 
 
 def exchange(value, axis):
@@ -71,20 +73,21 @@
         return pltpu.make_async_copy(pieces[2 * s + side].at[p], target, sem.at[side, s, p])
 
     for side in range(2):
-        for s in range(8):
-            for p in range(4):
+        for p in range(4):
+            for s in range(8):
                 fetch(side, s, p).start()
     for p in range(4):
         a_ref[0, :, p * shard : (p + 1) * shard] = acts_ref[2 * p + core, 0:tokens, :]
         a_ref[1, :, p * shard : (p + 1) * shard] = acts_ref[2 * p + 1 - core, 0:tokens, :]
     head_rows = jnp.concatenate([acts_ref[j, 2 * tokens :, :] for j in range(PLANES)], axis=1)
-    for side in range(2):
-        for s in range(8):
-            for p in range(4):
-                fetch(side, s, p).wait()
+    for side, p, parts in CHUNKS:
+        for q in range(p, p + parts):
+            for s in range(8):
+                fetch(side, s, q).wait()
+        at = slice(p * shard, (p + parts) * shard)
         for j in range(PLANES):
-            part = jnp.dot(a_ref[side], w_ref[side, j], preferred_element_type=F32)
-            if side == 0:
+            part = jnp.dot(a_ref[side, :, at], w_ref[side, j, at], preferred_element_type=F32)
+            if side == 0 and p == 0:
                 proj_ref[j] = part
             else:
                 proj_ref[j] += part

time: 170 us -> 170 us (level)
  no operation moved by 1% of the time
where the time goes in v4:
time: 170 us; the launch traced here: 169 us
  starting transfers between devices  70.1 us (41%)
  waiting for transfers between devices  53.4 us (31%)
  blocking collectives  29.8 us (18%)
  Pallas kernels  7.16 us (4%)
  local copies, waits for them, and re-layouts  3.79 us (2%)
  other arithmetic  2.42 us (1%)
    ppermute x4, waiting for transfers between devices, from_plane(): return lax.ppermute(value, ('y', 'x', 'core', 'mp'), pairs)  46.2 us
    all_to_all x2, blocking collectives, exchange(): return lax.all_to_all(value, axis, split_axis=0, concat_axis=0, tiled=True)  29.8 us
    ppermute x10, starting transfers between devices, swap(): return lax.ppermute(value, axis, [(s, s ^ 1) for s in range(size)])  28.1 us
    ppermute x4, starting transfers between devices, from_plane(): return lax.ppermute(value, ('y', 'x', 'core', 'mp'), pairs)  15.9 us
    ppermute x4, starting transfers between devices, shift(): lax.ppermute(value, axis, [(s, (s + step) % size) for s in range(size)])  13 us
    all_to_all x1, starting transfers between devices, exchange(): return lax.all_to_all(value, axis, split_axis=0, concat_axis=0, tiled=True)  11 us
    pallas_call x1, Pallas kernels, score(): pl.pallas_call(score_kernel, out_shape=jax.ShapeDtypeStruct((owners, 2, 1...  6.29 us
    ppermute x4, waiting for transfers between devices, shift(): lax.ppermute(value, axis, [(s, (s + step) % size) for s in range(size)])  4.72 us
  transfers between devices with their start and end apart: 20, of which 7 were waited for; matrix products, arithmetic and copies ran while one was open for 1% of the time, Pallas kernels for 0%

profile of v4, /device:TPU:1, one launch (start us, length us, event | category | flops | bytes accessed | tf_op | source)
XLA Modules:
  0.0 168.7 jit_solution(2932703414088702082)
XLA Ops:
  0.7 1.3 copy.31
  2.0 0.1 copy-done.2
  2.3 1.4 pad_maximum_fusion
  3.7 11.0 %all-to-all-start = ((bf16[8,496,256]{2,1,0:T(8,128)(2,1)}), bf16[8,496,256]{2,1,0:T(8,128)(2,1)S(1)}, u32[]{:S(2)}, u32[]{:S(2)}) async-start(bf16[8,496,256]{2,1,0:T(8,128)(2,1)} %pad_maximum_fusion), calls=%async_computation | async-start | bytes 4063232 | tf_op jit(solution)/shard_map/all_to_all | solution.py:21
  14.8 3.4 %collective-permute-start.2 = (bf16[256,256]{1,0:T(8,128)(2,1)S(1)}, bf16[256,256]{1,0:T(8,128)(2,1)S(1)}, u32[]{:S(2)}, u32[]{:S(2)}) collective-permute-start(bf16[256,256]{1,0:T(8,128)(2,1)S(1)} %dynamic-slice_bitcast_fusion.1), channel_id=1, source_target_pairs={{7,0},{0,1},{1,2},{2,3},{3,4},{4,5},{5,6},{6,7},{15,8},{8,9},{9,10... | collective-permute-start | bytes 393224 | tf_op jit(solution)/shard_map/ppermute | solution.py:53
  18.2 4.0 %collective-permute-start.3 = (bf16[256,256]{1,0:T(8,128)(2,1)S(1)}, bf16[256,256]{1,0:T(8,128)(2,1)S(1)}, u32[]{:S(2)}, u32[]{:S(2)}) collective-permute-start(bf16[256,256]{1,0:T(8,128)(2,1)S(1)} %dynamic-slice_bitcast_fusion), channel_id=1, source_target_pairs={{6,0},{7,1},{0,2},{1,3},{2,4},{3,5},{4,6},{5,7},{14,8},{15,9},{8,1... | collective-permute-start | bytes 393224 | tf_op jit(solution)/shard_map/ppermute | solution.py:53
  22.2 3.4 %collective-permute-start.1 = (bf16[256,256]{1,0:T(8,128)(2,1)S(1)}, bf16[256,256]{1,0:T(8,128)(2,1)S(1)}, u32[]{:S(2)}, u32[]{:S(2)}) collective-permute-start(bf16[256,256]{1,0:T(8,128)(2,1)S(1)} %dynamic-slice_bitcast_fusion.2), channel_id=1, source_target_pairs={{1,0},{2,1},{3,2},{4,3},{5,4},{6,5},{7,6},{0,7},{9,8},{10,9},{11,1... | collective-permute-start | bytes 393224 | tf_op jit(solution)/shard_map/ppermute | solution.py:53
  25.7 5.2 %collective-permute-start = (bf16[256,256]{1,0:T(8,128)(2,1)S(1)}, bf16[256,256]{1,0:T(8,128)(2,1)S(1)}, u32[]{:S(2)}, u32[]{:S(2)}) collective-permute-start(bf16[256,256]{1,0:T(8,128)(2,1)S(1)} %dynamic-slice_bitcast_fusion.3), channel_id=1, source_target_pairs={{4,0},{5,1},{6,2},{7,3},{0,4},{1,5},{2,6},{3,7},{12,8},{13,9},{14,... | collective-permute-start | bytes 393224 | tf_op jit(solution)/shard_map/ppermute | solution.py:53
  30.9 32.7 %collective-permute-done.2 = bf16[256,256]{1,0:T(8,128)(2,1)S(1)} collective-permute-done((bf16[256,256]{1,0:T(8,128)(2,1)S(1)}, bf16[256,256]{1,0:T(8,128)(2,1)S(1)}, u32[]{:S(2)}, u32[]{:S(2)}) %collective-permute-start.2) | collective-permute-done | bytes 131104 | tf_op jit(solution)/shard_map/ppermute | solution.py:53
  63.6 5.9 %collective-permute-done.3 = bf16[256,256]{1,0:T(8,128)(2,1)S(1)} collective-permute-done((bf16[256,256]{1,0:T(8,128)(2,1)S(1)}, bf16[256,256]{1,0:T(8,128)(2,1)S(1)}, u32[]{:S(2)}, u32[]{:S(2)}) %collective-permute-start.3) | collective-permute-done | bytes 131104 | tf_op jit(solution)/shard_map/ppermute | solution.py:53
  69.5 7.6 %collective-permute-done = bf16[256,256]{1,0:T(8,128)(2,1)S(1)} collective-permute-done((bf16[256,256]{1,0:T(8,128)(2,1)S(1)}, bf16[256,256]{1,0:T(8,128)(2,1)S(1)}, u32[]{:S(2)}, u32[]{:S(2)}) %collective-permute-start) | collective-permute-done | bytes 131104 | tf_op jit(solution)/shard_map/ppermute | solution.py:53
  77.2 1.9 %collective-permute-start.7 = (bf16[4,256,256]{2,1,0:T(8,128)(2,1)S(1)}, bf16[4,256,256]{2,1,0:T(8,128)(2,1)S(1)}, u32[]{:S(2)}, u32[]{:S(2)}) collective-permute-start(bf16[4,256,256]{2,1,0:T(8,128)(2,1)S(1)} %pad_maximum_fusion.1.refs_0_), channel_id=1, source_target_pairs={{0,16},{16,32},{32,48},{48,0},{1,17},{17,33},{33,49},{49,1},{2,18}... | collective-permute-start | bytes 1572872 | tf_op jit(solution)/shard_map/ppermute | solution.py:26
  79.1 0.1 broadcast_in_dim.107
  79.2 0.1 add.154
  79.4 4.6 %collective-permute-start.9 = (bf16[4,256,256]{2,1,0:T(8,128)(2,1)S(1)}, bf16[4,256,256]{2,1,0:T(8,128)(2,1)}, u32[]{:S(2)}, u32[]{:S(2)}) collective-permute-start(bf16[4,256,256]{2,1,0:T(8,128)(2,1)S(1)} %pad_maximum_fusion.1.refs_0_), channel_id=1, source_target_pairs={{0,48},{16,0},{32,16},{48,32},{1,49},{17,1},{33,17},{49,33},{2,50}... | collective-permute-start | bytes 1572872 | tf_op jit(solution)/shard_map/ppermute | solution.py:26
  84.0 1.9 %collective-permute-start.5 = (bf16[4,256,256]{2,1,0:T(8,128)(2,1)S(1)}, bf16[4,256,256]{2,1,0:T(8,128)(2,1)}, u32[]{:S(2)}, u32[]{:S(2)}) collective-permute-start(bf16[4,256,256]{2,1,0:T(8,128)(2,1)S(1)} %pad_maximum_fusion.1.refs_0_), channel_id=1, source_target_pairs={{0,64},{64,0},{128,192},{192,128},{256,320},{320,256},{384,448},{4... | collective-permute-start | bytes 1572872 | tf_op jit(solution)/shard_map/ppermute | solution.py:36
  85.9 3.4 %collective-permute-start.4 = (bf16[4,256,256]{2,1,0:T(8,128)(2,1)S(1)}, bf16[4,256,256]{2,1,0:T(8,128)(2,1)S(1)}, u32[]{:S(2)}, u32[]{:S(2)}) collective-permute-start(bf16[4,256,256]{2,1,0:T(8,128)(2,1)S(1)} %pad_maximum_fusion.1.refs_0_), channel_id=1, source_target_pairs={{0,8},{8,0},{1,9},{9,1},{2,10},{10,2},{3,11},{11,3},{4,12},{12,4},... | collective-permute-start | bytes 1572872 | tf_op jit(solution)/shard_map/ppermute | solution.py:36
  89.4 3.9 %collective-permute-done.7.refs_4_ = bf16[4,256,256]{2,1,0:T(8,128)(2,1)S(1)} collective-permute-done((bf16[4,256,256]{2,1,0:T(8,128)(2,1)S(1)}, bf16[4,256,256]{2,1,0:T(8,128)(2,1)S(1)}, u32[]{:S(2)}, u32[]{:S(2)}) %collective-permute-start.7) | collective-permute-done | bytes 524320 | tf_op jit(solution)/shard_map/ppermute | solution.py:26
  93.2 1.9 %collective-permute-start.15 = (bf16[4,256,256]{2,1,0:T(8,128)(2,1)S(1)}, bf16[4,256,256]{2,1,0:T(8,128)(2,1)}, u32[]{:S(2)}, u32[]{:S(2)}) collective-permute-start(bf16[4,256,256]{2,1,0:T(8,128)(2,1)S(1)} %collective-permute-done.7.refs_4_), channel_id=1, source_target_pairs={{0,16},{16,32},{32,48},{48,0},{1,17},{17,33},{33,49},{49,1},{2,18}... | collective-permute-start | bytes 1572872 | tf_op jit(solution)/shard_map/ppermute | solution.py:26
  95.2 0.2 select_reduce_fusion
  95.5 2.1 %collective-permute-start.11 = (bf16[4,256,256]{2,1,0:T(8,128)(2,1)S(1)}, bf16[4,256,256]{2,1,0:T(8,128)(2,1)}, u32[]{:S(2)}, u32[]{:S(2)}) collective-permute-start(bf16[4,256,256]{2,1,0:T(8,128)(2,1)S(1)} %collective-permute-done.7.refs_4_), channel_id=1, source_target_pairs={{0,448},{64,128},{128,64},{192,256},{256,192},{320,384},{384,320},... | collective-permute-start | bytes 1572872 | tf_op jit(solution)/shard_map/ppermute | solution.py:31
  97.6 3.5 %collective-permute-start.8 = (bf16[4,256,256]{2,1,0:T(8,128)(2,1)S(1)}, bf16[4,256,256]{2,1,0:T(8,128)(2,1)}, u32[]{:S(2)}, u32[]{:S(2)}) collective-permute-start(bf16[4,256,256]{2,1,0:T(8,128)(2,1)S(1)} %collective-permute-done.7.refs_4_), channel_id=1, source_target_pairs={{0,8},{8,0},{1,9},{9,1},{2,10},{10,2},{3,11},{11,3},{4,12},{12,4},... | collective-permute-start | bytes 1572872 | tf_op jit(solution)/shard_map/ppermute | solution.py:36
  101.2 1.9 %collective-permute-start.10 = (bf16[4,256,256]{2,1,0:T(8,128)(2,1)}, bf16[4,256,256]{2,1,0:T(8,128)(2,1)}, u32[]{:S(2)}, u32[]{:S(2)}) collective-permute-start(bf16[4,256,256]{2,1,0:T(8,128)(2,1)} %collective-permute-done.9.refs_6_), channel_id=1, source_target_pairs={{0,8},{8,0},{1,9},{9,1},{2,10},{10,2},{3,11},{11,3},{4,12},{12,4},... | collective-permute-start | bytes 1572872 | tf_op jit(solution)/shard_map/ppermute | solution.py:36
  103.1 4.6 %collective-permute-start.13 = (bf16[4,256,256]{2,1,0:T(8,128)(2,1)}, bf16[4,256,256]{2,1,0:T(8,128)(2,1)}, u32[]{:S(2)}, u32[]{:S(2)}) collective-permute-start(bf16[4,256,256]{2,1,0:T(8,128)(2,1)} %collective-permute-done.5.refs_2_), channel_id=1, source_target_pairs={{0,48},{16,0},{32,16},{48,32},{1,49},{17,1},{33,17},{49,33},{2,50}... | collective-permute-start | bytes 1572872 | tf_op jit(solution)/shard_map/ppermute | solution.py:26
  107.7 0.8 collective-permute-done.15.refs_12_
  108.6 3.7 %collective-permute-start.17 = (bf16[4,256,256]{2,1,0:T(8,128)(2,1)}, bf16[4,256,256]{2,1,0:T(8,128)(2,1)}, u32[]{:S(2)}, u32[]{:S(2)}) collective-permute-start(bf16[4,256,256]{2,1,0:T(8,128)(2,1)} %collective-permute-done.15.refs_12_), channel_id=1, source_target_pairs={{0,64},{64,0},{128,192},{192,128},{256,320},{320,256},{384,448},{4... | collective-permute-start | bytes 1572872 | tf_op jit(solution)/shard_map/ppermute | solution.py:36
  112.3 0.2 select_reduce_fusion.1
  112.5 0.2 convert_reduce_fusion
  112.7 0.1 compare_select_fusion.10
  112.9 3.0 %collective-permute-start.6 = (bf16[4,256,256]{2,1,0:T(8,128)(2,1)}, bf16[4,256,256]{2,1,0:T(8,128)(2,1)}, u32[]{:S(2)}, u32[]{:S(2)}) collective-permute-start(bf16[4,256,256]{2,1,0:T(8,128)(2,1)} %collective-permute-done.5.refs_2_), channel_id=1, source_target_pairs={{0,8},{8,0},{1,9},{9,1},{2,10},{10,2},{3,11},{11,3},{4,12},{12,4},... | collective-permute-start | bytes 1572872 | tf_op jit(solution)/shard_map/ppermute | solution.py:36
  115.9 1.9 %collective-permute-start.16 = (bf16[4,256,256]{2,1,0:T(8,128)(2,1)}, bf16[4,256,256]{2,1,0:T(8,128)(2,1)}, u32[]{:S(2)}, u32[]{:S(2)}) collective-permute-start(bf16[4,256,256]{2,1,0:T(8,128)(2,1)} %collective-permute-done.15.refs_12_), channel_id=1, source_target_pairs={{0,8},{8,0},{1,9},{9,1},{2,10},{10,2},{3,11},{11,3},{4,12},{12,4},... | collective-permute-start | bytes 1572872 | tf_op jit(solution)/shard_map/ppermute | solution.py:36
  117.9 2.4 %collective-permute-start.12 = (bf16[4,256,256]{2,1,0:T(8,128)(2,1)}, bf16[4,256,256]{2,1,0:T(8,128)(2,1)}, u32[]{:S(2)}, u32[]{:S(2)}) collective-permute-start(bf16[4,256,256]{2,1,0:T(8,128)(2,1)} %collective-permute-done.11.refs_8_), channel_id=1, source_target_pairs={{0,8},{8,0},{1,9},{9,1},{2,10},{10,2},{3,11},{11,3},{4,12},{12,4},... | collective-permute-start | bytes 1572872 | tf_op jit(solution)/shard_map/ppermute | solution.py:36
  120.3 1.9 %collective-permute-start.14 = (bf16[4,256,256]{2,1,0:T(8,128)(2,1)}, bf16[4,256,256]{2,1,0:T(8,128)(2,1)}, u32[]{:S(2)}, u32[]{:S(2)}) collective-permute-start(bf16[4,256,256]{2,1,0:T(8,128)(2,1)} %collective-permute-done.13.refs_10_), channel_id=1, source_target_pairs={{0,8},{8,0},{1,9},{9,1},{2,10},{10,2},{3,11},{11,3},{4,12},{12,4},... | collective-permute-start | bytes 1572872 | tf_op jit(solution)/shard_map/ppermute | solution.py:36
  122.2 0.9 collective-permute-done.17.refs_14_
  123.1 4.3 %collective-permute-start.18 = (bf16[4,256,256]{2,1,0:T(8,128)(2,1)}, bf16[4,256,256]{2,1,0:T(8,128)(2,1)}, u32[]{:S(2)}, u32[]{:S(2)}) collective-permute-start(bf16[4,256,256]{2,1,0:T(8,128)(2,1)} %collective-permute-done.17.refs_14_), channel_id=1, source_target_pairs={{0,8},{8,0},{1,9},{9,1},{2,10},{10,2},{3,11},{11,3},{4,12},{12,4},... | collective-permute-start | bytes 1572872 | tf_op jit(solution)/shard_map/ppermute | solution.py:36
  127.6 1.6 collective-permute-done.18.refs_15_
  129.2 0.1 broadcast_in_dim.113.refs_16_
  129.4 6.3 %score.1 = f32[64,2,128]{2,1,0:T(2,128)S(1)} custom-call(s32[33]{0:T(128)S(1)} %pad_add_fusion.where_ref, bf16[8,496,256]{2,1,0:T(8,128)(2,1)S(1)} %all-to-all-done.acts_ref, bf16[4,256,256]{2,1,0:T(8,128)(2,1)} %copy-done, bf16[4,256,256]{2,1,0:T(8,128)(2,1)} %copy-done.4, bf16[4,256,256]{2,1,0:T(8,128)(2,1)} %collective-permute-done.5.refs_2_, ...), custom_call_target="tpu_custom_call" | custom-call | tf_op jit(solution)/shard_map/score/pallas_call | solution.py:134
  135.7 18.1 %all_to_all.15 = f32[64,2,128]{2,1,0:T(2,128)S(1)} all-to-all(f32[64,2,128]{2,1,0:T(2,128)S(1)} %score.1), channel_id=1, replica_groups=mesh['y'=8,'x'=4,'core'=2,'mp'=8] {'y','x','core'}, dimensions={0} | all-to-all | bytes 131072 | tf_op jit(solution)/shard_map/all_to_all | solution.py:21
  153.8 0.1 copy.32
  153.9 0.1 copy.33
  154.1 0.2 reshape.143
  154.3 0.6 fusion
  154.9 0.2 fusion.5
  155.1 11.7 %all_to_all.16 = f32[8,34,128]{2,1,0:T(8,128)S(1)} all-to-all(f32[8,34,128]{2,1,0:T(8,128)S(1)} %broadcast_in_dim.115), channel_id=1, replica_groups=mesh['y'=8,'x'=4,'core'=2,'mp'=8] {'mp'}, dimensions={0} | all-to-all | bytes 278528 | tf_op jit(solution)/shard_map/all_to_all | solution.py:21
  166.9 0.1 reshape.145
  167.1 0.8 reshape.146
  167.9 0.9 finish.1
  (68 shorter events, 1.1 us)
Async XLA Ops:
  0.6 1.5 copy-start.2
  0.6 1.6 copy-start.6
  0.7 1.6 copy-start.9
  3.7 11.0 %copy-start.1 = (bf16[2048,256]{1,0:T(8,128)(2,1)S(1)}, bf16[2048,256]{1,0:T(8,128)(2,1)}, u32[]{:S(2)}) copy-start(bf16[2048,256]{1,0:T(8,128)(2,1)} %param.10) | copy-start | bytes 3145732
  3.7 125.5 %all-to-all-start = ((bf16[8,496,256]{2,1,0:T(8,128)(2,1)}), bf16[8,496,256]{2,1,0:T(8,128)(2,1)S(1)}, u32[]{:S(2)}, u32[]{:S(2)}) async-start(bf16[8,496,256]{2,1,0:T(8,128)(2,1)} %pad_maximum_fusion), calls=%async_computation | async-start | bytes 4063232 | tf_op jit(solution)/shard_map/all_to_all | solution.py:21
  14.7 64.5 %copy-start.5 = (s32[384]{0:T(512)S(1)}, s32[384]{0:T(512)}, u32[]{:S(2)}) copy-start(s32[384]{0:T(512)} %param.15) | copy-start | bytes 4612
  14.7 64.6 %copy-start.8 = (s32[960]{0:T(1024)S(1)}, s32[960]{0:T(1024)}, u32[]{:S(2)}) copy-start(s32[960]{0:T(1024)} %param.13) | copy-start | bytes 11524
  14.7 80.5 %copy-start.7 = (s32[960]{0:T(1024)S(1)}, s32[960]{0:T(1024)}, u32[]{:S(2)}) copy-start(s32[960]{0:T(1024)} %param.14) | copy-start | bytes 11524
  14.8 48.7 %collective-permute-start.2 = (bf16[256,256]{1,0:T(8,128)(2,1)S(1)}, bf16[256,256]{1,0:T(8,128)(2,1)S(1)}, u32[]{:S(2)}, u32[]{:S(2)}) collective-permute-start(bf16[256,256]{1,0:T(8,128)(2,1)S(1)} %dynamic-slice_bitcast_fusion.1), channel_id=1, source_target_pairs={{7,0},{0,1},{1,2},{2,3},{3,4},{4,5},{5,6},{6,7},{15,8},{8,9},{9,10... | collective-permute-start | bytes 393224 | tf_op jit(solution)/shard_map/ppermute | solution.py:53
  18.2 51.3 %collective-permute-start.3 = (bf16[256,256]{1,0:T(8,128)(2,1)S(1)}, bf16[256,256]{1,0:T(8,128)(2,1)S(1)}, u32[]{:S(2)}, u32[]{:S(2)}) collective-permute-start(bf16[256,256]{1,0:T(8,128)(2,1)S(1)} %dynamic-slice_bitcast_fusion), channel_id=1, source_target_pairs={{6,0},{7,1},{0,2},{1,3},{2,4},{3,5},{4,6},{5,7},{14,8},{15,9},{8,1... | collective-permute-start | bytes 393224 | tf_op jit(solution)/shard_map/ppermute | solution.py:53
  22.2 47.3 %collective-permute-start.1 = (bf16[256,256]{1,0:T(8,128)(2,1)S(1)}, bf16[256,256]{1,0:T(8,128)(2,1)S(1)}, u32[]{:S(2)}, u32[]{:S(2)}) collective-permute-start(bf16[256,256]{1,0:T(8,128)(2,1)S(1)} %dynamic-slice_bitcast_fusion.2), channel_id=1, source_target_pairs={{1,0},{2,1},{3,2},{4,3},{5,4},{6,5},{7,6},{0,7},{9,8},{10,9},{11,1... | collective-permute-start | bytes 393224 | tf_op jit(solution)/shard_map/ppermute | solution.py:53
  25.7 51.4 %collective-permute-start = (bf16[256,256]{1,0:T(8,128)(2,1)S(1)}, bf16[256,256]{1,0:T(8,128)(2,1)S(1)}, u32[]{:S(2)}, u32[]{:S(2)}) collective-permute-start(bf16[256,256]{1,0:T(8,128)(2,1)S(1)} %dynamic-slice_bitcast_fusion.3), channel_id=1, source_target_pairs={{4,0},{5,1},{6,2},{7,3},{0,4},{1,5},{2,6},{3,7},{12,8},{13,9},{14,... | collective-permute-start | bytes 393224 | tf_op jit(solution)/shard_map/ppermute | solution.py:53
  77.1 52.2 %copy-start = (bf16[4,256,256]{2,1,0:T(8,128)(2,1)}, bf16[4,256,256]{2,1,0:T(8,128)(2,1)S(1)}, u32[]{:S(2)}) copy-start(bf16[4,256,256]{2,1,0:T(8,128)(2,1)S(1)} %pad_maximum_fusion.1.refs_0_) | copy-start | bytes 1572868
  77.2 16.1 %collective-permute-start.7 = (bf16[4,256,256]{2,1,0:T(8,128)(2,1)S(1)}, bf16[4,256,256]{2,1,0:T(8,128)(2,1)S(1)}, u32[]{:S(2)}, u32[]{:S(2)}) collective-permute-start(bf16[4,256,256]{2,1,0:T(8,128)(2,1)S(1)} %pad_maximum_fusion.1.refs_0_), channel_id=1, source_target_pairs={{0,16},{16,32},{32,48},{48,0},{1,17},{17,33},{33,49},{49,1},{2,18}... | collective-permute-start | bytes 1572872 | tf_op jit(solution)/shard_map/ppermute | solution.py:26
  79.4 18.2 %collective-permute-start.9 = (bf16[4,256,256]{2,1,0:T(8,128)(2,1)S(1)}, bf16[4,256,256]{2,1,0:T(8,128)(2,1)}, u32[]{:S(2)}, u32[]{:S(2)}) collective-permute-start(bf16[4,256,256]{2,1,0:T(8,128)(2,1)S(1)} %pad_maximum_fusion.1.refs_0_), channel_id=1, source_target_pairs={{0,48},{16,0},{32,16},{48,32},{1,49},{17,1},{33,17},{49,33},{2,50}... | collective-permute-start | bytes 1572872 | tf_op jit(solution)/shard_map/ppermute | solution.py:26
  84.0 17.2 %collective-permute-start.5 = (bf16[4,256,256]{2,1,0:T(8,128)(2,1)S(1)}, bf16[4,256,256]{2,1,0:T(8,128)(2,1)}, u32[]{:S(2)}, u32[]{:S(2)}) collective-permute-start(bf16[4,256,256]{2,1,0:T(8,128)(2,1)S(1)} %pad_maximum_fusion.1.refs_0_), channel_id=1, source_target_pairs={{0,64},{64,0},{128,192},{192,128},{256,320},{320,256},{384,448},{4... | collective-permute-start | bytes 1572872 | tf_op jit(solution)/shard_map/ppermute | solution.py:36
  85.9 17.2 %collective-permute-start.4 = (bf16[4,256,256]{2,1,0:T(8,128)(2,1)S(1)}, bf16[4,256,256]{2,1,0:T(8,128)(2,1)S(1)}, u32[]{:S(2)}, u32[]{:S(2)}) collective-permute-start(bf16[4,256,256]{2,1,0:T(8,128)(2,1)S(1)} %pad_maximum_fusion.1.refs_0_), channel_id=1, source_target_pairs={{0,8},{8,0},{1,9},{9,1},{2,10},{10,2},{3,11},{11,3},{4,12},{12,4},... | collective-permute-start | bytes 1572872 | tf_op jit(solution)/shard_map/ppermute | solution.py:36
  93.2 36.1 %copy-start.3 = (bf16[4,256,256]{2,1,0:T(8,128)(2,1)}, bf16[4,256,256]{2,1,0:T(8,128)(2,1)S(1)}, u32[]{:S(2)}) copy-start(bf16[4,256,256]{2,1,0:T(8,128)(2,1)S(1)} %collective-permute-done.7.refs_4_) | copy-start | bytes 1572868
  93.2 15.3 %collective-permute-start.15 = (bf16[4,256,256]{2,1,0:T(8,128)(2,1)S(1)}, bf16[4,256,256]{2,1,0:T(8,128)(2,1)}, u32[]{:S(2)}, u32[]{:S(2)}) collective-permute-start(bf16[4,256,256]{2,1,0:T(8,128)(2,1)S(1)} %collective-permute-done.7.refs_4_), channel_id=1, source_target_pairs={{0,16},{16,32},{32,48},{48,0},{1,17},{17,33},{33,49},{49,1},{2,18}... | collective-permute-start | bytes 1572872 | tf_op jit(solution)/shard_map/ppermute | solution.py:26
  95.5 20.5 %collective-permute-start.11 = (bf16[4,256,256]{2,1,0:T(8,128)(2,1)S(1)}, bf16[4,256,256]{2,1,0:T(8,128)(2,1)}, u32[]{:S(2)}, u32[]{:S(2)}) collective-permute-start(bf16[4,256,256]{2,1,0:T(8,128)(2,1)S(1)} %collective-permute-done.7.refs_4_), channel_id=1, source_target_pairs={{0,448},{64,128},{128,64},{192,256},{256,192},{320,384},{384,320},... | collective-permute-start | bytes 1572872 | tf_op jit(solution)/shard_map/ppermute | solution.py:31
  97.6 20.3 %collective-permute-start.8 = (bf16[4,256,256]{2,1,0:T(8,128)(2,1)S(1)}, bf16[4,256,256]{2,1,0:T(8,128)(2,1)}, u32[]{:S(2)}, u32[]{:S(2)}) collective-permute-start(bf16[4,256,256]{2,1,0:T(8,128)(2,1)S(1)} %collective-permute-done.7.refs_4_), channel_id=1, source_target_pairs={{0,8},{8,0},{1,9},{9,1},{2,10},{10,2},{3,11},{11,3},{4,12},{12,4},... | collective-permute-start | bytes 1572872 | tf_op jit(solution)/shard_map/ppermute | solution.py:36
  101.2 11.8 %collective-permute-start.10 = (bf16[4,256,256]{2,1,0:T(8,128)(2,1)}, bf16[4,256,256]{2,1,0:T(8,128)(2,1)}, u32[]{:S(2)}, u32[]{:S(2)}) collective-permute-start(bf16[4,256,256]{2,1,0:T(8,128)(2,1)} %collective-permute-done.9.refs_6_), channel_id=1, source_target_pairs={{0,8},{8,0},{1,9},{9,1},{2,10},{10,2},{3,11},{11,3},{4,12},{12,4},... | collective-permute-start | bytes 1572872 | tf_op jit(solution)/shard_map/ppermute | solution.py:36
  103.1 5.5 %copy-start.4 = (bf16[4,256,256]{2,1,0:T(8,128)(2,1)}, bf16[4,256,256]{2,1,0:T(8,128)(2,1)S(1)}, u32[]{:S(2)}) copy-start(bf16[4,256,256]{2,1,0:T(8,128)(2,1)S(1)} %collective-permute-done.4.refs_1_) | copy-start | bytes 1572868
  103.1 17.2 %collective-permute-start.13 = (bf16[4,256,256]{2,1,0:T(8,128)(2,1)}, bf16[4,256,256]{2,1,0:T(8,128)(2,1)}, u32[]{:S(2)}, u32[]{:S(2)}) collective-permute-start(bf16[4,256,256]{2,1,0:T(8,128)(2,1)} %collective-permute-done.5.refs_2_), channel_id=1, source_target_pairs={{0,48},{16,0},{32,16},{48,32},{1,49},{17,1},{33,17},{49,33},{2,50}... | collective-permute-start | bytes 1572872 | tf_op jit(solution)/shard_map/ppermute | solution.py:26
  108.6 14.5 %collective-permute-start.17 = (bf16[4,256,256]{2,1,0:T(8,128)(2,1)}, bf16[4,256,256]{2,1,0:T(8,128)(2,1)}, u32[]{:S(2)}, u32[]{:S(2)}) collective-permute-start(bf16[4,256,256]{2,1,0:T(8,128)(2,1)} %collective-permute-done.15.refs_12_), channel_id=1, source_target_pairs={{0,64},{64,0},{128,192},{192,128},{256,320},{320,256},{384,448},{4... | collective-permute-start | bytes 1572872 | tf_op jit(solution)/shard_map/ppermute | solution.py:36
  112.9 14.6 %collective-permute-start.6 = (bf16[4,256,256]{2,1,0:T(8,128)(2,1)}, bf16[4,256,256]{2,1,0:T(8,128)(2,1)}, u32[]{:S(2)}, u32[]{:S(2)}) collective-permute-start(bf16[4,256,256]{2,1,0:T(8,128)(2,1)} %collective-permute-done.5.refs_2_), channel_id=1, source_target_pairs={{0,8},{8,0},{1,9},{9,1},{2,10},{10,2},{3,11},{11,3},{4,12},{12,4},... | collective-permute-start | bytes 1572872 | tf_op jit(solution)/shard_map/ppermute | solution.py:36
  115.9 11.7 %collective-permute-start.16 = (bf16[4,256,256]{2,1,0:T(8,128)(2,1)}, bf16[4,256,256]{2,1,0:T(8,128)(2,1)}, u32[]{:S(2)}, u32[]{:S(2)}) collective-permute-start(bf16[4,256,256]{2,1,0:T(8,128)(2,1)} %collective-permute-done.15.refs_12_), channel_id=1, source_target_pairs={{0,8},{8,0},{1,9},{9,1},{2,10},{10,2},{3,11},{11,3},{4,12},{12,4},... | collective-permute-start | bytes 1572872 | tf_op jit(solution)/shard_map/ppermute | solution.py:36
  117.9 9.7 %collective-permute-start.12 = (bf16[4,256,256]{2,1,0:T(8,128)(2,1)}, bf16[4,256,256]{2,1,0:T(8,128)(2,1)}, u32[]{:S(2)}, u32[]{:S(2)}) collective-permute-start(bf16[4,256,256]{2,1,0:T(8,128)(2,1)} %collective-permute-done.11.refs_8_), channel_id=1, source_target_pairs={{0,8},{8,0},{1,9},{9,1},{2,10},{10,2},{3,11},{11,3},{4,12},{12,4},... | collective-permute-start | bytes 1572872 | tf_op jit(solution)/shard_map/ppermute | solution.py:36
  120.3 7.3 %collective-permute-start.14 = (bf16[4,256,256]{2,1,0:T(8,128)(2,1)}, bf16[4,256,256]{2,1,0:T(8,128)(2,1)}, u32[]{:S(2)}, u32[]{:S(2)}) collective-permute-start(bf16[4,256,256]{2,1,0:T(8,128)(2,1)} %collective-permute-done.13.refs_10_), channel_id=1, source_target_pairs={{0,8},{8,0},{1,9},{9,1},{2,10},{10,2},{3,11},{11,3},{4,12},{12,4},... | collective-permute-start | bytes 1572872 | tf_op jit(solution)/shard_map/ppermute | solution.py:36
  123.1 6.1 %collective-permute-start.18 = (bf16[4,256,256]{2,1,0:T(8,128)(2,1)}, bf16[4,256,256]{2,1,0:T(8,128)(2,1)}, u32[]{:S(2)}, u32[]{:S(2)}) collective-permute-start(bf16[4,256,256]{2,1,0:T(8,128)(2,1)} %collective-permute-done.17.refs_14_), channel_id=1, source_target_pairs={{0,8},{8,0},{1,9},{9,1},{2,10},{10,2},{3,11},{11,3},{4,12},{12,4},... | collective-permute-start | bytes 1572872 | tf_op jit(solution)/shard_map/ppermute | solution.py:36
